TPU v7x, 512 devices: a whole 4x8x8 slice. The times are simulated.
512 devices in a mesh: cp: 128 (over z, y, core), tp: 4 (over x).
Axes of the slice: x: 4, y: 8, z: 8, core: 2. Of those that a mesh axis runs over, the one named last changes fastest.
Arguments:
- queries: bfloat16 [49152, 4096], P('cp', 'tp'), may hold values from -56 to 56
- keys: bfloat16 [49152, 1024], P('cp', 'tp'), may hold values from -6 to 6
- values: bfloat16 [49152, 1024], P('cp', 'tp'), may hold values from -6 to 6
- lengths: int32 [32], replicated, may hold values from 1 to 2689, 49152 in all
Outputs:
- attended: bfloat16 [49152, 4096], P('cp', 'tp')
Inputs may be any that keep to these rules, and one draw needn't show every extreme that they name: `lengths`: the 32 documents fill the 49152 tokens; each has at most 2689 tokens and one has exactly 2689.
All inputs are finite; a program needn't handle non-finite values.
Results may differ from a plain program's by a relative error of at most 0.0065.
Values may be sent and summed in bfloat16 or wider, within the bound.
No kernel may reach another device: no remote copies, remote signals or barrier semaphores. Data moves between devices by JAX's collectives and lax.ppermute only.
A program may use at most 64 MiB of HBM per device.

v0:
```python
import jax
import jax.numpy as jnp
from jax import lax
from jax.sharding import PartitionSpec as P

HEAD_DIM = 128
LEVELS = 3


def passed_along(value, axis, steps):
    count = lax.axis_size(axis)
    leading, last = (max(0, -steps), min(count, count - steps))
    return lax.ppermute(value, axis, [(source, source + steps) for source in range(leading, last)])


def document_of(doc_starts, position):
    return jnp.sum((doc_starts[None, :] <= position[:, None]).astype(jnp.int32), axis=1) - 1


def body(queries, keys, values, lengths):
    tok_rows = queries.shape[0]
    kv_heads = keys.shape[1] // HEAD_DIM
    group_size = queries.shape[1] // keys.shape[1]
    logit_scale_factor = HEAD_DIM ** (-0.5)
    doc_ends = jnp.cumsum(lengths)
    doc_starts = doc_ends - lengths
    anchor = lax.axis_index("cp") * tok_rows
    reach_blocks = min(2**LEVELS, lax.axis_size("cp"))
    query_pos = anchor + jnp.arange(tok_rows, dtype=jnp.int32)
    query_doc = document_of(doc_starts, query_pos)
    grouped = queries.reshape(tok_rows, kv_heads, group_size, HEAD_DIM).transpose(1, 2, 0, 3)
    keys_major = keys.reshape(tok_rows, kv_heads, HEAD_DIM).transpose(1, 0, 2)
    values_major = values.reshape(tok_rows, kv_heads, HEAD_DIM).transpose(1, 0, 2)
    running = (
        jnp.full((kv_heads, group_size, tok_rows), -1e30, jnp.float32),
        jnp.zeros((kv_heads, group_size, tok_rows), jnp.float32),
        jnp.zeros((kv_heads, group_size, tok_rows, HEAD_DIM), jnp.float32),
    )

    def absorb(running, key_block, value_block, key_start):
        key_pos = key_start + jnp.arange(key_block.shape[1], dtype=jnp.int32)
        allowed = query_doc[:, None] == document_of(doc_starts, key_pos)[None, :]
        allowed = allowed & (key_pos[None, :] <= query_pos[:, None]) & (key_pos[None, :] >= 0)
        max_old, denominator, weighted_value_sum = running
        attention_logits = (
            jnp.einsum("xayu,xku->xayk", grouped, key_block, preferred_element_type=jnp.float32)
            * logit_scale_factor
        )
        attention_logits = jnp.where(allowed, attention_logits, -1e30)
        max_new = jnp.maximum(max_old, jnp.max(attention_logits, axis=-1))
        weights = jnp.where(allowed, jnp.exp(attention_logits - max_new[..., None]), 0.0)
        rescale = jnp.exp(max_old - max_new)
        denominator = denominator * rescale + jnp.sum(weights, axis=-1)
        weighted_value_sum = weighted_value_sum * rescale[..., None] + jnp.einsum(
            "xayk,xkf->xayf",
            weights.astype(jnp.bfloat16),
            value_block,
            preferred_element_type=jnp.float32,
        )
        return (max_new, denominator, weighted_value_sum)

    running = absorb(running, keys_major, values_major, anchor)
    window_keys, window_values = (keys_major, values_major)
    blocks_held = 1
    while blocks_held < reach_blocks:
        got_keys, got_values = passed_along((window_keys, window_values), "cp", blocks_held)
        for segment in range(blocks_held):
            running = absorb(
                running,
                got_keys[:, segment * tok_rows : (segment + 1) * tok_rows],
                got_values[:, segment * tok_rows : (segment + 1) * tok_rows],
                anchor - (2 * blocks_held - 1 - segment) * tok_rows,
            )
        window_keys = jnp.concatenate([got_keys, window_keys], axis=1)
        window_values = jnp.concatenate([got_values, window_values], axis=1)
        blocks_held = blocks_held * 2
    max_last, denominator, weighted_value_sum = running
    result = weighted_value_sum / denominator[..., None]
    return result.transpose(2, 0, 1, 3).reshape(tok_rows, -1).astype(jnp.bfloat16)


def solution(mesh):
    in_specs = (P("cp", "tp"), P("cp", "tp"), P("cp", "tp"), P())
    out_specs = P("cp", "tp")
    return jax.shard_map(body, mesh=mesh, in_specs=in_specs, out_specs=out_specs, check_vma=False)
```

profile of v0, /device:TPU:330, one launch (start us, length us, event | category | flops | bytes accessed | tf_op | source)
XLA Modules:
  0.0 120.1 jit_solution(1341993625354651391)
XLA Ops:
  0.0 1.1 copy.33
  1.1 0.2 copy.34
  1.3 1.9 %collective-permute-start = (bf16[2,384,128]{2,1,0:T(8,128)(2,1)S(1)}, bf16[2,384,128]{2,1,0:T(8,128)(2,1)S(1)}, u32[]{:S(2)}, u32[]{:S(2)}) collective-permute-start(bf16[2,384,128]{2,1,0:T(8,128)(2,1)S(1)} %bitcast.370), channel_id=1, source_target_pairs={{0,4},{4,8},{8,12},{12,16},{16,20},{20,24},{24,28},{28,32},{32,36}... | collective-permute-start | bytes 589832 | tf_op jit(solution)/shard_map/ppermute | solution.py:13
  3.2 1.1 copy.35
  4.3 3.6 %collective-permute-start.1 = (bf16[2,384,128]{1,2,0:T(8,128)(2,1)S(1)}, bf16[2,384,128]{1,2,0:T(8,128)(2,1)S(1)}, u32[]{:S(2)}, u32[]{:S(2)}) collective-permute-start(bf16[2,384,128]{1,2,0:T(8,128)(2,1)S(1)} %bitcast.373), channel_id=1, source_target_pairs={{0,4},{4,8},{8,12},{12,16},{16,20},{20,24},{24,28},{28,32},{32,36}... | collective-permute-start | bytes 589832 | tf_op jit(solution)/shard_map/ppermute | solution.py:13
  8.1 0.7 copy.31
  8.8 0.1 reduce-window.9
  8.8 0.1 reduce
  9.0 0.7 sub.209
  9.6 1.9 %reshape.379 = bf16[384,2,4,128]{3,2,1,0:T(4,128)(2,1)S(1)} reshape(bf16[384,1024]{1,0:T(8,128)(2,1)} %param.4) | data formatting | bytes 1572864 | tf_op jit(solution)/shard_map/reshape | solution.py:31
  11.6 0.1 convert_reduce_fusion
  11.8 1.3 %and_and_fusion.7 = (pred[384,384]{0,1:T(8,128)(4,1)S(1)}, pred[384,384]{0,1:T(8,128)(4,1)S(1)}, pred[384,384]{0,1:T(8,128)(4,1)S(1)}, pred[384,384]{0,1:T(8,128...) fusion(s32[384]{0:T(512)S(1)} %iota_add_fusion.7, s32[384]{0:T(512)S(1)} %get-tuple-element.63, ...), kind=kLoop, calls=%fused_computation.98 | loop fusion | flops 3538944 | bytes 905472 | tf_op jit(solution)/shard_map/and | solution.py:43
  13.1 1.0 fusion
  14.1 0.6 and_and_fusion.6
  14.7 3.5 %collective-permute-start.2 = (bf16[2,768,128]{2,1,0:T(8,128)(2,1)S(1)}, bf16[2,768,128]{2,1,0:T(8,128)(2,1)S(1)}, u32[]{:S(2)}, u32[]{:S(2)}) collective-permute-start(bf16[2,768,128]{2,1,0:T(8,128)(2,1)S(1)} %pad_maximum_fusion.2), channel_id=1, source_target_pairs={{0,8},{4,12},{8,16},{12,20},{16,24},{20,28},{24,32},{28,36},{32,40... | collective-permute-start | bytes 1179656 | tf_op jit(solution)/shard_map/ppermute | solution.py:13
  18.2 4.7 %collective-permute-start.3 = (bf16[2,768,128]{1,2,0:T(8,128)(2,1)S(1)}, bf16[2,768,128]{1,2,0:T(8,128)(2,1)S(1)}, u32[]{:S(2)}, u32[]{:S(2)}) collective-permute-start(bf16[2,768,128]{1,2,0:T(8,128)(2,1)S(1)} %pad_maximum_fusion.3), channel_id=1, source_target_pairs={{0,8},{4,12},{8,16},{12,20},{16,24},{20,28},{24,32},{28,36},{32,40... | collective-permute-start | bytes 1179656 | tf_op jit(solution)/shard_map/ppermute | solution.py:13
  23.0 1.0 fusion.1
  23.9 4.7 %collective-permute-done.2 = bf16[2,768,128]{2,1,0:T(8,128)(2,1)S(1)} collective-permute-done((bf16[2,768,128]{2,1,0:T(8,128)(2,1)S(1)}, bf16[2,768,128]{2,1,0:T(8,128)(2,1)S(1)}, u32[]{:S(2)}, u32[]{:S(2)}) %collective-permute-start.2) | collective-permute-done | bytes 393248 | tf_op jit(solution)/shard_map/ppermute | solution.py:13
  28.6 5.7 %collective-permute-start.4 = (bf16[2,1536,128]{2,1,0:T(8,128)(2,1)S(1)}, bf16[2,1536,128]{2,1,0:T(8,128)(2,1)S(1)}, u32[]{:S(2)}, u32[]{:S(2)}) collective-permute-start(bf16[2,1536,128]{2,1,0:T(8,128)(2,1)S(1)} %pad_maximum_fusion), channel_id=1, source_target_pairs={{0,16},{4,20},{8,24},{12,28},{16,32},{20,36},{24,40},{28,44},{32,4... | collective-permute-start | bytes 2359304 | tf_op jit(solution)/shard_map/ppermute | solution.py:13
  34.4 4.3 %collective-permute-done.3 = bf16[2,768,128]{1,2,0:T(8,128)(2,1)S(1)} collective-permute-done((bf16[2,768,128]{1,2,0:T(8,128)(2,1)S(1)}, bf16[2,768,128]{1,2,0:T(8,128)(2,1)S(1)}, u32[]{:S(2)}, u32[]{:S(2)}) %collective-permute-start.3) | collective-permute-done | bytes 393248 | tf_op jit(solution)/shard_map/ppermute | solution.py:13
  38.6 0.1 pad_maximum_fusion.1
  38.7 5.0 %collective-permute-start.5 = (bf16[2,1536,128]{1,2,0:T(8,128)(2,1)S(1)}, bf16[2,1536,128]{1,2,0:T(8,128)(2,1)S(1)}, u32[]{:S(2)}, u32[]{:S(2)}) collective-permute-start(bf16[2,1536,128]{1,2,0:T(8,128)(2,1)S(1)} %pad_maximum_fusion.1), channel_id=1, source_target_pairs={{0,16},{4,20},{8,24},{12,28},{16,32},{20,36},{24,40},{28,44},{32,4... | collective-permute-start | bytes 2359304 | tf_op jit(solution)/shard_map/ppermute | solution.py:13
  43.7 1.0 fusion.3
  44.7 3.1 %fusion.2 = (f32[2,4,384]{2,1,0:T(4,128)S(1)}, f32[2,384,4,384]{3,1,2,0:T(8,128)}) fusion(pred[384,384]{0,1:T(8,128)(4,1)S(1)} %get-tuple-element.39, bf16[384,2,4,128]{3,2,1,0:T(4,128)(2,1)S(1)} %reshape.379, bf16[2,768,128]{2,1,0:T(8,128)(2,1)S(1)} %collective-permute-done.2), kind=kOutput, calls=%fused_computation.18 | convolution fusion | flops 305525760 | bytes 5861376 | tf_op jit(solution)/shard_map/xayu,xku->xayk/dot_general | solution.py:46
  47.7 41.8 %collective-permute-done.4 = bf16[2,1536,128]{2,1,0:T(8,128)(2,1)S(1)} collective-permute-done((bf16[2,1536,128]{2,1,0:T(8,128)(2,1)S(1)}, bf16[2,1536,128]{2,1,0:T(8,128)(2,1)S(1)}, u32[]{:S(2)}, u32[]{:S(2)}) %collective-permute-start.4) | collective-permute-done | bytes 786464 | tf_op jit(solution)/shard_map/ppermute | solution.py:13
  89.6 1.0 fusion.7
  90.5 1.0 fusion.5
  91.5 1.0 fusion.4
  92.5 1.0 fusion.6
  93.5 1.2 fusion.8
  94.6 2.7 %fusion.38 = f32[2,4,384,128]{2,3,1,0:T(8,128)} fusion(bf16[2,384,128,1]{1,2,3,0:T(8,128)(2,1)S(1)} %bitcast.376, f32[2,4,384,384]{2,3,1,0:T(8,128)S(1)} %get-tuple-element.55, f32[2,4,384]{2,1,0:T(4,128)S(1)} %get-tuple-element.31, pred[384,384]{0,1:T(8,128)(4,1)S(1)} %get-tuple-element.32), kind=kOutput, calls=%fused_computation.47 | convolution fusion | flops 307888128 | bytes 6647808 | tf_op jit(solution)/shard_map/xayk,xkf->xayf/dot_general | solution.py:54
  97.3 1.2 fusion.16
  98.5 1.2 fusion.18
  99.6 1.1 fusion.22
  100.8 1.4 %fusion.20 = f32[2,4,384]{2,1,0:T(4,128)S(1)} fusion(f32[2,384,4,384]{3,1,2,0:T(8,128)S(1)} %get-tuple-element.43, f32[2,4,384]{2,1,0:T(4,128)S(1)} %get-tuple-element.23, pred[384,384]{0,1:T(8,128)(4,1)S(1)} %get-tuple-element.36), kind=kLoop, calls=%fused_computation.36 | loop fusion | flops 5895168 | bytes 4890624 | tf_op jit(solution)/shard_map/reduce_sum | solution.py:53
  102.2 1.2 fusion.14
  103.4 1.2 fusion.12
  104.5 1.2 fusion.10
  105.7 2.7 %fusion.34 = f32[2,4,384,128]{2,3,1,0:T(8,128)} fusion(f32[2,384,4,384]{3,1,2,0:T(8,128)S(1)} %bitcast.369, f32[2,4,384]{2,1,0:T(4,128)S(1)} %get-tuple-element.27, pred[384,384]{0,1:T(8,128)(4,1)S(1)} %get-tuple-element.39, bf16[2,768,128]{1,2,0:T(8,128)(2,1)S(1)} %collective-permute-done.3), kind=kOutput, calls=%fused_computation.45 | convolution fusion | flops 307888128 | bytes 6647808 | tf_op jit(solution)/shard_map/xayk,xkf->xayf/dot_general | solution.py:54
  108.4 1.5 %fusion.36 = f32[2,4,384,128]{2,3,1,0:T(8,128)S(1)} fusion(f32[2,4,384,384]{2,3,1,0:T(8,128)S(1)} %get-tuple-element.53, f32[2,4,384]{2,1,0:T(4,128)S(1)} %get-tuple-element.28, pred[384,384]{0,1:T(8,128)(4,1)S(1)} %get-tuple-element.38, bf16[2,384,128]{1,2,0:T(8,128)(2,1)S(1)} %collective-permute-done.1), kind=kOutput, calls=%fused_computation.46 | convolution fusion | flops 307888128 | bytes 6647808 | tf_op jit(solution)/shard_map/xayk,xkf->xayf/dot_general | solution.py:54
  109.9 0.1 bitcast_add_fusion.8
  110.0 1.5 %fusion.32 = f32[2,4,384,128]{2,3,1,0:T(8,128)S(1)} fusion(f32[2,384,4,384]{3,1,2,0:T(8,128)S(1)} %get-tuple-element.49, f32[2,4,384]{2,1,0:T(4,128)S(1)} %get-tuple-element.26, pred[384,384]{0,1:T(8,128)(4,1)S(1)} %get-tuple-element.33, bf16[2,768,128]{1,2,0:T(8,128)(2,1)S(1)} %collective-permute-done.3), kind=kOutput, calls=%fused_computation.44 | convolution fusion | flops 307888128 | bytes 6647808 | tf_op jit(solution)/shard_map/xayk,xkf->xayf/dot_general | solution.py:54
  111.6 1.5 %fusion.30 = f32[2,4,384,128]{2,3,1,0:T(8,128)S(1)} fusion(f32[2,384,4,384]{3,1,2,0:T(8,128)S(1)} %get-tuple-element.47, f32[2,4,384]{2,1,0:T(4,128)S(1)} %get-tuple-element.25, pred[384,384]{0,1:T(8,128)(4,1)S(1)} %get-tuple-element.34, bf16[2,1536,128]{1,2,0:T(8,128)(2,1)S(1)} %collective-permute-done.5), kind=kOutput, calls=%fused_computation.43 | convolution fusion | flops 307888128 | bytes 6647808 | tf_op jit(solution)/shard_map/xayk,xkf->xayf/dot_general | solution.py:54
  113.1 1.5 %fusion.28 = f32[2,4,384,128]{2,3,1,0:T(8,128)S(1)} fusion(f32[2,384,4,384]{3,1,2,0:T(8,128)S(1)} %get-tuple-element.45, f32[2,4,384]{2,1,0:T(4,128)S(1)} %get-tuple-element.24, pred[384,384]{0,1:T(8,128)(4,1)S(1)} %get-tuple-element.35, bf16[2,1536,128]{1,2,0:T(8,128)(2,1)S(1)} %collective-permute-done.5), kind=kOutput, calls=%fused_computation.42 | convolution fusion | flops 307888128 | bytes 6647808 | tf_op jit(solution)/shard_map/xayk,xkf->xayf/dot_general | solution.py:54
  114.6 1.5 %fusion.26 = f32[2,4,384,128]{2,3,1,0:T(8,128)S(1)} fusion(f32[2,384,4,384]{3,1,2,0:T(8,128)S(1)} %get-tuple-element.43, f32[2,4,384]{2,1,0:T(4,128)S(1)} %get-tuple-element.23, pred[384,384]{0,1:T(8,128)(4,1)S(1)} %get-tuple-element.36, bf16[2,1536,128]{1,2,0:T(8,128)(2,1)S(1)} %collective-permute-done.5), kind=kOutput, calls=%fused_computation.41 | convolution fusion | flops 307888128 | bytes 6647808 | tf_op jit(solution)/shard_map/xayk,xkf->xayf/dot_general | solution.py:54
  116.2 0.3 copy-done.1
  116.5 2.4 %fusion.49 = bf16[384,2,4,128]{0,3,2,1:T(8,128)(2,1)S(1)} fusion(f32[2,4,384,128]{2,3,1,0:T(8,128)S(1)} %fusion.26, f32[2,4,384,128]{2,3,1,0:T(8,128)S(1)} %fusion.28, f32[2,4,384,128]{2,3,1,0:T(8,128)S(1)} %fusion.30, f32[2,4,384,128]{2,3,1,0:T(8,128)S(1)} %fusion.32, f32[2,4,384,128]{2,3,1,0:T(8,128)S(1)} %copy-done.1, ...), kind=kOutput, calls=%fused_computation.58 | convolution fusion | flops 314572800 | bytes 16982016 | tf_op jit(solution)/shard_map/xayk,xkf->xayf/dot_general | solution.py:54
  118.9 1.2 copy.44
  (32 shorter events, 0.3 us)
Async XLA Ops:
  1.3 13.4 %collective-permute-start = (bf16[2,384,128]{2,1,0:T(8,128)(2,1)S(1)}, bf16[2,384,128]{2,1,0:T(8,128)(2,1)S(1)}, u32[]{:S(2)}, u32[]{:S(2)}) collective-permute-start(bf16[2,384,128]{2,1,0:T(8,128)(2,1)S(1)} %bitcast.370), channel_id=1, source_target_pairs={{0,4},{4,8},{8,12},{12,16},{16,20},{20,24},{24,28},{28,32},{32,36}... | collective-permute-start | bytes 589832 | tf_op jit(solution)/shard_map/ppermute | solution.py:13
  4.3 13.9 %collective-permute-start.1 = (bf16[2,384,128]{1,2,0:T(8,128)(2,1)S(1)}, bf16[2,384,128]{1,2,0:T(8,128)(2,1)S(1)}, u32[]{:S(2)}, u32[]{:S(2)}) collective-permute-start(bf16[2,384,128]{1,2,0:T(8,128)(2,1)S(1)} %bitcast.373), channel_id=1, source_target_pairs={{0,4},{4,8},{8,12},{12,16},{16,20},{20,24},{24,28},{28,32},{32,36}... | collective-permute-start | bytes 589832 | tf_op jit(solution)/shard_map/ppermute | solution.py:13
  14.7 13.9 %collective-permute-start.2 = (bf16[2,768,128]{2,1,0:T(8,128)(2,1)S(1)}, bf16[2,768,128]{2,1,0:T(8,128)(2,1)S(1)}, u32[]{:S(2)}, u32[]{:S(2)}) collective-permute-start(bf16[2,768,128]{2,1,0:T(8,128)(2,1)S(1)} %pad_maximum_fusion.2), channel_id=1, source_target_pairs={{0,8},{4,12},{8,16},{12,20},{16,24},{20,28},{24,32},{28,36},{32,40... | collective-permute-start | bytes 1179656 | tf_op jit(solution)/shard_map/ppermute | solution.py:13
  18.2 20.4 %collective-permute-start.3 = (bf16[2,768,128]{1,2,0:T(8,128)(2,1)S(1)}, bf16[2,768,128]{1,2,0:T(8,128)(2,1)S(1)}, u32[]{:S(2)}, u32[]{:S(2)}) collective-permute-start(bf16[2,768,128]{1,2,0:T(8,128)(2,1)S(1)} %pad_maximum_fusion.3), channel_id=1, source_target_pairs={{0,8},{4,12},{8,16},{12,20},{16,24},{20,28},{24,32},{28,36},{32,40... | collective-permute-start | bytes 1179656 | tf_op jit(solution)/shard_map/ppermute | solution.py:13
  28.6 60.9 %collective-permute-start.4 = (bf16[2,1536,128]{2,1,0:T(8,128)(2,1)S(1)}, bf16[2,1536,128]{2,1,0:T(8,128)(2,1)S(1)}, u32[]{:S(2)}, u32[]{:S(2)}) collective-permute-start(bf16[2,1536,128]{2,1,0:T(8,128)(2,1)S(1)} %pad_maximum_fusion), channel_id=1, source_target_pairs={{0,16},{4,20},{8,24},{12,28},{16,32},{20,36},{24,40},{28,44},{32,4... | collective-permute-start | bytes 2359304 | tf_op jit(solution)/shard_map/ppermute | solution.py:13
  38.7 72.8 %collective-permute-start.5 = (bf16[2,1536,128]{1,2,0:T(8,128)(2,1)S(1)}, bf16[2,1536,128]{1,2,0:T(8,128)(2,1)S(1)}, u32[]{:S(2)}, u32[]{:S(2)}) collective-permute-start(bf16[2,1536,128]{1,2,0:T(8,128)(2,1)S(1)} %pad_maximum_fusion.1), channel_id=1, source_target_pairs={{0,16},{4,20},{8,24},{12,28},{16,32},{20,36},{24,40},{28,44},{32,4... | collective-permute-start | bytes 2359304 | tf_op jit(solution)/shard_map/ppermute | solution.py:13
  99.6 3.7 %slice-start = ((s8[4718592]{0:T(1024)(128)(4,1)}), s8[4194304]{0:T(1024)(128)(4,1)S(1)}, s32[]{:S(2)}) async-start(s8[4718592]{0:T(1024)(128)(4,1)} %bitcast.368), calls=%async_computation | async-start | bytes 8388608
  100.8 2.6 %slice-start.1 = ((s8[4718592]{0:T(1024)(128)(4,1)}), s8[524288]{0:T(1024)(128)(4,1)S(1)}, s32[]{:S(2)}) async-start(s8[4718592]{0:T(1024)(128)(4,1)} %bitcast.368), calls=%async_computation.1 | async-start | bytes 1048576
  114.6 1.6 %copy-start = (f32[2,4,384,128]{2,3,1,0:T(8,128)S(1)}, f32[2,4,384,128]{2,3,1,0:T(8,128)}, u32[]{:S(2)}) copy-start(f32[2,4,384,128]{2,3,1,0:T(8,128)} %fusion.38) | copy-start | bytes 4718596
  114.6 1.9 %copy-start.1 = (f32[2,4,384,128]{2,3,1,0:T(8,128)S(1)}, f32[2,4,384,128]{2,3,1,0:T(8,128)}, u32[]{:S(2)}) copy-start(f32[2,4,384,128]{2,3,1,0:T(8,128)} %fusion.34) | copy-start | bytes 4718596
where the time goes:
time: 120 us
  waiting for transfers between devices  50.8 us (42%)
  matrix products  25.3 us (21%)
  starting transfers between devices  24.4 us (20%)
  other arithmetic  12.7 us (11%)
  local copies, waits for them, and re-layouts  6.54 us (5%)
    ppermute x6, waiting for transfers between devices, passed_along(): lax.ppermute(value, axis, [(source, source + steps) for source in range(l...  50.8 us
    ppermute x6, starting transfers between devices, passed_along(): lax.ppermute(value, axis, [(source, source + steps) for source in range(l...  24.4 us
    dot_general x8, matrix products, absorb(): jnp.einsum('xayk,xkf->xayf', weights.astype(jnp.bfloat16), value_block, p...  15.4 us
    dot_general x8, matrix products, absorb(): jnp.einsum('xayu,xku->xayk', grouped, key_block, preferred_element_type=j...  9.81 us
    reduce_sum x8, other arithmetic, absorb(): denominator = denominator * rescale + jnp.sum(weights, axis=-1)  9.46 us
    unnamed x10, local copies, waits for them, and re-layouts  2.52 us
  transfers between devices with their start and end apart: 6, of which 3 were waited for; matrix products, arithmetic and copies ran while one was open for 29% of the time, Pallas kernels for 0%

commit v1 on v0

v1 whole, which is shorter than its diff:
```python
import functools

import jax
import jax.numpy as jnp
from jax import lax
from jax.experimental import pallas as pl
from jax.experimental.pallas import tpu as pltpu
from jax.sharding import PartitionSpec as P

HEAD_DIM = 128
RING = 8
TILE = 256
LANES = 128
NEG = -1e30
SCALE = HEAD_DIM**-0.5 * 1.4426950408889634
NONE = 1 << 20


def shifted(pairs):
    return [(a, b) for a, b in pairs if b is not None]


def routes(count):
    chips = count // 2
    dev = lambda n, c: 2 * n + c
    back = lambda n: n - n % RING + (n % RING - RING // 4) % RING
    inside = [n for n in range(chips) if n + 3 < chips]
    return {
        "cross": [(dev(n, c), dev(n + 1, 1 - c)) for n in range(chips - 1) for c in (0, 1)],
        "ahead": [(dev(n, c), dev(n + 1, c)) for n in range(chips - 1) for c in (0, 1)],
        "swap": [(dev(n, c), dev(n, 1 - c)) for n in range(chips) for c in (0, 1)],
        "mate": [(dev(n, 0), dev(n, 1)) for n in range(chips)],
        "back1": [(dev(n, 1), dev(back(n), 0)) for n in inside],
        "back2": [(dev(back(n), 0), dev((n + 4) % chips, 0)) for n in inside],
        "last": [(dev((n + 4) % chips, 0), dev(n + 3, 0)) for n in inside]
        + [(dev(n, 1), dev(n + 1, 1)) for n in range(chips - 1)],
    }


def attend_kernel(blocks, first, final, tok, heads, group, *refs):
    refs = list(refs)
    lengths, q_ref = refs.pop(0), refs.pop(0)
    kv_refs = [refs.pop(0) for _ in blocks]
    state_in = None if first else refs.pop(0)
    out_ref = refs.pop(0)
    state = refs.pop(0) if final else out_ref
    me = lax.axis_index("cp")
    anchor = me * tok
    odd = me % 2 == 1
    rows = group * tok
    tiles = rows // TILE
    chunks = tok // LANES

    lane = lax.broadcasted_iota(jnp.int32, (1, LANES), 1)
    pos = [anchor + k * LANES + lane for k in range(chunks)]
    low = [jnp.zeros((1, LANES), jnp.int32) for _ in range(chunks)]
    begin = jnp.int32(0)
    lead = jnp.int32(0)
    for d in range(lengths.shape[0]):
        low = [jnp.where(p >= begin, begin, l) for p, l in zip(pos, low)]
        lead = jnp.where(begin <= anchor, begin, lead)
        begin = begin + lengths[d]

    def wide(parts, t):
        per = TILE // LANES
        return jnp.concatenate([parts[(t * per + k) % chunks] for k in range(per)], axis=1)

    def query_tile(g, t):
        at, left, parts = t * TILE, TILE, []
        while left:
            r, row = divmod(at, tok)
            n = min(left, tok - row)
            h = g * group + r
            parts.append(q_ref[row : row + n, h * HEAD_DIM : (h + 1) * HEAD_DIM])
            at, left = at + n, left - n
        return parts[0] if len(parts) == 1 else jnp.concatenate(parts, axis=0)

    def fold(kv_ref, start, diagonal, fresh, source):
        key_row = start + lax.broadcasted_iota(jnp.int32, (tok, TILE), 0)
        for g in range(heads):
            key = kv_ref[0, :, g * HEAD_DIM : (g + 1) * HEAD_DIM]
            value = kv_ref[1, :, g * HEAD_DIM : (g + 1) * HEAD_DIM]
            for t in range(tiles):
                n = g * tiles + t
                score = lax.dot_general(
                    key, query_tile(g, t), (((1,), (1,)), ((), ())), preferred_element_type=jnp.float32
                )
                live = key_row >= wide(low, t)
                if diagonal:
                    live = live & (key_row <= wide(pos, t))
                score = jnp.where(live, score, NEG)
                top = jnp.max(score, axis=0, keepdims=True)
                if not fresh:
                    old = source[n, HEAD_DIM : HEAD_DIM + 1, :]
                    top = jnp.maximum(top, old)
                weight = jnp.exp2((score - top) * SCALE)
                total = jnp.sum(weight, axis=0, keepdims=True)
                acc = lax.dot_general(
                    value, weight.astype(jnp.bfloat16), (((0,), (0,)), ((), ())), preferred_element_type=jnp.float32
                )
                if not fresh:
                    fade = jnp.exp2((old - top) * SCALE)
                    total = total + source[n, HEAD_DIM + 1 : HEAD_DIM + 2, :] * fade
                    acc = acc + source[n, :HEAD_DIM, :] * fade
                state[n, :HEAD_DIM, :] = acc
                state[n, HEAD_DIM : HEAD_DIM + 1, :] = top
                state[n, HEAD_DIM + 1 : HEAD_DIM + 2, :] = total

    if not first and final:
        state[...] = state_in[...]
    for j, (kv_ref, (even_back, odd_back)) in enumerate(zip(kv_refs, blocks)):
        if first and j == 0:
            fold(kv_ref, anchor, True, True, None)
            continue
        start = anchor - jnp.where(odd, odd_back, even_back) * tok
        pl.when((start >= 0) & (lead < start + tok))(
            functools.partial(fold, kv_ref, start, False, False, state)
        )

    if final:
        for g in range(heads):
            for t in range(tiles):
                n = g * tiles + t
                share = 1.0 / state[n, HEAD_DIM + 1 : HEAD_DIM + 2, :]
                done = (state[n, :HEAD_DIM, :] * share).T.astype(jnp.bfloat16)
                at, left = t * TILE, TILE
                while left:
                    r, row = divmod(at, tok)
                    m = min(left, tok - row)
                    h = g * group + r
                    o = at - t * TILE
                    out_ref[row : row + m, h * HEAD_DIM : (h + 1) * HEAD_DIM] = done[o : o + m, :]
                    at, left = at + m, left - m


def attend(lengths, queries, kvs, blocks, state, final):
    tok, width = queries.shape
    heads = kvs[0].shape[2] // HEAD_DIM
    group = width // kvs[0].shape[2]
    count = heads * group * tok // TILE
    first = state is None
    state_shape = jax.ShapeDtypeStruct((count, HEAD_DIM + 8, TILE), jnp.float32)
    vmem = pl.BlockSpec(memory_space=pltpu.VMEM)
    args = [lengths, queries, *kvs] + ([] if first else [state])
    aliases = {} if first or final else {len(args) - 1: 0}
    flops = 4 * tok * tok * width * len(kvs)
    return pl.pallas_call(
        functools.partial(attend_kernel, blocks, first, final, tok, heads, group),
        out_shape=jax.ShapeDtypeStruct((tok, width), jnp.bfloat16) if final else state_shape,
        in_specs=[pl.BlockSpec(memory_space=pltpu.SMEM)] + [vmem] * (len(args) - 1),
        out_specs=vmem,
        scratch_shapes=[pltpu.VMEM(state_shape.shape, jnp.float32)] if final else [],
        input_output_aliases=aliases,
        compiler_params=pltpu.CompilerParams(vmem_limit_bytes=24 << 20),
        cost_estimate=pl.CostEstimate(flops=flops, bytes_accessed=1 << 20, transcendentals=0),
    )(*args)


def body(queries, keys, values, lengths):
    ways = routes(lax.axis_size("cp"))
    move = lambda x, way: lax.ppermute(x, "cp", ways[way])
    after = lax.optimization_barrier
    step = functools.partial(attend, lengths, queries)
    even = lax.axis_index("cp") % 2 == 0
    own = jnp.stack([keys, values])
    got1 = move(own, "cross")
    far1 = move(own, "back1")
    mate0 = move(own, "mate")
    state = step([own], [(0, 0)], None, False)
    state, got1, far1, mate0 = after((state, got1, far1, mate0))
    got2 = move(got1, "ahead")
    far2 = move(far1, "back2")
    mate1 = move(got1, "swap")
    state = step([mate0, got1], [(NONE, 1), (1, 3)], state, False)
    state, mate1 = after((state, mate1))
    state = step([mate1], [(2, 2)], state, False)
    state, got2, far2 = after((state, got2, far2))
    got3 = move(jnp.where(even, far2, got2), "last")
    mate2 = move(got2, "swap")
    state = step([got2, far2], [(3, 5), (7, NONE)], state, False)
    state, mate2 = after((state, mate2))
    state = step([mate2], [(4, 4)], state, False)
    state, got3 = after((state, got3))
    mate3 = move(got3, "swap")
    state = step([got3], [(5, 7)], state, False)
    state, mate3 = after((state, mate3))
    return step([mate3], [(6, 6)], state, True)


def solution(mesh):
    in_specs = (P("cp", "tp"), P("cp", "tp"), P("cp", "tp"), P())
    out_specs = P("cp", "tp")
    return jax.shard_map(body, mesh=mesh, in_specs=in_specs, out_specs=out_specs, check_vma=False)
```

time: 120 us -> 78.5 us (0.65)
  the two profiles are of different devices: /device:TPU:330 before, /device:TPU:132 now
where the time goes in v1:
time: 78.5 us; the launch traced here: 78.2 us
  Pallas kernels  43.1 us (55%)
  starting transfers between devices  30.1 us (38%)
  local copies, waits for them, and re-layouts  3.52 us (4%)
  other arithmetic  1.18 us (2%)
    pallas_call x7, Pallas kernels, attend(): pl.pallas_call(functools.partial(attend_kernel, blocks, first, final, tok...  43.1 us
    ppermute x9, starting transfers between devices, body(): move = lambda x, way: lax.ppermute(x, 'cp', ways[way])  30.1 us
    unnamed x12, local copies, waits for them, and re-layouts  3.52 us
  transfers between devices with their start and end apart: 9, of which 0 were waited for; matrix products, arithmetic and copies ran while one was open for 0% of the time, Pallas kernels for 47%

profile of v1, /device:TPU:132, one launch (start us, length us, event | category | flops | bytes accessed | tf_op | source)
XLA Modules:
  0.0 78.2 jit_solution(15172214602481365611)
XLA Ops:
  0.0 0.0 copy-start.5
  0.0 0.0 copy-start.1
  0.0 1.1 %pad_maximum_fusion.refs_2_ = bf16[2,384,256]{2,1,0:T(8,128)(2,1)S(1)} fusion(bf16[1,384,256]{2,1,0:T(8,128)(2,1)} %bitcast.2, bf16[1,384,256]{2,1,0:T(8,128)(2,1)} %bitcast.3), kind=kLoop, calls=%fused_computation | loop fusion | flops 196608 | bytes 786432 | tf_op jit(solution)/shard_map/stack | solution.py:165
  1.1 2.9 %collective-permute-start = (bf16[2,384,256]{2,1,0:T(8,128)(2,1)S(1)}, bf16[2,384,256]{2,1,0:T(8,128)(2,1)}, u32[]{:S(2)}, u32[]{:S(2)}) collective-permute-start(bf16[2,384,256]{2,1,0:T(8,128)(2,1)S(1)} %pad_maximum_fusion.refs_2_), channel_id=1, source_target_pairs={{0,12},{4,8},{8,20},{12,16},{16,28},{20,24},{24,36},{28,32},{32,44... | collective-permute-start | bytes 1179656 | tf_op jit(solution)/shard_map/ppermute | solution.py:161
  4.1 1.3 %collective-permute-start.1 = (bf16[2,384,256]{2,1,0:T(8,128)(2,1)S(1)}, bf16[2,384,256]{2,1,0:T(8,128)(2,1)}, u32[]{:S(2)}, u32[]{:S(2)}) collective-permute-start(bf16[2,384,256]{2,1,0:T(8,128)(2,1)S(1)} %pad_maximum_fusion.refs_2_), channel_id=1, source_target_pairs={{4,48},{12,56},{20,0},{28,8},{36,16},{44,24},{52,32},{60,40},{68,1... | collective-permute-start | bytes 1179656 | tf_op jit(solution)/shard_map/ppermute | solution.py:161
  5.4 6.7 %collective-permute-start.2 = (bf16[2,384,256]{2,1,0:T(8,128)(2,1)S(1)}, bf16[2,384,256]{2,1,0:T(8,128)(2,1)S(1)}, u32[]{:S(2)}, u32[]{:S(2)}) collective-permute-start(bf16[2,384,256]{2,1,0:T(8,128)(2,1)S(1)} %pad_maximum_fusion.refs_2_), channel_id=1, source_target_pairs={{0,4},{8,12},{16,20},{24,28},{32,36},{40,44},{48,52},{56,60},{64,6... | collective-permute-start | bytes 1179656 | tf_op jit(solution)/shard_map/ppermute | solution.py:161
  12.1 0.0 copy-start
  12.1 1.1 %copy-done = bf16[384,1024]{1,0:T(8,128)(2,1)S(1)} copy-done((bf16[384,1024]{1,0:T(8,128)(2,1)S(1)}, bf16[384,1024]{1,0:T(8,128)(2,1)}, u32[]{:S(2)}) %copy-start) | copy-done | bytes 786456
  13.3 0.0 copy-start.4
  13.3 0.7 copy-done.4
  13.9 5.1 %shard_map.46.refs_4_ = f32[12,136,256]{2,1,0:T(8,128)S(1)} custom-call(s32[32]{0:T(128)S(1)} %copy-done.4, bf16[384,1024]{1,0:T(8,128)(2,1)S(1)} %copy-done, bf16[2,384,256]{2,1,0:T(8,128)(2,1)S(1)} %pad_maximum_fusion.refs_2_), custom_call_target="tpu_custom_call" | custom-call | flops 603979776 | bytes 1048576 | tf_op jit(solution)/shard_map/pallas_call | solution.py:147
  19.0 0.0 collective-permute-done.refs_3_
  19.0 0.0 collective-permute-done.1
  19.0 0.0 collective-permute-done.2.refs_2_
  19.0 0.0 copy-start.2
  19.0 0.7 copy-done.2
  19.8 1.9 %collective-permute-start.3 = (bf16[2,384,256]{2,1,0:T(8,128)(2,1)}, bf16[2,384,256]{2,1,0:T(8,128)(2,1)}, u32[]{:S(2)}, u32[]{:S(2)}) collective-permute-start(bf16[2,384,256]{2,1,0:T(8,128)(2,1)} %collective-permute-done.refs_3_), channel_id=1, source_target_pairs={{0,4},{4,0},{8,12},{12,8},{16,20},{20,16},{24,28},{28,24},{32,36},... | collective-permute-start | bytes 1179656 | tf_op jit(solution)/shard_map/ppermute | solution.py:161
  21.7 3.7 %collective-permute-start.4 = (bf16[2,384,256]{2,1,0:T(8,128)(2,1)}, bf16[2,384,256]{2,1,0:T(8,128)(2,1)S(1)}, u32[]{:S(2)}, u32[]{:S(2)}) collective-permute-start(bf16[2,384,256]{2,1,0:T(8,128)(2,1)} %collective-permute-done.refs_3_), channel_id=1, source_target_pairs={{0,8},{4,12},{8,16},{12,20},{16,24},{20,28},{24,32},{28,36},{32,40... | collective-permute-start | bytes 1179656 | tf_op jit(solution)/shard_map/ppermute | solution.py:161
  25.4 4.1 %collective-permute-start.5 = (bf16[2,384,256]{2,1,0:T(8,128)(2,1)}, bf16[2,384,256]{2,1,0:T(8,128)(2,1)S(1)}, u32[]{:S(2)}, u32[]{:S(2)}) collective-permute-start(bf16[2,384,256]{2,1,0:T(8,128)(2,1)} %collective-permute-done.1), channel_id=1, source_target_pairs={{48,32},{56,40},{0,48},{8,56},{16,64},{24,72},{32,80},{40,88},{112... | collective-permute-start | bytes 1179656 | tf_op jit(solution)/shard_map/ppermute | solution.py:161
  29.5 0.0 copy-done.5
  29.5 0.0 copy-done.1
  29.5 0.0 copy-start.3
  29.6 1.0 %copy-done.3 = bf16[2,384,256]{2,1,0:T(8,128)(2,1)S(1)} copy-done((bf16[2,384,256]{2,1,0:T(8,128)(2,1)S(1)}, bf16[2,384,256]{2,1,0:T(8,128)(2,1)}, u32[]{:S(2)}) %copy-start.3) | copy-done | bytes 393240
  30.5 5.6 %shard_map.47.refs_3_ = f32[12,136,256]{2,1,0:T(8,128)S(1)} custom-call(s32[32]{0:T(128)S(1)} %copy-done.5, bf16[384,1024]{1,0:T(8,128)(2,1)S(1)} %copy-done.1, bf16[2,384,256]{2,1,0:T(8,128)(2,1)S(1)} %copy-done.3, bf16[2,384,256]{2,1,0:T(8,128)(2,1)} %collective-permute-done.refs_3_, ...), custom_call_target="tpu_custom_call", output_to_operand_aliasing={{}: (4, {})} | custom-call | flops 1207959552 | bytes 1048576 | tf_op jit(solution)/shard_map/pallas_call | solution.py:147
  36.2 0.0 collective-permute-done.3.refs_2_
  36.2 5.8 %shard_map.48.refs_4_ = f32[12,136,256]{2,1,0:T(8,128)S(1)} custom-call(s32[32]{0:T(128)S(1)} %copy-done.5, bf16[384,1024]{1,0:T(8,128)(2,1)S(1)} %copy-done.1, bf16[2,384,256]{2,1,0:T(8,128)(2,1)} %collective-permute-done.3.refs_2_, f32[12,136,256]{2,1,0:T(8,128)S(1)} %shard_map.47.refs_3_), custom_call_target="tpu_custom_call", output_to_operand_aliasing={{}: (3, {})} | custom-call | flops 603979776 | bytes 1048576 | tf_op jit(solution)/shard_map/pallas_call | solution.py:147
  42.0 0.0 collective-permute-done.4.refs_2_
  42.0 0.0 collective-permute-done.5.refs_3_
  42.0 1.9 %collective-permute-start.6 = (bf16[2,384,256]{2,1,0:T(8,128)(2,1)S(1)}, bf16[2,384,256]{2,1,0:T(8,128)(2,1)S(1)}, u32[]{:S(2)}, u32[]{:S(2)}) collective-permute-start(bf16[2,384,256]{2,1,0:T(8,128)(2,1)S(1)} %collective-permute-done.4.refs_2_), channel_id=1, source_target_pairs={{0,4},{4,0},{8,12},{12,8},{16,20},{20,16},{24,28},{28,24},{32,36},... | collective-permute-start | bytes 1179656 | tf_op jit(solution)/shard_map/ppermute | solution.py:161
  44.0 5.6 %collective-permute-start.7 = (bf16[2,384,256]{2,1,0:T(8,128)(2,1)S(1)}, bf16[2,384,256]{2,1,0:T(8,128)(2,1)S(1)}, u32[]{:S(2)}, u32[]{:S(2)}) collective-permute-start(bf16[2,384,256]{2,1,0:T(8,128)(2,1)S(1)} %broadcast_select_fusion), channel_id=1, source_target_pairs={{32,24},{40,32},{48,40},{56,48},{64,56},{72,64},{80,72},{88,80},{9... | collective-permute-start | bytes 1179656 | tf_op jit(solution)/shard_map/ppermute | solution.py:161
  49.6 9.7 %shard_map.49.refs_3_ = f32[12,136,256]{2,1,0:T(8,128)S(1)} custom-call(s32[32]{0:T(128)S(1)} %copy-done.5, bf16[384,1024]{1,0:T(8,128)(2,1)S(1)} %copy-done.1, bf16[2,384,256]{2,1,0:T(8,128)(2,1)S(1)} %collective-permute-done.4.refs_2_, bf16[2,384,256]{2,1,0:T(8,128)(2,1)S(1)} %collective-permute-done.5.refs_3_, ...), custom_call_target="tpu_custom_call", output_to_operand_aliasing={{}: (4, {})} | custom-call | flops 1207959552 | bytes 1048576 | tf_op jit(solution)/shard_map/pallas_call | solution.py:147
  59.3 0.0 collective-permute-done.6.refs_2_
  59.3 5.4 %shard_map.50.refs_3_ = f32[12,136,256]{2,1,0:T(8,128)S(1)} custom-call(s32[32]{0:T(128)S(1)} %copy-done.5, bf16[384,1024]{1,0:T(8,128)(2,1)S(1)} %copy-done.1, bf16[2,384,256]{2,1,0:T(8,128)(2,1)S(1)} %collective-permute-done.6.refs_2_, f32[12,136,256]{2,1,0:T(8,128)S(1)} %shard_map.49.refs_3_), custom_call_target="tpu_custom_call", output_to_operand_aliasing={{}: (3, {})} | custom-call | flops 603979776 | bytes 1048576 | tf_op jit(solution)/shard_map/pallas_call | solution.py:147
  64.7 0.0 collective-permute-done.7.refs_2_
  64.7 1.9 %collective-permute-start.8 = (bf16[2,384,256]{2,1,0:T(8,128)(2,1)S(1)}, bf16[2,384,256]{2,1,0:T(8,128)(2,1)S(1)}, u32[]{:S(2)}, u32[]{:S(2)}) collective-permute-start(bf16[2,384,256]{2,1,0:T(8,128)(2,1)S(1)} %collective-permute-done.7.refs_2_), channel_id=1, source_target_pairs={{0,4},{4,0},{8,12},{12,8},{16,20},{20,16},{24,28},{28,24},{32,36},... | collective-permute-start | bytes 1179656 | tf_op jit(solution)/shard_map/ppermute | solution.py:161
  66.7 5.2 %shard_map.51.refs_3_ = f32[12,136,256]{2,1,0:T(8,128)S(1)} custom-call(s32[32]{0:T(128)S(1)} %copy-done.5, bf16[384,1024]{1,0:T(8,128)(2,1)S(1)} %copy-done.1, bf16[2,384,256]{2,1,0:T(8,128)(2,1)S(1)} %collective-permute-done.7.refs_2_, f32[12,136,256]{2,1,0:T(8,128)S(1)} %shard_map.50.refs_3_), custom_call_target="tpu_custom_call", output_to_operand_aliasing={{}: (3, {})} | custom-call | flops 603979776 | bytes 1048576 | tf_op jit(solution)/shard_map/pallas_call | solution.py:147
  71.8 0.0 collective-permute-done.8.refs_2_
  71.8 6.4 %shard_map.52 = bf16[384,1024]{1,0:T(8,128)(2,1)} custom-call(s32[32]{0:T(128)S(1)} %copy-done.5, bf16[384,1024]{1,0:T(8,128)(2,1)S(1)} %copy-done.1, bf16[2,384,256]{2,1,0:T(8,128)(2,1)S(1)} %collective-permute-done.8.refs_2_, f32[12,136,256]{2,1,0:T(8,128)S(1)} %shard_map.51.refs_3_), custom_call_target="tpu_custom_call" | custom-call | flops 603979776 | bytes 1048576 | tf_op jit(solution)/shard_map/pallas_call | solution.py:147
  (1 shorter events, 0.0 us)
Async XLA Ops:
  0.0 29.5 %copy-start.5 = (s32[32]{0:T(128)S(1)}, s32[32]{0:T(128)}, u32[]{:S(2)}) copy-start(s32[32]{0:T(128)} %refs_0_.13) | copy-start | bytes 388
  0.0 29.5 %copy-start.1 = (bf16[384,1024]{1,0:T(8,128)(2,1)S(1)}, bf16[384,1024]{1,0:T(8,128)(2,1)}, u32[]{:S(2)}) copy-start(bf16[384,1024]{1,0:T(8,128)(2,1)} %refs_1_.13) | copy-start | bytes 2359300
  1.1 17.9 %collective-permute-start = (bf16[2,384,256]{2,1,0:T(8,128)(2,1)S(1)}, bf16[2,384,256]{2,1,0:T(8,128)(2,1)}, u32[]{:S(2)}, u32[]{:S(2)}) collective-permute-start(bf16[2,384,256]{2,1,0:T(8,128)(2,1)S(1)} %pad_maximum_fusion.refs_2_), channel_id=1, source_target_pairs={{0,12},{4,8},{8,20},{12,16},{16,28},{20,24},{24,36},{28,32},{32,44... | collective-permute-start | bytes 1179656 | tf_op jit(solution)/shard_map/ppermute | solution.py:161
  4.1 14.9 %collective-permute-start.1 = (bf16[2,384,256]{2,1,0:T(8,128)(2,1)S(1)}, bf16[2,384,256]{2,1,0:T(8,128)(2,1)}, u32[]{:S(2)}, u32[]{:S(2)}) collective-permute-start(bf16[2,384,256]{2,1,0:T(8,128)(2,1)S(1)} %pad_maximum_fusion.refs_2_), channel_id=1, source_target_pairs={{4,48},{12,56},{20,0},{28,8},{36,16},{44,24},{52,32},{60,40},{68,1... | collective-permute-start | bytes 1179656 | tf_op jit(solution)/shard_map/ppermute | solution.py:161
  5.4 13.6 %collective-permute-start.2 = (bf16[2,384,256]{2,1,0:T(8,128)(2,1)S(1)}, bf16[2,384,256]{2,1,0:T(8,128)(2,1)S(1)}, u32[]{:S(2)}, u32[]{:S(2)}) collective-permute-start(bf16[2,384,256]{2,1,0:T(8,128)(2,1)S(1)} %pad_maximum_fusion.refs_2_), channel_id=1, source_target_pairs={{0,4},{8,12},{16,20},{24,28},{32,36},{40,44},{48,52},{56,60},{64,6... | collective-permute-start | bytes 1179656 | tf_op jit(solution)/shard_map/ppermute | solution.py:161
  12.1 1.1 %copy-start = (bf16[384,1024]{1,0:T(8,128)(2,1)S(1)}, bf16[384,1024]{1,0:T(8,128)(2,1)}, u32[]{:S(2)}) copy-start(bf16[384,1024]{1,0:T(8,128)(2,1)} %refs_1_.13) | copy-start | bytes 2359300
  13.3 0.7 copy-start.4
  19.0 0.7 copy-start.2
  19.8 16.4 %collective-permute-start.3 = (bf16[2,384,256]{2,1,0:T(8,128)(2,1)}, bf16[2,384,256]{2,1,0:T(8,128)(2,1)}, u32[]{:S(2)}, u32[]{:S(2)}) collective-permute-start(bf16[2,384,256]{2,1,0:T(8,128)(2,1)} %collective-permute-done.refs_3_), channel_id=1, source_target_pairs={{0,4},{4,0},{8,12},{12,8},{16,20},{20,16},{24,28},{28,24},{32,36},... | collective-permute-start | bytes 1179656 | tf_op jit(solution)/shard_map/ppermute | solution.py:161
  21.7 20.3 %collective-permute-start.4 = (bf16[2,384,256]{2,1,0:T(8,128)(2,1)}, bf16[2,384,256]{2,1,0:T(8,128)(2,1)S(1)}, u32[]{:S(2)}, u32[]{:S(2)}) collective-permute-start(bf16[2,384,256]{2,1,0:T(8,128)(2,1)} %collective-permute-done.refs_3_), channel_id=1, source_target_pairs={{0,8},{4,12},{8,16},{12,20},{16,24},{20,28},{24,32},{28,36},{32,40... | collective-permute-start | bytes 1179656 | tf_op jit(solution)/shard_map/ppermute | solution.py:161
  25.4 16.6 %collective-permute-start.5 = (bf16[2,384,256]{2,1,0:T(8,128)(2,1)}, bf16[2,384,256]{2,1,0:T(8,128)(2,1)S(1)}, u32[]{:S(2)}, u32[]{:S(2)}) collective-permute-start(bf16[2,384,256]{2,1,0:T(8,128)(2,1)} %collective-permute-done.1), channel_id=1, source_target_pairs={{48,32},{56,40},{0,48},{8,56},{16,64},{24,72},{32,80},{40,88},{112... | collective-permute-start | bytes 1179656 | tf_op jit(solution)/shard_map/ppermute | solution.py:161
  29.5 1.0 %copy-start.3 = (bf16[2,384,256]{2,1,0:T(8,128)(2,1)S(1)}, bf16[2,384,256]{2,1,0:T(8,128)(2,1)}, u32[]{:S(2)}) copy-start(bf16[2,384,256]{2,1,0:T(8,128)(2,1)} %copy-done.2) | copy-start | bytes 1179652
  42.0 17.3 %collective-permute-start.6 = (bf16[2,384,256]{2,1,0:T(8,128)(2,1)S(1)}, bf16[2,384,256]{2,1,0:T(8,128)(2,1)S(1)}, u32[]{:S(2)}, u32[]{:S(2)}) collective-permute-start(bf16[2,384,256]{2,1,0:T(8,128)(2,1)S(1)} %collective-permute-done.4.refs_2_), channel_id=1, source_target_pairs={{0,4},{4,0},{8,12},{12,8},{16,20},{20,16},{24,28},{28,24},{32,36},... | collective-permute-start | bytes 1179656 | tf_op jit(solution)/shard_map/ppermute | solution.py:161
  44.0 20.7 %collective-permute-start.7 = (bf16[2,384,256]{2,1,0:T(8,128)(2,1)S(1)}, bf16[2,384,256]{2,1,0:T(8,128)(2,1)S(1)}, u32[]{:S(2)}, u32[]{:S(2)}) collective-permute-start(bf16[2,384,256]{2,1,0:T(8,128)(2,1)S(1)} %broadcast_select_fusion), channel_id=1, source_target_pairs={{32,24},{40,32},{48,40},{56,48},{64,56},{72,64},{80,72},{88,80},{9... | collective-permute-start | bytes 1179656 | tf_op jit(solution)/shard_map/ppermute | solution.py:161
  64.7 7.1 %collective-permute-start.8 = (bf16[2,384,256]{2,1,0:T(8,128)(2,1)S(1)}, bf16[2,384,256]{2,1,0:T(8,128)(2,1)S(1)}, u32[]{:S(2)}, u32[]{:S(2)}) collective-permute-start(bf16[2,384,256]{2,1,0:T(8,128)(2,1)S(1)} %collective-permute-done.7.refs_2_), channel_id=1, source_target_pairs={{0,4},{4,0},{8,12},{12,8},{16,20},{20,16},{24,28},{28,24},{32,36},... | collective-permute-start | bytes 1179656 | tf_op jit(solution)/shard_map/ppermute | solution.py:161

commit v2 on v1

--- a/solution.py
+++ b/solution.py
@@ -9,11 +9,13 @@
 
 HEAD_DIM = 128
 RING = 8
-TILE = 256
+TILE = 512
 LANES = 128
 NEG = -1e30
 SCALE = HEAD_DIM**-0.5 * 1.4426950408889634
 NONE = 1 << 20
+DEPTH = 2
+BATCH = 1
 
 
 def shifted(pairs):
@@ -43,6 +45,7 @@
     kv_refs = [refs.pop(0) for _ in blocks]
     state_in = None if first else refs.pop(0)
     out_ref = refs.pop(0)
+    s_ref, p_ref, mask_ref = refs.pop(0), refs.pop(0), refs.pop(0)
     state = refs.pop(0) if final else out_ref
     me = lax.axis_index("cp")
     anchor = me * tok
@@ -75,47 +78,78 @@
             at, left = at + n, left - n
         return parts[0] if len(parts) == 1 else jnp.concatenate(parts, axis=0)
 
-    def fold(kv_ref, start, diagonal, fresh, source):
-        key_row = start + lax.broadcasted_iota(jnp.int32, (tok, TILE), 0)
-        for g in range(heads):
+    def fold(kv_ref, mode, source):
+        fresh = mode == "own"
+        total_tiles = heads * tiles
+        tops, shifts, fades = {}, {}, {}
+
+        def score_stage(n):
+            g, t = divmod(n, tiles)
             key = kv_ref[0, :, g * HEAD_DIM : (g + 1) * HEAD_DIM]
+            score = lax.dot_general(
+                key, query_tile(g, t), (((1,), (1,)), ((), ())), preferred_element_type=jnp.float32
+            )
+            if mode == "own":
+                score = score + wide([mask_ref[:, k * LANES : (k + 1) * LANES] for k in range(chunks)], t)
+            elif mode == "part":
+                score = score + wide([mask_ref[:, :LANES]] * chunks, t)
+            s_ref[n % DEPTH] = score
+            top = jnp.max(score, axis=0, keepdims=True)
+            shifts[n] = top
+            if not fresh:
+                joins = wide(low, t) == lead
+                old = source[n, HEAD_DIM : HEAD_DIM + 1, :]
+                top = jnp.where(joins, jnp.maximum(top, old), old)
+                shifts[n] = jnp.where(joins, top, -NEG)
+                fades[n] = jnp.exp2((old - top) * SCALE)
+            tops[n] = top
+
+        def weight_stage(n):
+            weight = jnp.exp2((s_ref[n % DEPTH] - shifts[n]) * SCALE)
+            p_ref[n % DEPTH] = weight.astype(jnp.bfloat16)
+            total = jnp.sum(weight, axis=0, keepdims=True)
+            if not fresh:
+                total = total + source[n, HEAD_DIM + 1 : HEAD_DIM + 2, :] * fades[n]
+            state[n, HEAD_DIM : HEAD_DIM + 1, :] = tops[n]
+            state[n, HEAD_DIM + 1 : HEAD_DIM + 2, :] = total
+
+        def value_stage(n):
+            g, t = divmod(n, tiles)
             value = kv_ref[1, :, g * HEAD_DIM : (g + 1) * HEAD_DIM]
-            for t in range(tiles):
-                n = g * tiles + t
-                score = lax.dot_general(
-                    key, query_tile(g, t), (((1,), (1,)), ((), ())), preferred_element_type=jnp.float32
-                )
-                live = key_row >= wide(low, t)
-                if diagonal:
-                    live = live & (key_row <= wide(pos, t))
-                score = jnp.where(live, score, NEG)
-                top = jnp.max(score, axis=0, keepdims=True)
-                if not fresh:
-                    old = source[n, HEAD_DIM : HEAD_DIM + 1, :]
-                    top = jnp.maximum(top, old)
-                weight = jnp.exp2((score - top) * SCALE)
-                total = jnp.sum(weight, axis=0, keepdims=True)
-                acc = lax.dot_general(
-                    value, weight.astype(jnp.bfloat16), (((0,), (0,)), ((), ())), preferred_element_type=jnp.float32
-                )
-                if not fresh:
-                    fade = jnp.exp2((old - top) * SCALE)
-                    total = total + source[n, HEAD_DIM + 1 : HEAD_DIM + 2, :] * fade
-                    acc = acc + source[n, :HEAD_DIM, :] * fade
-                state[n, :HEAD_DIM, :] = acc
-                state[n, HEAD_DIM : HEAD_DIM + 1, :] = top
-                state[n, HEAD_DIM + 1 : HEAD_DIM + 2, :] = total
+            acc = lax.dot_general(
+                value, p_ref[n % DEPTH], (((0,), (0,)), ((), ())), preferred_element_type=jnp.float32
+            )
+            if not fresh:
+                acc = acc + source[n, :HEAD_DIM, :] * fades[n]
+            state[n, :HEAD_DIM, :] = acc
+
+        for i in range(0, total_tiles + 2 * BATCH, BATCH):
+            for k in range(BATCH):
+                n = i + k
+                if n < total_tiles:
+                    score_stage(n)
+                if 0 <= n - BATCH < total_tiles:
+                    weight_stage(n - BATCH)
+                if 0 <= n - 2 * BATCH < total_tiles:
+                    value_stage(n - 2 * BATCH)
 
     if not first and final:
         state[...] = state_in[...]
     for j, (kv_ref, (even_back, odd_back)) in enumerate(zip(kv_refs, blocks)):
         if first and j == 0:
-            fold(kv_ref, anchor, True, True, None)
+            key_row = anchor + lax.broadcasted_iota(jnp.int32, (tok, LANES), 0)
+            for k in range(chunks):
+                live = (key_row >= low[k]) & (key_row <= pos[k])
+                mask_ref[:, k * LANES : (k + 1) * LANES] = jnp.where(live, 0.0, NEG)
+            fold(kv_ref, "own", None)
             continue
         start = anchor - jnp.where(odd, odd_back, even_back) * tok
-        pl.when((start >= 0) & (lead < start + tok))(
-            functools.partial(fold, kv_ref, start, False, False, state)
-        )
+
+        @pl.when((start >= 0) & (lead < start + tok))
+        def _():
+            key_row = start + lax.broadcasted_iota(jnp.int32, (tok, LANES), 0)
+            mask_ref[:, :LANES] = jnp.where(key_row >= lead, 0.0, NEG)
+            fold(kv_ref, "part", state)
 
     if final:
         for g in range(heads):
@@ -131,6 +165,39 @@
                     o = at - t * TILE
                     out_ref[row : row + m, h * HEAD_DIM : (h + 1) * HEAD_DIM] = done[o : o + m, :]
                     at, left = at + m, left - m
+
+
+def small_call(kernel, outs, *args):
+    vmem = pl.BlockSpec(memory_space=pltpu.VMEM)
+    return pl.pallas_call(
+        kernel,
+        out_shape=outs,
+        in_specs=[vmem] * len(args),
+        out_specs=jax.tree.map(lambda _: vmem, outs),
+        compiler_params=pltpu.CompilerParams(vmem_limit_bytes=4 << 20),
+        cost_estimate=pl.CostEstimate(flops=1 << 20, bytes_accessed=1 << 20, transcendentals=0),
+    )(*args)
+
+
+def stack_kernel(k_ref, v_ref, out_ref):
+    out_ref[0] = k_ref[...]
+    out_ref[1] = v_ref[...]
+
+
+def keep_kernel(q_ref, out_ref):
+    out_ref[...] = q_ref[...]
+
+
+def pick_kernel(even_ref, odd_ref, out_ref):
+    odd = lax.axis_index("cp") % 2 == 1
+
+    @pl.when(odd)
+    def _():
+        out_ref[...] = odd_ref[...]
+
+    @pl.when(jnp.logical_not(odd))
+    def _():
+        out_ref[...] = even_ref[...]
 
 
 def attend(lengths, queries, kvs, blocks, state, final):
@@ -149,9 +216,14 @@
         out_shape=jax.ShapeDtypeStruct((tok, width), jnp.bfloat16) if final else state_shape,
         in_specs=[pl.BlockSpec(memory_space=pltpu.SMEM)] + [vmem] * (len(args) - 1),
         out_specs=vmem,
-        scratch_shapes=[pltpu.VMEM(state_shape.shape, jnp.float32)] if final else [],
+        scratch_shapes=[
+            pltpu.VMEM((DEPTH, tok, TILE), jnp.float32),
+            pltpu.VMEM((DEPTH, tok, TILE), jnp.bfloat16),
+            pltpu.VMEM((tok, tok), jnp.float32),
+            *([pltpu.VMEM(state_shape.shape, jnp.float32)] if final else []),
+        ],
         input_output_aliases=aliases,
-        compiler_params=pltpu.CompilerParams(vmem_limit_bytes=24 << 20),
+        compiler_params=pltpu.CompilerParams(vmem_limit_bytes=16 << 20),
         cost_estimate=pl.CostEstimate(flops=flops, bytes_accessed=1 << 20, transcendentals=0),
     )(*args)
 
@@ -161,8 +233,7 @@
     move = lambda x, way: lax.ppermute(x, "cp", ways[way])
     after = lax.optimization_barrier
     step = functools.partial(attend, lengths, queries)
-    even = lax.axis_index("cp") % 2 == 0
-    own = jnp.stack([keys, values])
+    own = small_call(stack_kernel, jax.ShapeDtypeStruct((2, *keys.shape), keys.dtype), keys, values)
     got1 = move(own, "cross")
     far1 = move(own, "back1")
     mate0 = move(own, "mate")
@@ -175,7 +246,7 @@
     state, mate1 = after((state, mate1))
     state = step([mate1], [(2, 2)], state, False)
     state, got2, far2 = after((state, got2, far2))
-    got3 = move(jnp.where(even, far2, got2), "last")
+    got3 = move(small_call(pick_kernel, jax.ShapeDtypeStruct(got2.shape, got2.dtype), far2, got2), "last")
     mate2 = move(got2, "swap")
     state = step([got2, far2], [(3, 5), (7, NONE)], state, False)
     state, mate2 = after((state, mate2))

time: 78.5 us -> 66 us (0.84)
  the two profiles are of different devices: /device:TPU:132 before, /device:TPU:263 now
where the time goes in v2:
time: 66 us; the launch traced here: 65.3 us
  waiting for transfers between devices  26.2 us (40%)
  starting transfers between devices  25.6 us (39%)
  Pallas kernels  9.72 us (15%)
  local copies, waits for them, and re-layouts  3.65 us (6%)
    ppermute x9, waiting for transfers between devices, body(): move = lambda x, way: lax.ppermute(x, 'cp', ways[way])  26.2 us
    ppermute x9, starting transfers between devices, body(): move = lambda x, way: lax.ppermute(x, 'cp', ways[way])  25.6 us
    pallas_call x7, Pallas kernels, attend(): pl.pallas_call(functools.partial(attend_kernel, blocks, first, final, tok...  9.65 us
    unnamed x12, local copies, waits for them, and re-layouts  3.65 us
  transfers between devices with their start and end apart: 9, of which 5 were waited for; matrix products, arithmetic and copies ran while one was open for 0% of the time, Pallas kernels for 12%

profile of v2, /device:TPU:263, one launch (start us, length us, event | category | flops | bytes accessed | tf_op | source)
XLA Modules:
  0.0 65.3 jit_solution(11453997845941281480)
XLA Ops:
  0.0 0.0 copy-start.2
  0.0 0.9 %copy-done.2 = bf16[384,256]{1,0:T(8,128)(2,1)S(1)} copy-done((bf16[384,256]{1,0:T(8,128)(2,1)S(1)}, bf16[384,256]{1,0:T(8,128)(2,1)}, u32[]{:S(2)}) %copy-start.2) | copy-done | bytes 196632
  0.9 0.0 copy-start.3
  0.9 0.9 %copy-done.3 = bf16[384,256]{1,0:T(8,128)(2,1)S(1)} copy-done((bf16[384,256]{1,0:T(8,128)(2,1)S(1)}, bf16[384,256]{1,0:T(8,128)(2,1)}, u32[]{:S(2)}) %copy-start.3) | copy-done | bytes 196632
  1.9 0.0 copy-start.5
  1.9 1.3 %collective-permute-start.2 = (bf16[2,384,256]{2,1,0:T(8,128)(2,1)S(1)}, bf16[2,384,256]{2,1,0:T(8,128)(2,1)S(1)}, u32[]{:S(2)}, u32[]{:S(2)}) collective-permute-start(bf16[2,384,256]{2,1,0:T(8,128)(2,1)S(1)} %shard_map.46.refs_2_), channel_id=1, source_target_pairs={{0,4},{8,12},{16,20},{24,28},{32,36},{40,44},{48,52},{56,60},{64,6... | collective-permute-start | bytes 1179656 | tf_op jit(solution)/shard_map/ppermute | solution.py:233
  3.2 6.9 %collective-permute-start.1 = (bf16[2,384,256]{2,1,0:T(8,128)(2,1)S(1)}, bf16[2,384,256]{2,1,0:T(8,128)(2,1)S(1)}, u32[]{:S(2)}, u32[]{:S(2)}) collective-permute-start(bf16[2,384,256]{2,1,0:T(8,128)(2,1)S(1)} %shard_map.46.refs_2_), channel_id=1, source_target_pairs={{4,48},{12,56},{20,0},{28,8},{36,16},{44,24},{52,32},{60,40},{68,1... | collective-permute-start | bytes 1179656 | tf_op jit(solution)/shard_map/ppermute | solution.py:233
  10.1 1.9 %collective-permute-start = (bf16[2,384,256]{2,1,0:T(8,128)(2,1)S(1)}, bf16[2,384,256]{2,1,0:T(8,128)(2,1)S(1)}, u32[]{:S(2)}, u32[]{:S(2)}) collective-permute-start(bf16[2,384,256]{2,1,0:T(8,128)(2,1)S(1)} %shard_map.46.refs_2_), channel_id=1, source_target_pairs={{0,12},{4,8},{8,20},{12,16},{16,28},{20,24},{24,36},{28,32},{32,44... | collective-permute-start | bytes 1179656 | tf_op jit(solution)/shard_map/ppermute | solution.py:233
  12.1 0.0 copy-start
  12.1 1.1 %copy-done = bf16[384,1024]{1,0:T(8,128)(2,1)S(1)} copy-done((bf16[384,1024]{1,0:T(8,128)(2,1)S(1)}, bf16[384,1024]{1,0:T(8,128)(2,1)}, u32[]{:S(2)}) %copy-start) | copy-done | bytes 786456
  13.2 0.0 copy-start.4
  13.2 0.7 copy-done.4
  13.8 2.5 %shard_map.47.refs_4_ = f32[6,136,512]{2,1,0:T(8,128)S(1)} custom-call(s32[32]{0:T(128)S(1)} %copy-done.4, bf16[384,1024]{1,0:T(8,128)(2,1)S(1)} %copy-done, bf16[2,384,256]{2,1,0:T(8,128)(2,1)S(1)} %shard_map.46.refs_2_), custom_call_target="tpu_custom_call" | custom-call | flops 603979776 | bytes 1048576 | tf_op jit(solution)/shard_map/pallas_call | solution.py:214
  16.4 0.0 collective-permute-done.2.refs_2_
  16.4 2.6 %collective-permute-done.1 = bf16[2,384,256]{2,1,0:T(8,128)(2,1)S(1)} collective-permute-done((bf16[2,384,256]{2,1,0:T(8,128)(2,1)S(1)}, bf16[2,384,256]{2,1,0:T(8,128)(2,1)S(1)}, u32[]{:S(2)}, u32[]{:S(2)}) %collective-permute-start.1) | collective-permute-done | bytes 393248 | tf_op jit(solution)/shard_map/ppermute | solution.py:233
  19.0 3.5 %collective-permute-done.refs_3_ = bf16[2,384,256]{2,1,0:T(8,128)(2,1)S(1)} collective-permute-done((bf16[2,384,256]{2,1,0:T(8,128)(2,1)S(1)}, bf16[2,384,256]{2,1,0:T(8,128)(2,1)S(1)}, u32[]{:S(2)}, u32[]{:S(2)}) %collective-permute-start) | collective-permute-done | bytes 393248 | tf_op jit(solution)/shard_map/ppermute | solution.py:233
  22.5 1.9 %collective-permute-start.3 = (bf16[2,384,256]{2,1,0:T(8,128)(2,1)S(1)}, bf16[2,384,256]{2,1,0:T(8,128)(2,1)S(1)}, u32[]{:S(2)}, u32[]{:S(2)}) collective-permute-start(bf16[2,384,256]{2,1,0:T(8,128)(2,1)S(1)} %collective-permute-done.refs_3_), channel_id=1, source_target_pairs={{0,4},{4,0},{8,12},{12,8},{16,20},{20,16},{24,28},{28,24},{32,36},... | collective-permute-start | bytes 1179656 | tf_op jit(solution)/shard_map/ppermute | solution.py:233
  24.5 0.7 %collective-permute-start.5 = (bf16[2,384,256]{2,1,0:T(8,128)(2,1)S(1)}, bf16[2,384,256]{2,1,0:T(8,128)(2,1)S(1)}, u32[]{:S(2)}, u32[]{:S(2)}) collective-permute-start(bf16[2,384,256]{2,1,0:T(8,128)(2,1)S(1)} %collective-permute-done.1), channel_id=1, source_target_pairs={{48,32},{56,40},{0,48},{8,56},{16,64},{24,72},{32,80},{40,88},{112... | collective-permute-start | bytes 1179656 | tf_op jit(solution)/shard_map/ppermute | solution.py:233
  25.2 2.2 %collective-permute-start.4 = (bf16[2,384,256]{2,1,0:T(8,128)(2,1)S(1)}, bf16[2,384,256]{2,1,0:T(8,128)(2,1)S(1)}, u32[]{:S(2)}, u32[]{:S(2)}) collective-permute-start(bf16[2,384,256]{2,1,0:T(8,128)(2,1)S(1)} %collective-permute-done.refs_3_), channel_id=1, source_target_pairs={{0,8},{4,12},{8,16},{12,20},{16,24},{20,28},{24,32},{28,36},{32,40... | collective-permute-start | bytes 1179656 | tf_op jit(solution)/shard_map/ppermute | solution.py:233
  27.4 0.0 copy-done.5
  27.4 2.8 %shard_map.48.refs_3_ = f32[6,136,512]{2,1,0:T(8,128)S(1)} custom-call(s32[32]{0:T(128)S(1)} %copy-done.5, bf16[384,1024]{1,0:T(8,128)(2,1)S(1)} %copy-done, bf16[2,384,256]{2,1,0:T(8,128)(2,1)S(1)} %collective-permute-done.2.refs_2_, bf16[2,384,256]{2,1,0:T(8,128)(2,1)S(1)} %collective-permute-done.refs_3_, ...), custom_call_target="tpu_custom_call", output_to_operand_aliasing={{}: (4, {})} | custom-call | flops 1207959552 | bytes 1048576 | tf_op jit(solution)/shard_map/pallas_call | solution.py:214
  30.2 0.0 copy-start.1
  30.2 0.0 collective-permute-done.3.refs_2_
  30.2 0.6 shard_map.49.refs_4_
  30.8 0.0 collective-permute-done.5.refs_3_.even_ref
  30.8 10.4 %collective-permute-done.4.refs_2_.odd_ref = bf16[2,384,256]{2,1,0:T(8,128)(2,1)S(1)} collective-permute-done((bf16[2,384,256]{2,1,0:T(8,128)(2,1)S(1)}, bf16[2,384,256]{2,1,0:T(8,128)(2,1)S(1)}, u32[]{:S(2)}, u32[]{:S(2)}) %collective-permute-start.4) | collective-permute-done | bytes 393248 | tf_op jit(solution)/shard_map/ppermute | solution.py:233
  41.2 6.8 %collective-permute-start.6 = (bf16[2,384,256]{2,1,0:T(8,128)(2,1)S(1)}, bf16[2,384,256]{2,1,0:T(8,128)(2,1)S(1)}, u32[]{:S(2)}, u32[]{:S(2)}) collective-permute-start(bf16[2,384,256]{2,1,0:T(8,128)(2,1)S(1)} %collective-permute-done.4.refs_2_.odd_ref), channel_id=1, source_target_pairs={{0,4},{4,0},{8,12},{12,8},{16,20},{20,16},{24,28},{28,24},{32,36},... | collective-permute-start | bytes 1179656 | tf_op jit(solution)/shard_map/ppermute | solution.py:233
  48.1 1.9 %collective-permute-start.7 = (bf16[2,384,256]{2,1,0:T(8,128)(2,1)S(1)}, bf16[2,384,256]{2,1,0:T(8,128)(2,1)S(1)}, u32[]{:S(2)}, u32[]{:S(2)}) collective-permute-start(bf16[2,384,256]{2,1,0:T(8,128)(2,1)S(1)} %shard_map.52), channel_id=1, source_target_pairs={{32,24},{40,32},{48,40},{56,48},{64,56},{72,64},{80,72},{88,80},{9... | collective-permute-start | bytes 1179656 | tf_op jit(solution)/shard_map/ppermute | solution.py:233
  50.0 0.0 copy-done.1
  50.0 0.8 %shard_map.50.refs_3_ = f32[6,136,512]{2,1,0:T(8,128)S(1)} custom-call(s32[32]{0:T(128)S(1)} %copy-done.5, bf16[384,1024]{1,0:T(8,128)(2,1)S(1)} %copy-done.1, bf16[2,384,256]{2,1,0:T(8,128)(2,1)S(1)} %collective-permute-done.4.refs_2_.odd_ref, bf16[2,384,256]{2,1,0:T(8,128)(2,1)S(1)} %collective-permute-done.5.refs_3_.even_ref, ...), custom_call_target="tpu_custom_call", output_to_operand_aliasing={{}: (4, {})} | custom-call | flops 1207959552 | bytes 1048576 | tf_op jit(solution)/shard_map/pallas_call | solution.py:214
  50.8 0.0 collective-permute-done.6.refs_2_
  50.8 0.6 shard_map.51.refs_3_
  51.4 8.5 %collective-permute-done.7.refs_2_ = bf16[2,384,256]{2,1,0:T(8,128)(2,1)S(1)} collective-permute-done((bf16[2,384,256]{2,1,0:T(8,128)(2,1)S(1)}, bf16[2,384,256]{2,1,0:T(8,128)(2,1)S(1)}, u32[]{:S(2)}, u32[]{:S(2)}) %collective-permute-start.7) | collective-permute-done | bytes 393248 | tf_op jit(solution)/shard_map/ppermute | solution.py:233
  59.9 1.9 %collective-permute-start.8 = (bf16[2,384,256]{2,1,0:T(8,128)(2,1)S(1)}, bf16[2,384,256]{2,1,0:T(8,128)(2,1)S(1)}, u32[]{:S(2)}, u32[]{:S(2)}) collective-permute-start(bf16[2,384,256]{2,1,0:T(8,128)(2,1)S(1)} %collective-permute-done.7.refs_2_), channel_id=1, source_target_pairs={{0,4},{4,0},{8,12},{12,8},{16,20},{20,16},{24,28},{28,24},{32,36},... | collective-permute-start | bytes 1179656 | tf_op jit(solution)/shard_map/ppermute | solution.py:233
  61.8 0.6 shard_map.53.refs_3_
  62.4 1.1 %collective-permute-done.8.refs_2_ = bf16[2,384,256]{2,1,0:T(8,128)(2,1)S(1)} collective-permute-done((bf16[2,384,256]{2,1,0:T(8,128)(2,1)S(1)}, bf16[2,384,256]{2,1,0:T(8,128)(2,1)S(1)}, u32[]{:S(2)}, u32[]{:S(2)}) %collective-permute-start.8) | collective-permute-done | bytes 393248 | tf_op jit(solution)/shard_map/ppermute | solution.py:233
  63.5 1.8 %shard_map.54 = bf16[384,1024]{1,0:T(8,128)(2,1)} custom-call(s32[32]{0:T(128)S(1)} %copy-done.5, bf16[384,1024]{1,0:T(8,128)(2,1)S(1)} %copy-done.1, bf16[2,384,256]{2,1,0:T(8,128)(2,1)S(1)} %collective-permute-done.8.refs_2_, f32[6,136,512]{2,1,0:T(8,128)S(1)} %shard_map.53.refs_3_), custom_call_target="tpu_custom_call" | custom-call | flops 603979776 | bytes 1048576 | tf_op jit(solution)/shard_map/pallas_call | solution.py:214
  (2 shorter events, 0.1 us)
Async XLA Ops:
  0.0 0.9 %copy-start.2 = (bf16[384,256]{1,0:T(8,128)(2,1)S(1)}, bf16[384,256]{1,0:T(8,128)(2,1)}, u32[]{:S(2)}) copy-start(bf16[384,256]{1,0:T(8,128)(2,1)} %k_ref.1) | copy-start | bytes 589828
  0.9 0.9 %copy-start.3 = (bf16[384,256]{1,0:T(8,128)(2,1)S(1)}, bf16[384,256]{1,0:T(8,128)(2,1)}, u32[]{:S(2)}) copy-start(bf16[384,256]{1,0:T(8,128)(2,1)} %v_ref.1) | copy-start | bytes 589828
  1.9 25.5 %copy-start.5 = (s32[32]{0:T(128)S(1)}, s32[32]{0:T(128)}, u32[]{:S(2)}) copy-start(s32[32]{0:T(128)} %refs_0_.13) | copy-start | bytes 388
  1.9 14.5 %collective-permute-start.2 = (bf16[2,384,256]{2,1,0:T(8,128)(2,1)S(1)}, bf16[2,384,256]{2,1,0:T(8,128)(2,1)S(1)}, u32[]{:S(2)}, u32[]{:S(2)}) collective-permute-start(bf16[2,384,256]{2,1,0:T(8,128)(2,1)S(1)} %shard_map.46.refs_2_), channel_id=1, source_target_pairs={{0,4},{8,12},{16,20},{24,28},{32,36},{40,44},{48,52},{56,60},{64,6... | collective-permute-start | bytes 1179656 | tf_op jit(solution)/shard_map/ppermute | solution.py:233
  3.2 15.8 %collective-permute-start.1 = (bf16[2,384,256]{2,1,0:T(8,128)(2,1)S(1)}, bf16[2,384,256]{2,1,0:T(8,128)(2,1)S(1)}, u32[]{:S(2)}, u32[]{:S(2)}) collective-permute-start(bf16[2,384,256]{2,1,0:T(8,128)(2,1)S(1)} %shard_map.46.refs_2_), channel_id=1, source_target_pairs={{4,48},{12,56},{20,0},{28,8},{36,16},{44,24},{52,32},{60,40},{68,1... | collective-permute-start | bytes 1179656 | tf_op jit(solution)/shard_map/ppermute | solution.py:233
  10.1 12.4 %collective-permute-start = (bf16[2,384,256]{2,1,0:T(8,128)(2,1)S(1)}, bf16[2,384,256]{2,1,0:T(8,128)(2,1)S(1)}, u32[]{:S(2)}, u32[]{:S(2)}) collective-permute-start(bf16[2,384,256]{2,1,0:T(8,128)(2,1)S(1)} %shard_map.46.refs_2_), channel_id=1, source_target_pairs={{0,12},{4,8},{8,20},{12,16},{16,28},{20,24},{24,36},{28,32},{32,44... | collective-permute-start | bytes 1179656 | tf_op jit(solution)/shard_map/ppermute | solution.py:233
  12.1 1.1 %copy-start = (bf16[384,1024]{1,0:T(8,128)(2,1)S(1)}, bf16[384,1024]{1,0:T(8,128)(2,1)}, u32[]{:S(2)}) copy-start(bf16[384,1024]{1,0:T(8,128)(2,1)} %refs_1_.13) | copy-start | bytes 2359300
  13.2 0.7 %copy-start.4 = (s32[32]{0:T(128)S(1)}, s32[32]{0:T(128)}, u32[]{:S(2)}) copy-start(s32[32]{0:T(128)} %refs_0_.13) | copy-start | bytes 388
  22.5 7.7 %collective-permute-start.3 = (bf16[2,384,256]{2,1,0:T(8,128)(2,1)S(1)}, bf16[2,384,256]{2,1,0:T(8,128)(2,1)S(1)}, u32[]{:S(2)}, u32[]{:S(2)}) collective-permute-start(bf16[2,384,256]{2,1,0:T(8,128)(2,1)S(1)} %collective-permute-done.refs_3_), channel_id=1, source_target_pairs={{0,4},{4,0},{8,12},{12,8},{16,20},{20,16},{24,28},{28,24},{32,36},... | collective-permute-start | bytes 1179656 | tf_op jit(solution)/shard_map/ppermute | solution.py:233
  24.5 6.3 %collective-permute-start.5 = (bf16[2,384,256]{2,1,0:T(8,128)(2,1)S(1)}, bf16[2,384,256]{2,1,0:T(8,128)(2,1)S(1)}, u32[]{:S(2)}, u32[]{:S(2)}) collective-permute-start(bf16[2,384,256]{2,1,0:T(8,128)(2,1)S(1)} %collective-permute-done.1), channel_id=1, source_target_pairs={{48,32},{56,40},{0,48},{8,56},{16,64},{24,72},{32,80},{40,88},{112... | collective-permute-start | bytes 1179656 | tf_op jit(solution)/shard_map/ppermute | solution.py:233
  25.2 16.1 %collective-permute-start.4 = (bf16[2,384,256]{2,1,0:T(8,128)(2,1)S(1)}, bf16[2,384,256]{2,1,0:T(8,128)(2,1)S(1)}, u32[]{:S(2)}, u32[]{:S(2)}) collective-permute-start(bf16[2,384,256]{2,1,0:T(8,128)(2,1)S(1)} %collective-permute-done.refs_3_), channel_id=1, source_target_pairs={{0,8},{4,12},{8,16},{12,20},{16,24},{20,28},{24,32},{28,36},{32,40... | collective-permute-start | bytes 1179656 | tf_op jit(solution)/shard_map/ppermute | solution.py:233
  30.2 19.8 %copy-start.1 = (bf16[384,1024]{1,0:T(8,128)(2,1)S(1)}, bf16[384,1024]{1,0:T(8,128)(2,1)}, u32[]{:S(2)}) copy-start(bf16[384,1024]{1,0:T(8,128)(2,1)} %refs_1_.13) | copy-start | bytes 2359300
  41.2 9.6 %collective-permute-start.6 = (bf16[2,384,256]{2,1,0:T(8,128)(2,1)S(1)}, bf16[2,384,256]{2,1,0:T(8,128)(2,1)S(1)}, u32[]{:S(2)}, u32[]{:S(2)}) collective-permute-start(bf16[2,384,256]{2,1,0:T(8,128)(2,1)S(1)} %collective-permute-done.4.refs_2_.odd_ref), channel_id=1, source_target_pairs={{0,4},{4,0},{8,12},{12,8},{16,20},{20,16},{24,28},{28,24},{32,36},... | collective-permute-start | bytes 1179656 | tf_op jit(solution)/shard_map/ppermute | solution.py:233
  48.1 11.8 %collective-permute-start.7 = (bf16[2,384,256]{2,1,0:T(8,128)(2,1)S(1)}, bf16[2,384,256]{2,1,0:T(8,128)(2,1)S(1)}, u32[]{:S(2)}, u32[]{:S(2)}) collective-permute-start(bf16[2,384,256]{2,1,0:T(8,128)(2,1)S(1)} %shard_map.52), channel_id=1, source_target_pairs={{32,24},{40,32},{48,40},{56,48},{64,56},{72,64},{80,72},{88,80},{9... | collective-permute-start | bytes 1179656 | tf_op jit(solution)/shard_map/ppermute | solution.py:233
  59.9 3.6 %collective-permute-start.8 = (bf16[2,384,256]{2,1,0:T(8,128)(2,1)S(1)}, bf16[2,384,256]{2,1,0:T(8,128)(2,1)S(1)}, u32[]{:S(2)}, u32[]{:S(2)}) collective-permute-start(bf16[2,384,256]{2,1,0:T(8,128)(2,1)S(1)} %collective-permute-done.7.refs_2_), channel_id=1, source_target_pairs={{0,4},{4,0},{8,12},{12,8},{16,20},{20,16},{24,28},{28,24},{32,36},... | collective-permute-start | bytes 1179656 | tf_op jit(solution)/shard_map/ppermute | solution.py:233

commit v3 on v2

--- a/solution.py
+++ b/solution.py
@@ -6,6 +6,7 @@
 from jax.experimental import pallas as pl
 from jax.experimental.pallas import tpu as pltpu
 from jax.sharding import PartitionSpec as P
+
 
 HEAD_DIM = 128
 RING = 8
@@ -16,10 +17,6 @@
 NONE = 1 << 20
 DEPTH = 2
 BATCH = 1
-
-
-def shifted(pairs):
-    return [(a, b) for a, b in pairs if b is not None]
 
 
 def routes(count):
@@ -114,7 +111,7 @@
             state[n, HEAD_DIM + 1 : HEAD_DIM + 2, :] = total
 
         def value_stage(n):
-            g, t = divmod(n, tiles)
+            g, _ = divmod(n, tiles)
             value = kv_ref[1, :, g * HEAD_DIM : (g + 1) * HEAD_DIM]
             acc = lax.dot_general(
                 value, p_ref[n % DEPTH], (((0,), (0,)), ((), ())), preferred_element_type=jnp.float32
@@ -182,10 +179,6 @@
 def stack_kernel(k_ref, v_ref, out_ref):
     out_ref[0] = k_ref[...]
     out_ref[1] = v_ref[...]
-
-
-def keep_kernel(q_ref, out_ref):
-    out_ref[...] = q_ref[...]
 
 
 def pick_kernel(even_ref, odd_ref, out_ref):
@@ -230,7 +223,10 @@
 
 def body(queries, keys, values, lengths):
     ways = routes(lax.axis_size("cp"))
-    move = lambda x, way: lax.ppermute(x, "cp", ways[way])
+
+    def move(x, way):
+        return lax.ppermute(x, "cp", ways[way])
+
     after = lax.optimization_barrier
     step = functools.partial(attend, lengths, queries)
     own = small_call(stack_kernel, jax.ShapeDtypeStruct((2, *keys.shape), keys.dtype), keys, values)
@@ -238,14 +234,14 @@
     far1 = move(own, "back1")
     mate0 = move(own, "mate")
     state = step([own], [(0, 0)], None, False)
-    state, got1, far1, mate0 = after((state, got1, far1, mate0))
+    state, got1, mate0 = after((state, got1, mate0))
     got2 = move(got1, "ahead")
     far2 = move(far1, "back2")
     mate1 = move(got1, "swap")
     state = step([mate0, got1], [(NONE, 1), (1, 3)], state, False)
     state, mate1 = after((state, mate1))
     state = step([mate1], [(2, 2)], state, False)
-    state, got2, far2 = after((state, got2, far2))
+    state, got2 = after((state, got2))
     got3 = move(small_call(pick_kernel, jax.ShapeDtypeStruct(got2.shape, got2.dtype), far2, got2), "last")
     mate2 = move(got2, "swap")
     state = step([got2, far2], [(3, 5), (7, NONE)], state, False)

time: 66 us -> 62.9 us (0.953)
  the two profiles are of different devices: /device:TPU:263 before, /device:TPU:453 now
where the time goes in v3:
time: 62.9 us; the launch traced here: 62.5 us
  Pallas kernels  22.6 us (36%)
  starting transfers between devices  22 us (35%)
  waiting for transfers between devices  14 us (22%)
  local copies, waits for them, and re-layouts  3.65 us (6%)
    pallas_call x7, Pallas kernels, attend(): pl.pallas_call(functools.partial(attend_kernel, blocks, first, final, tok...  22.5 us
    ppermute x9, starting transfers between devices, move(): return lax.ppermute(x, 'cp', ways[way])  22 us
    ppermute x9, waiting for transfers between devices, move(): return lax.ppermute(x, 'cp', ways[way])  14 us
    unnamed x12, local copies, waits for them, and re-layouts  3.65 us
  transfers between devices with their start and end apart: 9, of which 3 were waited for; matrix products, arithmetic and copies ran while one was open for 0% of the time, Pallas kernels for 30%

profile of v3, /device:TPU:453, one launch (start us, length us, event | category | flops | bytes accessed | tf_op | source)
XLA Modules:
  0.0 62.5 jit_solution(2190656526052737993)
XLA Ops:
  0.0 0.0 copy-start.2
  0.0 0.9 %copy-done.2 = bf16[384,256]{1,0:T(8,128)(2,1)S(1)} copy-done((bf16[384,256]{1,0:T(8,128)(2,1)S(1)}, bf16[384,256]{1,0:T(8,128)(2,1)}, u32[]{:S(2)}) %copy-start.2) | copy-done | bytes 196632
  0.9 0.0 copy-start.3
  0.9 0.9 %copy-done.3 = bf16[384,256]{1,0:T(8,128)(2,1)S(1)} copy-done((bf16[384,256]{1,0:T(8,128)(2,1)S(1)}, bf16[384,256]{1,0:T(8,128)(2,1)}, u32[]{:S(2)}) %copy-start.3) | copy-done | bytes 196632
  1.9 0.0 copy-start.5
  1.9 1.3 %collective-permute-start.1 = (bf16[2,384,256]{2,1,0:T(8,128)(2,1)S(1)}, bf16[2,384,256]{2,1,0:T(8,128)(2,1)S(1)}, u32[]{:S(2)}, u32[]{:S(2)}) collective-permute-start(bf16[2,384,256]{2,1,0:T(8,128)(2,1)S(1)} %shard_map.46.refs_2_), channel_id=1, source_target_pairs={{0,4},{8,12},{16,20},{24,28},{32,36},{40,44},{48,52},{56,60},{64,6... | collective-permute-start | bytes 1179656 | tf_op jit(solution)/shard_map/ppermute | solution.py:228
  3.2 4.2 %collective-permute-start = (bf16[2,384,256]{2,1,0:T(8,128)(2,1)S(1)}, bf16[2,384,256]{2,1,0:T(8,128)(2,1)S(1)}, u32[]{:S(2)}, u32[]{:S(2)}) collective-permute-start(bf16[2,384,256]{2,1,0:T(8,128)(2,1)S(1)} %shard_map.46.refs_2_), channel_id=1, source_target_pairs={{0,12},{4,8},{8,20},{12,16},{16,28},{20,24},{24,36},{28,32},{32,44... | collective-permute-start | bytes 1179656 | tf_op jit(solution)/shard_map/ppermute | solution.py:228
  7.4 4.6 %collective-permute-start.4 = (bf16[2,384,256]{2,1,0:T(8,128)(2,1)S(1)}, bf16[2,384,256]{2,1,0:T(8,128)(2,1)S(1)}, u32[]{:S(2)}, u32[]{:S(2)}) collective-permute-start(bf16[2,384,256]{2,1,0:T(8,128)(2,1)S(1)} %shard_map.46.refs_2_), channel_id=1, source_target_pairs={{4,48},{12,56},{20,0},{28,8},{36,16},{44,24},{52,32},{60,40},{68,1... | collective-permute-start | bytes 1179656 | tf_op jit(solution)/shard_map/ppermute | solution.py:228
  12.1 0.0 copy-start
  12.1 1.1 %copy-done = bf16[384,1024]{1,0:T(8,128)(2,1)S(1)} copy-done((bf16[384,1024]{1,0:T(8,128)(2,1)S(1)}, bf16[384,1024]{1,0:T(8,128)(2,1)}, u32[]{:S(2)}) %copy-start) | copy-done | bytes 786456
  13.2 0.0 copy-start.4
  13.2 0.7 %copy-done.4 = s32[32]{0:T(128)S(1)} copy-done((s32[32]{0:T(128)S(1)}, s32[32]{0:T(128)}, u32[]{:S(2)}) %copy-start.4) | copy-done | bytes 152
  13.8 2.5 %shard_map.47.refs_4_ = f32[6,136,512]{2,1,0:T(8,128)S(1)} custom-call(s32[32]{0:T(128)S(1)} %copy-done.4, bf16[384,1024]{1,0:T(8,128)(2,1)S(1)} %copy-done, bf16[2,384,256]{2,1,0:T(8,128)(2,1)S(1)} %shard_map.46.refs_2_), custom_call_target="tpu_custom_call" | custom-call | flops 603979776 | bytes 1048576 | tf_op jit(solution)/shard_map/pallas_call | solution.py:207
  16.4 0.0 collective-permute-done.1.refs_2_
  16.4 2.8 %collective-permute-done.refs_3_ = bf16[2,384,256]{2,1,0:T(8,128)(2,1)S(1)} collective-permute-done((bf16[2,384,256]{2,1,0:T(8,128)(2,1)S(1)}, bf16[2,384,256]{2,1,0:T(8,128)(2,1)S(1)}, u32[]{:S(2)}, u32[]{:S(2)}) %collective-permute-start) | collective-permute-done | bytes 393248 | tf_op jit(solution)/shard_map/ppermute | solution.py:228
  19.2 2.4 %collective-permute-start.2 = (bf16[2,384,256]{2,1,0:T(8,128)(2,1)S(1)}, bf16[2,384,256]{2,1,0:T(8,128)(2,1)S(1)}, u32[]{:S(2)}, u32[]{:S(2)}) collective-permute-start(bf16[2,384,256]{2,1,0:T(8,128)(2,1)S(1)} %collective-permute-done.refs_3_), channel_id=1, source_target_pairs={{0,4},{4,0},{8,12},{12,8},{16,20},{20,16},{24,28},{28,24},{32,36},... | collective-permute-start | bytes 1179656 | tf_op jit(solution)/shard_map/ppermute | solution.py:228
  21.6 1.9 %collective-permute-start.3 = (bf16[2,384,256]{2,1,0:T(8,128)(2,1)S(1)}, bf16[2,384,256]{2,1,0:T(8,128)(2,1)S(1)}, u32[]{:S(2)}, u32[]{:S(2)}) collective-permute-start(bf16[2,384,256]{2,1,0:T(8,128)(2,1)S(1)} %collective-permute-done.refs_3_), channel_id=1, source_target_pairs={{0,8},{4,12},{8,16},{12,20},{16,24},{20,28},{24,32},{28,36},{32,40... | collective-permute-start | bytes 1179656 | tf_op jit(solution)/shard_map/ppermute | solution.py:228
  23.5 0.0 collective-permute-done.4
  23.5 0.7 %collective-permute-start.5 = (bf16[2,384,256]{2,1,0:T(8,128)(2,1)S(1)}, bf16[2,384,256]{2,1,0:T(8,128)(2,1)S(1)}, u32[]{:S(2)}, u32[]{:S(2)}) collective-permute-start(bf16[2,384,256]{2,1,0:T(8,128)(2,1)S(1)} %collective-permute-done.4), channel_id=1, source_target_pairs={{48,32},{56,40},{0,48},{8,56},{16,64},{24,72},{32,80},{40,88},{112... | collective-permute-start | bytes 1179656 | tf_op jit(solution)/shard_map/ppermute | solution.py:228
  24.2 0.0 copy-done.5
  24.2 4.9 %shard_map.48.refs_3_ = f32[6,136,512]{2,1,0:T(8,128)S(1)} custom-call(s32[32]{0:T(128)S(1)} %copy-done.5, bf16[384,1024]{1,0:T(8,128)(2,1)S(1)} %copy-done, bf16[2,384,256]{2,1,0:T(8,128)(2,1)S(1)} %collective-permute-done.1.refs_2_, bf16[2,384,256]{2,1,0:T(8,128)(2,1)S(1)} %collective-permute-done.refs_3_, ...), custom_call_target="tpu_custom_call", output_to_operand_aliasing={{}: (4, {})} | custom-call | flops 1207959552 | bytes 1048576 | tf_op jit(solution)/shard_map/pallas_call | solution.py:207
  29.2 0.0 copy-start.1
  29.2 0.0 collective-permute-done.2.refs_2_
  29.2 2.7 %shard_map.49.refs_4_ = f32[6,136,512]{2,1,0:T(8,128)S(1)} custom-call(s32[32]{0:T(128)S(1)} %copy-done.5, bf16[384,1024]{1,0:T(8,128)(2,1)S(1)} %copy-done, bf16[2,384,256]{2,1,0:T(8,128)(2,1)S(1)} %collective-permute-done.2.refs_2_, f32[6,136,512]{2,1,0:T(8,128)S(1)} %shard_map.48.refs_3_), custom_call_target="tpu_custom_call", output_to_operand_aliasing={{}: (3, {})} | custom-call | flops 603979776 | bytes 1048576 | tf_op jit(solution)/shard_map/pallas_call | solution.py:207
  31.9 8.2 %collective-permute-done.3.refs_2_.odd_ref = bf16[2,384,256]{2,1,0:T(8,128)(2,1)S(1)} collective-permute-done((bf16[2,384,256]{2,1,0:T(8,128)(2,1)S(1)}, bf16[2,384,256]{2,1,0:T(8,128)(2,1)S(1)}, u32[]{:S(2)}, u32[]{:S(2)}) %collective-permute-start.3) | collective-permute-done | bytes 393248 | tf_op jit(solution)/shard_map/ppermute | solution.py:228
  40.1 3.1 %collective-permute-start.6 = (bf16[2,384,256]{2,1,0:T(8,128)(2,1)S(1)}, bf16[2,384,256]{2,1,0:T(8,128)(2,1)S(1)}, u32[]{:S(2)}, u32[]{:S(2)}) collective-permute-start(bf16[2,384,256]{2,1,0:T(8,128)(2,1)S(1)} %collective-permute-done.3.refs_2_.odd_ref), channel_id=1, source_target_pairs={{0,4},{4,0},{8,12},{12,8},{16,20},{20,16},{24,28},{28,24},{32,36},... | collective-permute-start | bytes 1179656 | tf_op jit(solution)/shard_map/ppermute | solution.py:228
  43.2 0.0 collective-permute-done.5.refs_3_.even_ref
  43.3 1.9 %collective-permute-start.7 = (bf16[2,384,256]{2,1,0:T(8,128)(2,1)S(1)}, bf16[2,384,256]{2,1,0:T(8,128)(2,1)S(1)}, u32[]{:S(2)}, u32[]{:S(2)}) collective-permute-start(bf16[2,384,256]{2,1,0:T(8,128)(2,1)S(1)} %shard_map.52), channel_id=1, source_target_pairs={{32,24},{40,32},{48,40},{56,48},{64,56},{72,64},{80,72},{88,80},{9... | collective-permute-start | bytes 1179656 | tf_op jit(solution)/shard_map/ppermute | solution.py:228
  45.2 0.0 copy-done.1
  45.2 2.9 %shard_map.50.refs_3_ = f32[6,136,512]{2,1,0:T(8,128)S(1)} custom-call(s32[32]{0:T(128)S(1)} %copy-done.5, bf16[384,1024]{1,0:T(8,128)(2,1)S(1)} %copy-done.1, bf16[2,384,256]{2,1,0:T(8,128)(2,1)S(1)} %collective-permute-done.3.refs_2_.odd_ref, bf16[2,384,256]{2,1,0:T(8,128)(2,1)S(1)} %collective-permute-done.5.refs_3_.even_ref, ...), custom_call_target="tpu_custom_call", output_to_operand_aliasing={{}: (4, {})} | custom-call | flops 1207959552 | bytes 1048576 | tf_op jit(solution)/shard_map/pallas_call | solution.py:207
  48.2 0.0 collective-permute-done.6.refs_2_
  48.2 2.7 %shard_map.51.refs_3_ = f32[6,136,512]{2,1,0:T(8,128)S(1)} custom-call(s32[32]{0:T(128)S(1)} %copy-done.5, bf16[384,1024]{1,0:T(8,128)(2,1)S(1)} %copy-done.1, bf16[2,384,256]{2,1,0:T(8,128)(2,1)S(1)} %collective-permute-done.6.refs_2_, f32[6,136,512]{2,1,0:T(8,128)S(1)} %shard_map.50.refs_3_), custom_call_target="tpu_custom_call", output_to_operand_aliasing={{}: (3, {})} | custom-call | flops 603979776 | bytes 1048576 | tf_op jit(solution)/shard_map/pallas_call | solution.py:207
  50.9 3.0 %collective-permute-done.7.refs_2_ = bf16[2,384,256]{2,1,0:T(8,128)(2,1)S(1)} collective-permute-done((bf16[2,384,256]{2,1,0:T(8,128)(2,1)S(1)}, bf16[2,384,256]{2,1,0:T(8,128)(2,1)S(1)}, u32[]{:S(2)}, u32[]{:S(2)}) %collective-permute-start.7) | collective-permute-done | bytes 393248 | tf_op jit(solution)/shard_map/ppermute | solution.py:228
  53.9 1.9 %collective-permute-start.8 = (bf16[2,384,256]{2,1,0:T(8,128)(2,1)S(1)}, bf16[2,384,256]{2,1,0:T(8,128)(2,1)S(1)}, u32[]{:S(2)}, u32[]{:S(2)}) collective-permute-start(bf16[2,384,256]{2,1,0:T(8,128)(2,1)S(1)} %collective-permute-done.7.refs_2_), channel_id=1, source_target_pairs={{0,4},{4,0},{8,12},{12,8},{16,20},{20,16},{24,28},{28,24},{32,36},... | collective-permute-start | bytes 1179656 | tf_op jit(solution)/shard_map/ppermute | solution.py:228
  55.8 2.7 %shard_map.53.refs_3_ = f32[6,136,512]{2,1,0:T(8,128)S(1)} custom-call(s32[32]{0:T(128)S(1)} %copy-done.5, bf16[384,1024]{1,0:T(8,128)(2,1)S(1)} %copy-done.1, bf16[2,384,256]{2,1,0:T(8,128)(2,1)S(1)} %collective-permute-done.7.refs_2_, f32[6,136,512]{2,1,0:T(8,128)S(1)} %shard_map.51.refs_3_), custom_call_target="tpu_custom_call", output_to_operand_aliasing={{}: (3, {})} | custom-call | flops 603979776 | bytes 1048576 | tf_op jit(solution)/shard_map/pallas_call | solution.py:207
  58.5 0.0 collective-permute-done.8.refs_2_
  58.6 3.9 %shard_map.54 = bf16[384,1024]{1,0:T(8,128)(2,1)} custom-call(s32[32]{0:T(128)S(1)} %copy-done.5, bf16[384,1024]{1,0:T(8,128)(2,1)S(1)} %copy-done.1, bf16[2,384,256]{2,1,0:T(8,128)(2,1)S(1)} %collective-permute-done.8.refs_2_, f32[6,136,512]{2,1,0:T(8,128)S(1)} %shard_map.53.refs_3_), custom_call_target="tpu_custom_call" | custom-call | flops 603979776 | bytes 1048576 | tf_op jit(solution)/shard_map/pallas_call | solution.py:207
  (2 shorter events, 0.1 us)
Async XLA Ops:
  0.0 0.9 %copy-start.2 = (bf16[384,256]{1,0:T(8,128)(2,1)S(1)}, bf16[384,256]{1,0:T(8,128)(2,1)}, u32[]{:S(2)}) copy-start(bf16[384,256]{1,0:T(8,128)(2,1)} %k_ref.1) | copy-start | bytes 589828
  0.9 0.9 %copy-start.3 = (bf16[384,256]{1,0:T(8,128)(2,1)S(1)}, bf16[384,256]{1,0:T(8,128)(2,1)}, u32[]{:S(2)}) copy-start(bf16[384,256]{1,0:T(8,128)(2,1)} %v_ref.1) | copy-start | bytes 589828
  1.9 22.3 %copy-start.5 = (s32[32]{0:T(128)S(1)}, s32[32]{0:T(128)}, u32[]{:S(2)}) copy-start(s32[32]{0:T(128)} %refs_0_.13) | copy-start | bytes 388
  1.9 14.5 %collective-permute-start.1 = (bf16[2,384,256]{2,1,0:T(8,128)(2,1)S(1)}, bf16[2,384,256]{2,1,0:T(8,128)(2,1)S(1)}, u32[]{:S(2)}, u32[]{:S(2)}) collective-permute-start(bf16[2,384,256]{2,1,0:T(8,128)(2,1)S(1)} %shard_map.46.refs_2_), channel_id=1, source_target_pairs={{0,4},{8,12},{16,20},{24,28},{32,36},{40,44},{48,52},{56,60},{64,6... | collective-permute-start | bytes 1179656 | tf_op jit(solution)/shard_map/ppermute | solution.py:228
  3.2 16.0 %collective-permute-start = (bf16[2,384,256]{2,1,0:T(8,128)(2,1)S(1)}, bf16[2,384,256]{2,1,0:T(8,128)(2,1)S(1)}, u32[]{:S(2)}, u32[]{:S(2)}) collective-permute-start(bf16[2,384,256]{2,1,0:T(8,128)(2,1)S(1)} %shard_map.46.refs_2_), channel_id=1, source_target_pairs={{0,12},{4,8},{8,20},{12,16},{16,28},{20,24},{24,36},{28,32},{32,44... | collective-permute-start | bytes 1179656 | tf_op jit(solution)/shard_map/ppermute | solution.py:228
  7.4 16.1 %collective-permute-start.4 = (bf16[2,384,256]{2,1,0:T(8,128)(2,1)S(1)}, bf16[2,384,256]{2,1,0:T(8,128)(2,1)S(1)}, u32[]{:S(2)}, u32[]{:S(2)}) collective-permute-start(bf16[2,384,256]{2,1,0:T(8,128)(2,1)S(1)} %shard_map.46.refs_2_), channel_id=1, source_target_pairs={{4,48},{12,56},{20,0},{28,8},{36,16},{44,24},{52,32},{60,40},{68,1... | collective-permute-start | bytes 1179656 | tf_op jit(solution)/shard_map/ppermute | solution.py:228
  12.1 1.1 %copy-start = (bf16[384,1024]{1,0:T(8,128)(2,1)S(1)}, bf16[384,1024]{1,0:T(8,128)(2,1)}, u32[]{:S(2)}) copy-start(bf16[384,1024]{1,0:T(8,128)(2,1)} %refs_1_.13) | copy-start | bytes 2359300
  13.2 0.7 %copy-start.4 = (s32[32]{0:T(128)S(1)}, s32[32]{0:T(128)}, u32[]{:S(2)}) copy-start(s32[32]{0:T(128)} %refs_0_.13) | copy-start | bytes 388
  19.2 10.0 %collective-permute-start.2 = (bf16[2,384,256]{2,1,0:T(8,128)(2,1)S(1)}, bf16[2,384,256]{2,1,0:T(8,128)(2,1)S(1)}, u32[]{:S(2)}, u32[]{:S(2)}) collective-permute-start(bf16[2,384,256]{2,1,0:T(8,128)(2,1)S(1)} %collective-permute-done.refs_3_), channel_id=1, source_target_pairs={{0,4},{4,0},{8,12},{12,8},{16,20},{20,16},{24,28},{28,24},{32,36},... | collective-permute-start | bytes 1179656 | tf_op jit(solution)/shard_map/ppermute | solution.py:228
  21.6 18.6 %collective-permute-start.3 = (bf16[2,384,256]{2,1,0:T(8,128)(2,1)S(1)}, bf16[2,384,256]{2,1,0:T(8,128)(2,1)S(1)}, u32[]{:S(2)}, u32[]{:S(2)}) collective-permute-start(bf16[2,384,256]{2,1,0:T(8,128)(2,1)S(1)} %collective-permute-done.refs_3_), channel_id=1, source_target_pairs={{0,8},{4,12},{8,16},{12,20},{16,24},{20,28},{24,32},{28,36},{32,40... | collective-permute-start | bytes 1179656 | tf_op jit(solution)/shard_map/ppermute | solution.py:228
  23.5 19.7 %collective-permute-start.5 = (bf16[2,384,256]{2,1,0:T(8,128)(2,1)S(1)}, bf16[2,384,256]{2,1,0:T(8,128)(2,1)S(1)}, u32[]{:S(2)}, u32[]{:S(2)}) collective-permute-start(bf16[2,384,256]{2,1,0:T(8,128)(2,1)S(1)} %collective-permute-done.4), channel_id=1, source_target_pairs={{48,32},{56,40},{0,48},{8,56},{16,64},{24,72},{32,80},{40,88},{112... | collective-permute-start | bytes 1179656 | tf_op jit(solution)/shard_map/ppermute | solution.py:228
  29.2 16.0 %copy-start.1 = (bf16[384,1024]{1,0:T(8,128)(2,1)S(1)}, bf16[384,1024]{1,0:T(8,128)(2,1)}, u32[]{:S(2)}) copy-start(bf16[384,1024]{1,0:T(8,128)(2,1)} %refs_1_.13) | copy-start | bytes 2359300
  40.1 8.0 %collective-permute-start.6 = (bf16[2,384,256]{2,1,0:T(8,128)(2,1)S(1)}, bf16[2,384,256]{2,1,0:T(8,128)(2,1)S(1)}, u32[]{:S(2)}, u32[]{:S(2)}) collective-permute-start(bf16[2,384,256]{2,1,0:T(8,128)(2,1)S(1)} %collective-permute-done.3.refs_2_.odd_ref), channel_id=1, source_target_pairs={{0,4},{4,0},{8,12},{12,8},{16,20},{20,16},{24,28},{28,24},{32,36},... | collective-permute-start | bytes 1179656 | tf_op jit(solution)/shard_map/ppermute | solution.py:228
  43.3 10.6 %collective-permute-start.7 = (bf16[2,384,256]{2,1,0:T(8,128)(2,1)S(1)}, bf16[2,384,256]{2,1,0:T(8,128)(2,1)S(1)}, u32[]{:S(2)}, u32[]{:S(2)}) collective-permute-start(bf16[2,384,256]{2,1,0:T(8,128)(2,1)S(1)} %shard_map.52), channel_id=1, source_target_pairs={{32,24},{40,32},{48,40},{56,48},{64,56},{72,64},{80,72},{88,80},{9... | collective-permute-start | bytes 1179656 | tf_op jit(solution)/shard_map/ppermute | solution.py:228
  53.9 4.7 %collective-permute-start.8 = (bf16[2,384,256]{2,1,0:T(8,128)(2,1)S(1)}, bf16[2,384,256]{2,1,0:T(8,128)(2,1)S(1)}, u32[]{:S(2)}, u32[]{:S(2)}) collective-permute-start(bf16[2,384,256]{2,1,0:T(8,128)(2,1)S(1)} %collective-permute-done.7.refs_2_), channel_id=1, source_target_pairs={{0,4},{4,0},{8,12},{12,8},{16,20},{20,16},{24,28},{28,24},{32,36},... | collective-permute-start | bytes 1179656 | tf_op jit(solution)/shard_map/ppermute | solution.py:228

commit v4 on v3

--- a/solution.py
+++ b/solution.py
@@ -23,23 +23,23 @@
     chips = count // 2
     dev = lambda n, c: 2 * n + c
     back = lambda n: n - n % RING + (n % RING - RING // 4) % RING
-    inside = [n for n in range(chips) if n + 3 < chips]
+    inside = [n for n in range(chips) if n + 4 < chips]
     return {
         "cross": [(dev(n, c), dev(n + 1, 1 - c)) for n in range(chips - 1) for c in (0, 1)],
         "ahead": [(dev(n, c), dev(n + 1, c)) for n in range(chips - 1) for c in (0, 1)],
         "swap": [(dev(n, c), dev(n, 1 - c)) for n in range(chips) for c in (0, 1)],
-        "mate": [(dev(n, 0), dev(n, 1)) for n in range(chips)],
-        "back1": [(dev(n, 1), dev(back(n), 0)) for n in inside],
-        "back2": [(dev(back(n), 0), dev((n + 4) % chips, 0)) for n in inside],
-        "last": [(dev((n + 4) % chips, 0), dev(n + 3, 0)) for n in inside]
-        + [(dev(n, 1), dev(n + 1, 1)) for n in range(chips - 1)],
+        "back1": [(dev(n, 1), dev(back(n), 0)) for n in inside] + [(dev(n, 0), dev(n, 1)) for n in range(chips)],
+        "back2": [(dev(back(n), 0), dev(n + 4, 0)) for n in inside],
     }
 
 
 def attend_kernel(blocks, first, final, tok, heads, group, *refs):
     refs = list(refs)
     lengths, q_ref = refs.pop(0), refs.pop(0)
-    kv_refs = [refs.pop(0) for _ in blocks]
+    kv_refs = []
+    while len(kv_refs) < len(blocks):
+        ref = refs.pop(0)
+        kv_refs += [ref] if len(ref.shape) == 3 else [ref.at[j] for j in range(ref.shape[0])]
     state_in = None if first else refs.pop(0)
     out_ref = refs.pop(0)
     s_ref, p_ref, mask_ref = refs.pop(0), refs.pop(0), refs.pop(0)
@@ -164,46 +164,17 @@
                     at, left = at + m, left - m
 
 
-def small_call(kernel, outs, *args):
-    vmem = pl.BlockSpec(memory_space=pltpu.VMEM)
-    return pl.pallas_call(
-        kernel,
-        out_shape=outs,
-        in_specs=[vmem] * len(args),
-        out_specs=jax.tree.map(lambda _: vmem, outs),
-        compiler_params=pltpu.CompilerParams(vmem_limit_bytes=4 << 20),
-        cost_estimate=pl.CostEstimate(flops=1 << 20, bytes_accessed=1 << 20, transcendentals=0),
-    )(*args)
-
-
-def stack_kernel(k_ref, v_ref, out_ref):
-    out_ref[0] = k_ref[...]
-    out_ref[1] = v_ref[...]
-
-
-def pick_kernel(even_ref, odd_ref, out_ref):
-    odd = lax.axis_index("cp") % 2 == 1
-
-    @pl.when(odd)
-    def _():
-        out_ref[...] = odd_ref[...]
-
-    @pl.when(jnp.logical_not(odd))
-    def _():
-        out_ref[...] = even_ref[...]
-
-
 def attend(lengths, queries, kvs, blocks, state, final):
     tok, width = queries.shape
-    heads = kvs[0].shape[2] // HEAD_DIM
-    group = width // kvs[0].shape[2]
+    heads = kvs[0].shape[-1] // HEAD_DIM
+    group = width // kvs[0].shape[-1]
     count = heads * group * tok // TILE
     first = state is None
     state_shape = jax.ShapeDtypeStruct((count, HEAD_DIM + 8, TILE), jnp.float32)
     vmem = pl.BlockSpec(memory_space=pltpu.VMEM)
     args = [lengths, queries, *kvs] + ([] if first else [state])
     aliases = {} if first or final else {len(args) - 1: 0}
-    flops = 4 * tok * tok * width * len(kvs)
+    flops = 4 * tok * tok * width * len(blocks)
     return pl.pallas_call(
         functools.partial(attend_kernel, blocks, first, final, tok, heads, group),
         out_shape=jax.ShapeDtypeStruct((tok, width), jnp.bfloat16) if final else state_shape,
@@ -228,25 +199,25 @@
         return lax.ppermute(x, "cp", ways[way])
 
     after = lax.optimization_barrier
+    own = jnp.stack([keys, values])
     step = functools.partial(attend, lengths, queries)
-    own = small_call(stack_kernel, jax.ShapeDtypeStruct((2, *keys.shape), keys.dtype), keys, values)
     got1 = move(own, "cross")
-    far1 = move(own, "back1")
-    mate0 = move(own, "mate")
+    mix1 = move(own, "back1")
     state = step([own], [(0, 0)], None, False)
-    state, got1, mate0 = after((state, got1, mate0))
+    state, got1 = after((state, got1))
     got2 = move(got1, "ahead")
-    far2 = move(far1, "back2")
     mate1 = move(got1, "swap")
-    state = step([mate0, got1], [(NONE, 1), (1, 3)], state, False)
+    far2 = move(mix1, "back2")
+    state = step([mix1, got1], [(NONE, 1), (1, 3)], state, False)
     state, mate1 = after((state, mate1))
     state = step([mate1], [(2, 2)], state, False)
     state, got2 = after((state, got2))
-    got3 = move(small_call(pick_kernel, jax.ShapeDtypeStruct(got2.shape, got2.dtype), far2, got2), "last")
+    got3 = move(got2, "ahead")
     mate2 = move(got2, "swap")
-    state = step([got2, far2], [(3, 5), (7, NONE)], state, False)
+    state = step([got2], [(3, 5)], state, False)
     state, mate2 = after((state, mate2))
-    state = step([mate2], [(4, 4)], state, False)
+    state, far2 = after((state, far2))
+    state = step([mate2, far2], [(4, 4), (7, NONE)], state, False)
     state, got3 = after((state, got3))
     mate3 = move(got3, "swap")
     state = step([got3], [(5, 7)], state, False)

time: 62.9 us -> 65.7 us (1.045)
  the two profiles are of different devices: /device:TPU:453 before, /device:TPU:455 now
where the time goes in v4:
time: 65.7 us; the launch traced here: 65.4 us
  starting transfers between devices  22.5 us (34%)
  Pallas kernels  22.5 us (34%)
  waiting for transfers between devices  17.4 us (26%)
  local copies, waits for them, and re-layouts  1.78 us (3%)
  other arithmetic  1.06 us (2%)
    pallas_call x7, Pallas kernels, attend(): pl.pallas_call(functools.partial(attend_kernel, blocks, first, final, tok...  22.5 us
    ppermute x8, starting transfers between devices, move(): return lax.ppermute(x, 'cp', ways[way])  22.5 us
    ppermute x8, waiting for transfers between devices, move(): return lax.ppermute(x, 'cp', ways[way])  17.4 us
    unnamed x4, local copies, waits for them, and re-layouts  1.78 us
  transfers between devices with their start and end apart: 8, of which 3 were waited for; matrix products, arithmetic and copies ran while one was open for 0% of the time, Pallas kernels for 28%

profile of v4, /device:TPU:455, one launch (start us, length us, event | category | flops | bytes accessed | tf_op | source)
XLA Modules:
  0.0 65.4 jit_solution(10976452936080549948)
XLA Ops:
  0.0 1.1 %pad_maximum_fusion.refs_2_ = bf16[2,384,256]{2,1,0:T(8,128)(2,1)S(1)} fusion(bf16[1,384,256]{2,1,0:T(8,128)(2,1)} %bitcast.2, bf16[1,384,256]{2,1,0:T(8,128)(2,1)} %bitcast.3), kind=kLoop, calls=%fused_computation | loop fusion | flops 196608 | bytes 786432 | tf_op jit(solution)/shard_map/stack | solution.py:202
  1.1 3.8 %collective-permute-start.1 = (bf16[2,384,256]{2,1,0:T(8,128)(2,1)S(1)}, bf16[2,384,256]{2,1,0:T(8,128)(2,1)S(1)}, u32[]{:S(2)}, u32[]{:S(2)}) collective-permute-start(bf16[2,384,256]{2,1,0:T(8,128)(2,1)S(1)} %pad_maximum_fusion.refs_2_), channel_id=1, source_target_pairs={{0,12},{4,8},{8,20},{12,16},{16,28},{20,24},{24,36},{28,32},{32,44... | collective-permute-start | bytes 1179656 | tf_op jit(solution)/shard_map/ppermute | solution.py:199
  4.8 4.7 %collective-permute-start = (bf16[2,384,256]{2,1,0:T(8,128)(2,1)S(1)}, bf16[2,384,256]{2,1,0:T(8,128)(2,1)S(1)}, u32[]{:S(2)}, u32[]{:S(2)}) collective-permute-start(bf16[2,384,256]{2,1,0:T(8,128)(2,1)S(1)} %pad_maximum_fusion.refs_2_), channel_id=1, source_target_pairs={{4,48},{12,56},{20,0},{28,8},{36,16},{44,24},{52,32},{60,40},{68,1... | collective-permute-start | bytes 1179656 | tf_op jit(solution)/shard_map/ppermute | solution.py:199
  9.5 0.0 copy-start
  9.6 1.1 %copy-done = bf16[384,1024]{1,0:T(8,128)(2,1)S(1)} copy-done((bf16[384,1024]{1,0:T(8,128)(2,1)S(1)}, bf16[384,1024]{1,0:T(8,128)(2,1)}, u32[]{:S(2)}) %copy-start) | copy-done | bytes 786456
  10.7 0.0 copy-start.1
  10.7 0.7 copy-done.1
  11.3 2.5 %shard_map.46.refs_4_ = f32[6,136,512]{2,1,0:T(8,128)S(1)} custom-call(s32[32]{0:T(128)S(1)} %copy-done.1, bf16[384,1024]{1,0:T(8,128)(2,1)S(1)} %copy-done, bf16[2,384,256]{2,1,0:T(8,128)(2,1)S(1)} %pad_maximum_fusion.refs_2_), custom_call_target="tpu_custom_call" | custom-call | flops 603979776 | bytes 1048576 | tf_op jit(solution)/shard_map/pallas_call | solution.py:178
  13.9 2.9 %collective-permute-done.1.refs_3_ = bf16[2,384,256]{2,1,0:T(8,128)(2,1)S(1)} collective-permute-done((bf16[2,384,256]{2,1,0:T(8,128)(2,1)S(1)}, bf16[2,384,256]{2,1,0:T(8,128)(2,1)S(1)}, u32[]{:S(2)}, u32[]{:S(2)}) %collective-permute-start.1) | collective-permute-done | bytes 393248 | tf_op jit(solution)/shard_map/ppermute | solution.py:199
  16.7 2.3 %collective-permute-start.2 = (bf16[2,384,256]{2,1,0:T(8,128)(2,1)S(1)}, bf16[2,384,256]{2,1,0:T(8,128)(2,1)S(1)}, u32[]{:S(2)}, u32[]{:S(2)}) collective-permute-start(bf16[2,384,256]{2,1,0:T(8,128)(2,1)S(1)} %collective-permute-done.1.refs_3_), channel_id=1, source_target_pairs={{0,4},{4,0},{8,12},{12,8},{16,20},{20,16},{24,28},{28,24},{32,36},... | collective-permute-start | bytes 1179656 | tf_op jit(solution)/shard_map/ppermute | solution.py:199
  19.0 1.9 %collective-permute-start.3 = (bf16[2,384,256]{2,1,0:T(8,128)(2,1)S(1)}, bf16[2,384,256]{2,1,0:T(8,128)(2,1)S(1)}, u32[]{:S(2)}, u32[]{:S(2)}) collective-permute-start(bf16[2,384,256]{2,1,0:T(8,128)(2,1)S(1)} %collective-permute-done.1.refs_3_), channel_id=1, source_target_pairs={{0,8},{4,12},{8,16},{12,20},{16,24},{20,28},{24,32},{28,36},{32,40... | collective-permute-start | bytes 1179656 | tf_op jit(solution)/shard_map/ppermute | solution.py:199
  21.0 0.0 collective-permute-done.refs_2_
  21.0 4.9 %shard_map.47.refs_3_ = f32[6,136,512]{2,1,0:T(8,128)S(1)} custom-call(s32[32]{0:T(128)S(1)} %copy-done.1, bf16[384,1024]{1,0:T(8,128)(2,1)S(1)} %copy-done, bf16[2,384,256]{2,1,0:T(8,128)(2,1)S(1)} %collective-permute-done.refs_2_, bf16[2,384,256]{2,1,0:T(8,128)(2,1)S(1)} %collective-permute-done.1.refs_3_, ...), custom_call_target="tpu_custom_call", output_to_operand_aliasing={{}: (4, {})} | custom-call | flops 1207959552 | bytes 1048576 | tf_op jit(solution)/shard_map/pallas_call | solution.py:178
  25.9 0.0 collective-permute-done.2.refs_2_
  25.9 2.7 %shard_map.48.refs_3_ = f32[6,136,512]{2,1,0:T(8,128)S(1)} custom-call(s32[32]{0:T(128)S(1)} %copy-done.1, bf16[384,1024]{1,0:T(8,128)(2,1)S(1)} %copy-done, bf16[2,384,256]{2,1,0:T(8,128)(2,1)S(1)} %collective-permute-done.2.refs_2_, f32[6,136,512]{2,1,0:T(8,128)S(1)} %shard_map.47.refs_3_), custom_call_target="tpu_custom_call", output_to_operand_aliasing={{}: (3, {})} | custom-call | flops 603979776 | bytes 1048576 | tf_op jit(solution)/shard_map/pallas_call | solution.py:178
  28.7 4.9 %collective-permute-done.3.refs_2_ = bf16[2,384,256]{2,1,0:T(8,128)(2,1)S(1)} collective-permute-done((bf16[2,384,256]{2,1,0:T(8,128)(2,1)S(1)}, bf16[2,384,256]{2,1,0:T(8,128)(2,1)S(1)}, u32[]{:S(2)}, u32[]{:S(2)}) %collective-permute-start.3) | collective-permute-done | bytes 393248 | tf_op jit(solution)/shard_map/ppermute | solution.py:199
  33.6 2.9 %collective-permute-start.4 = (bf16[2,384,256]{2,1,0:T(8,128)(2,1)S(1)}, bf16[2,384,256]{2,1,0:T(8,128)(2,1)S(1)}, u32[]{:S(2)}, u32[]{:S(2)}) collective-permute-start(bf16[2,384,256]{2,1,0:T(8,128)(2,1)S(1)} %collective-permute-done.3.refs_2_), channel_id=1, source_target_pairs={{0,4},{4,0},{8,12},{12,8},{16,20},{20,16},{24,28},{28,24},{32,36},... | collective-permute-start | bytes 1179656 | tf_op jit(solution)/shard_map/ppermute | solution.py:199
  36.5 0.7 %collective-permute-start.5 = (bf16[2,384,256]{2,1,0:T(8,128)(2,1)S(1)}, bf16[2,384,256]{2,1,0:T(8,128)(2,1)S(1)}, u32[]{:S(2)}, u32[]{:S(2)}) collective-permute-start(bf16[2,384,256]{2,1,0:T(8,128)(2,1)S(1)} %collective-permute-done.refs_2_), channel_id=1, source_target_pairs={{48,32},{56,40},{0,48},{8,56},{16,64},{24,72},{32,80},{40,88},{112... | collective-permute-start | bytes 1179656 | tf_op jit(solution)/shard_map/ppermute | solution.py:199
  37.2 1.9 %collective-permute-start.6 = (bf16[2,384,256]{2,1,0:T(8,128)(2,1)S(1)}, bf16[2,384,256]{2,1,0:T(8,128)(2,1)S(1)}, u32[]{:S(2)}, u32[]{:S(2)}) collective-permute-start(bf16[2,384,256]{2,1,0:T(8,128)(2,1)S(1)} %collective-permute-done.3.refs_2_), channel_id=1, source_target_pairs={{0,8},{4,12},{8,16},{12,20},{16,24},{20,28},{24,32},{28,36},{32,40... | collective-permute-start | bytes 1179656 | tf_op jit(solution)/shard_map/ppermute | solution.py:199
  39.1 2.7 %shard_map.49.refs_4_ = f32[6,136,512]{2,1,0:T(8,128)S(1)} custom-call(s32[32]{0:T(128)S(1)} %copy-done.1, bf16[384,1024]{1,0:T(8,128)(2,1)S(1)} %copy-done, bf16[2,384,256]{2,1,0:T(8,128)(2,1)S(1)} %collective-permute-done.3.refs_2_, f32[6,136,512]{2,1,0:T(8,128)S(1)} %shard_map.48.refs_3_), custom_call_target="tpu_custom_call", output_to_operand_aliasing={{}: (3, {})} | custom-call | flops 603979776 | bytes 1048576 | tf_op jit(solution)/shard_map/pallas_call | solution.py:178
  41.8 0.0 collective-permute-done.4.refs_2_
  41.8 0.0 collective-permute-done.5.refs_3_
  41.9 3.0 %shard_map.50.refs_3_ = f32[6,136,512]{2,1,0:T(8,128)S(1)} custom-call(s32[32]{0:T(128)S(1)} %copy-done.1, bf16[384,1024]{1,0:T(8,128)(2,1)S(1)} %copy-done, bf16[2,384,256]{2,1,0:T(8,128)(2,1)S(1)} %collective-permute-done.4.refs_2_, bf16[2,384,256]{2,1,0:T(8,128)(2,1)S(1)} %collective-permute-done.5.refs_3_, ...), custom_call_target="tpu_custom_call", output_to_operand_aliasing={{}: (4, {})} | custom-call | flops 1207959552 | bytes 1048576 | tf_op jit(solution)/shard_map/pallas_call | solution.py:178
  44.8 9.6 %collective-permute-done.6.refs_2_ = bf16[2,384,256]{2,1,0:T(8,128)(2,1)S(1)} collective-permute-done((bf16[2,384,256]{2,1,0:T(8,128)(2,1)S(1)}, bf16[2,384,256]{2,1,0:T(8,128)(2,1)S(1)}, u32[]{:S(2)}, u32[]{:S(2)}) %collective-permute-start.6) | collective-permute-done | bytes 393248 | tf_op jit(solution)/shard_map/ppermute | solution.py:199
  54.4 4.3 %collective-permute-start.7 = (bf16[2,384,256]{2,1,0:T(8,128)(2,1)S(1)}, bf16[2,384,256]{2,1,0:T(8,128)(2,1)S(1)}, u32[]{:S(2)}, u32[]{:S(2)}) collective-permute-start(bf16[2,384,256]{2,1,0:T(8,128)(2,1)S(1)} %collective-permute-done.6.refs_2_), channel_id=1, source_target_pairs={{0,4},{4,0},{8,12},{12,8},{16,20},{20,16},{24,28},{28,24},{32,36},... | collective-permute-start | bytes 1179656 | tf_op jit(solution)/shard_map/ppermute | solution.py:199
  58.7 2.7 %shard_map.51.refs_3_ = f32[6,136,512]{2,1,0:T(8,128)S(1)} custom-call(s32[32]{0:T(128)S(1)} %copy-done.1, bf16[384,1024]{1,0:T(8,128)(2,1)S(1)} %copy-done, bf16[2,384,256]{2,1,0:T(8,128)(2,1)S(1)} %collective-permute-done.6.refs_2_, f32[6,136,512]{2,1,0:T(8,128)S(1)} %shard_map.50.refs_3_), custom_call_target="tpu_custom_call", output_to_operand_aliasing={{}: (3, {})} | custom-call | flops 603979776 | bytes 1048576 | tf_op jit(solution)/shard_map/pallas_call | solution.py:178
  61.4 0.0 collective-permute-done.7.refs_2_
  61.4 3.9 %shard_map.52 = bf16[384,1024]{1,0:T(8,128)(2,1)} custom-call(s32[32]{0:T(128)S(1)} %copy-done.1, bf16[384,1024]{1,0:T(8,128)(2,1)S(1)} %copy-done, bf16[2,384,256]{2,1,0:T(8,128)(2,1)S(1)} %collective-permute-done.7.refs_2_, f32[6,136,512]{2,1,0:T(8,128)S(1)} %shard_map.51.refs_3_), custom_call_target="tpu_custom_call" | custom-call | flops 603979776 | bytes 1048576 | tf_op jit(solution)/shard_map/pallas_call | solution.py:178
Async XLA Ops:
  1.1 15.7 %collective-permute-start.1 = (bf16[2,384,256]{2,1,0:T(8,128)(2,1)S(1)}, bf16[2,384,256]{2,1,0:T(8,128)(2,1)S(1)}, u32[]{:S(2)}, u32[]{:S(2)}) collective-permute-start(bf16[2,384,256]{2,1,0:T(8,128)(2,1)S(1)} %pad_maximum_fusion.refs_2_), channel_id=1, source_target_pairs={{0,12},{4,8},{8,20},{12,16},{16,28},{20,24},{24,36},{28,32},{32,44... | collective-permute-start | bytes 1179656 | tf_op jit(solution)/shard_map/ppermute | solution.py:199
  4.8 16.1 %collective-permute-start = (bf16[2,384,256]{2,1,0:T(8,128)(2,1)S(1)}, bf16[2,384,256]{2,1,0:T(8,128)(2,1)S(1)}, u32[]{:S(2)}, u32[]{:S(2)}) collective-permute-start(bf16[2,384,256]{2,1,0:T(8,128)(2,1)S(1)} %pad_maximum_fusion.refs_2_), channel_id=1, source_target_pairs={{4,48},{12,56},{20,0},{28,8},{36,16},{44,24},{52,32},{60,40},{68,1... | collective-permute-start | bytes 1179656 | tf_op jit(solution)/shard_map/ppermute | solution.py:199
  9.5 1.1 %copy-start = (bf16[384,1024]{1,0:T(8,128)(2,1)S(1)}, bf16[384,1024]{1,0:T(8,128)(2,1)}, u32[]{:S(2)}) copy-start(bf16[384,1024]{1,0:T(8,128)(2,1)} %refs_1_.13) | copy-start | bytes 2359300
  10.7 0.7 %copy-start.1 = (s32[32]{0:T(128)S(1)}, s32[32]{0:T(128)}, u32[]{:S(2)}) copy-start(s32[32]{0:T(128)} %refs_0_.13) | copy-start | bytes 388
  16.7 9.2 %collective-permute-start.2 = (bf16[2,384,256]{2,1,0:T(8,128)(2,1)S(1)}, bf16[2,384,256]{2,1,0:T(8,128)(2,1)S(1)}, u32[]{:S(2)}, u32[]{:S(2)}) collective-permute-start(bf16[2,384,256]{2,1,0:T(8,128)(2,1)S(1)} %collective-permute-done.1.refs_3_), channel_id=1, source_target_pairs={{0,4},{4,0},{8,12},{12,8},{16,20},{20,16},{24,28},{28,24},{32,36},... | collective-permute-start | bytes 1179656 | tf_op jit(solution)/shard_map/ppermute | solution.py:199
  19.0 14.6 %collective-permute-start.3 = (bf16[2,384,256]{2,1,0:T(8,128)(2,1)S(1)}, bf16[2,384,256]{2,1,0:T(8,128)(2,1)S(1)}, u32[]{:S(2)}, u32[]{:S(2)}) collective-permute-start(bf16[2,384,256]{2,1,0:T(8,128)(2,1)S(1)} %collective-permute-done.1.refs_3_), channel_id=1, source_target_pairs={{0,8},{4,12},{8,16},{12,20},{16,24},{20,28},{24,32},{28,36},{32,40... | collective-permute-start | bytes 1179656 | tf_op jit(solution)/shard_map/ppermute | solution.py:199
  33.6 8.2 %collective-permute-start.4 = (bf16[2,384,256]{2,1,0:T(8,128)(2,1)S(1)}, bf16[2,384,256]{2,1,0:T(8,128)(2,1)S(1)}, u32[]{:S(2)}, u32[]{:S(2)}) collective-permute-start(bf16[2,384,256]{2,1,0:T(8,128)(2,1)S(1)} %collective-permute-done.3.refs_2_), channel_id=1, source_target_pairs={{0,4},{4,0},{8,12},{12,8},{16,20},{20,16},{24,28},{28,24},{32,36},... | collective-permute-start | bytes 1179656 | tf_op jit(solution)/shard_map/ppermute | solution.py:199
  36.5 5.4 %collective-permute-start.5 = (bf16[2,384,256]{2,1,0:T(8,128)(2,1)S(1)}, bf16[2,384,256]{2,1,0:T(8,128)(2,1)S(1)}, u32[]{:S(2)}, u32[]{:S(2)}) collective-permute-start(bf16[2,384,256]{2,1,0:T(8,128)(2,1)S(1)} %collective-permute-done.refs_2_), channel_id=1, source_target_pairs={{48,32},{56,40},{0,48},{8,56},{16,64},{24,72},{32,80},{40,88},{112... | collective-permute-start | bytes 1179656 | tf_op jit(solution)/shard_map/ppermute | solution.py:199
  37.2 17.2 %collective-permute-start.6 = (bf16[2,384,256]{2,1,0:T(8,128)(2,1)S(1)}, bf16[2,384,256]{2,1,0:T(8,128)(2,1)S(1)}, u32[]{:S(2)}, u32[]{:S(2)}) collective-permute-start(bf16[2,384,256]{2,1,0:T(8,128)(2,1)S(1)} %collective-permute-done.3.refs_2_), channel_id=1, source_target_pairs={{0,8},{4,12},{8,16},{12,20},{16,24},{20,28},{24,32},{28,36},{32,40... | collective-permute-start | bytes 1179656 | tf_op jit(solution)/shard_map/ppermute | solution.py:199
  54.4 7.1 %collective-permute-start.7 = (bf16[2,384,256]{2,1,0:T(8,128)(2,1)S(1)}, bf16[2,384,256]{2,1,0:T(8,128)(2,1)S(1)}, u32[]{:S(2)}, u32[]{:S(2)}) collective-permute-start(bf16[2,384,256]{2,1,0:T(8,128)(2,1)S(1)} %collective-permute-done.6.refs_2_), channel_id=1, source_target_pairs={{0,4},{4,0},{8,12},{12,8},{16,20},{20,16},{24,28},{28,24},{32,36},... | collective-permute-start | bytes 1179656 | tf_op jit(solution)/shard_map/ppermute | solution.py:199

commit v5 on v4

--- a/solution.py
+++ b/solution.py
@@ -10,13 +10,13 @@
 
 HEAD_DIM = 128
 RING = 8
-TILE = 512
+TILE = 256
 LANES = 128
 NEG = -1e30
 SCALE = HEAD_DIM**-0.5 * 1.4426950408889634
 NONE = 1 << 20
-DEPTH = 2
-BATCH = 1
+DEPTH = 6
+BATCH = 3
 
 
 def routes(count):

time: 65.7 us -> 65.6 us (level)
  the two profiles are of different devices: /device:TPU:455 before, /device:TPU:451 now
where the time goes in v5:
time: 65.6 us; the launch traced here: 65.3 us
  starting transfers between devices  22.5 us (34%)
  Pallas kernels  22.2 us (34%)
  waiting for transfers between devices  17.6 us (27%)
  local copies, waits for them, and re-layouts  1.78 us (3%)
  other arithmetic  1.06 us (2%)
    ppermute x8, starting transfers between devices, move(): return lax.ppermute(x, 'cp', ways[way])  22.5 us
    pallas_call x7, Pallas kernels, attend(): pl.pallas_call(functools.partial(attend_kernel, blocks, first, final, tok...  22.2 us
    ppermute x8, waiting for transfers between devices, move(): return lax.ppermute(x, 'cp', ways[way])  17.6 us
    unnamed x4, local copies, waits for them, and re-layouts  1.78 us
  transfers between devices with their start and end apart: 8, of which 3 were waited for; matrix products, arithmetic and copies ran while one was open for 0% of the time, Pallas kernels for 28%

profile of v5, /device:TPU:451, one launch (start us, length us, event | category | flops | bytes accessed | tf_op | source)
XLA Modules:
  0.0 65.3 jit_solution(16462299542830469792)
XLA Ops:
  0.0 1.1 %pad_maximum_fusion.refs_2_ = bf16[2,384,256]{2,1,0:T(8,128)(2,1)S(1)} fusion(bf16[1,384,256]{2,1,0:T(8,128)(2,1)} %bitcast.2, bf16[1,384,256]{2,1,0:T(8,128)(2,1)} %bitcast.3), kind=kLoop, calls=%fused_computation | loop fusion | flops 196608 | bytes 786432 | tf_op jit(solution)/shard_map/stack | solution.py:202
  1.1 3.8 %collective-permute-start.1 = (bf16[2,384,256]{2,1,0:T(8,128)(2,1)S(1)}, bf16[2,384,256]{2,1,0:T(8,128)(2,1)S(1)}, u32[]{:S(2)}, u32[]{:S(2)}) collective-permute-start(bf16[2,384,256]{2,1,0:T(8,128)(2,1)S(1)} %pad_maximum_fusion.refs_2_), channel_id=1, source_target_pairs={{0,12},{4,8},{8,20},{12,16},{16,28},{20,24},{24,36},{28,32},{32,44... | collective-permute-start | bytes 1179656 | tf_op jit(solution)/shard_map/ppermute | solution.py:199
  4.8 4.7 %collective-permute-start = (bf16[2,384,256]{2,1,0:T(8,128)(2,1)S(1)}, bf16[2,384,256]{2,1,0:T(8,128)(2,1)S(1)}, u32[]{:S(2)}, u32[]{:S(2)}) collective-permute-start(bf16[2,384,256]{2,1,0:T(8,128)(2,1)S(1)} %pad_maximum_fusion.refs_2_), channel_id=1, source_target_pairs={{4,48},{12,56},{20,0},{28,8},{36,16},{44,24},{52,32},{60,40},{68,1... | collective-permute-start | bytes 1179656 | tf_op jit(solution)/shard_map/ppermute | solution.py:199
  9.5 0.0 copy-start
  9.6 1.1 %copy-done = bf16[384,1024]{1,0:T(8,128)(2,1)S(1)} copy-done((bf16[384,1024]{1,0:T(8,128)(2,1)S(1)}, bf16[384,1024]{1,0:T(8,128)(2,1)}, u32[]{:S(2)}) %copy-start) | copy-done | bytes 786456
  10.7 0.0 copy-start.1
  10.7 0.7 %copy-done.1 = s32[32]{0:T(128)S(1)} copy-done((s32[32]{0:T(128)S(1)}, s32[32]{0:T(128)}, u32[]{:S(2)}) %copy-start.1) | copy-done | bytes 152
  11.3 2.5 %shard_map.46.refs_4_ = f32[12,136,256]{2,1,0:T(8,128)S(1)} custom-call(s32[32]{0:T(128)S(1)} %copy-done.1, bf16[384,1024]{1,0:T(8,128)(2,1)S(1)} %copy-done, bf16[2,384,256]{2,1,0:T(8,128)(2,1)S(1)} %pad_maximum_fusion.refs_2_), custom_call_target="tpu_custom_call" | custom-call | flops 603979776 | bytes 1048576 | tf_op jit(solution)/shard_map/pallas_call | solution.py:178
  13.8 2.9 %collective-permute-done.1.refs_3_ = bf16[2,384,256]{2,1,0:T(8,128)(2,1)S(1)} collective-permute-done((bf16[2,384,256]{2,1,0:T(8,128)(2,1)S(1)}, bf16[2,384,256]{2,1,0:T(8,128)(2,1)S(1)}, u32[]{:S(2)}, u32[]{:S(2)}) %collective-permute-start.1) | collective-permute-done | bytes 393248 | tf_op jit(solution)/shard_map/ppermute | solution.py:199
  16.7 2.3 %collective-permute-start.2 = (bf16[2,384,256]{2,1,0:T(8,128)(2,1)S(1)}, bf16[2,384,256]{2,1,0:T(8,128)(2,1)S(1)}, u32[]{:S(2)}, u32[]{:S(2)}) collective-permute-start(bf16[2,384,256]{2,1,0:T(8,128)(2,1)S(1)} %collective-permute-done.1.refs_3_), channel_id=1, source_target_pairs={{0,4},{4,0},{8,12},{12,8},{16,20},{20,16},{24,28},{28,24},{32,36},... | collective-permute-start | bytes 1179656 | tf_op jit(solution)/shard_map/ppermute | solution.py:199
  19.0 1.9 %collective-permute-start.3 = (bf16[2,384,256]{2,1,0:T(8,128)(2,1)S(1)}, bf16[2,384,256]{2,1,0:T(8,128)(2,1)S(1)}, u32[]{:S(2)}, u32[]{:S(2)}) collective-permute-start(bf16[2,384,256]{2,1,0:T(8,128)(2,1)S(1)} %collective-permute-done.1.refs_3_), channel_id=1, source_target_pairs={{0,8},{4,12},{8,16},{12,20},{16,24},{20,28},{24,32},{28,36},{32,40... | collective-permute-start | bytes 1179656 | tf_op jit(solution)/shard_map/ppermute | solution.py:199
  21.0 0.0 collective-permute-done.refs_2_
  21.0 4.9 %shard_map.47.refs_3_ = f32[12,136,256]{2,1,0:T(8,128)S(1)} custom-call(s32[32]{0:T(128)S(1)} %copy-done.1, bf16[384,1024]{1,0:T(8,128)(2,1)S(1)} %copy-done, bf16[2,384,256]{2,1,0:T(8,128)(2,1)S(1)} %collective-permute-done.refs_2_, bf16[2,384,256]{2,1,0:T(8,128)(2,1)S(1)} %collective-permute-done.1.refs_3_, ...), custom_call_target="tpu_custom_call", output_to_operand_aliasing={{}: (4, {})} | custom-call | flops 1207959552 | bytes 1048576 | tf_op jit(solution)/shard_map/pallas_call | solution.py:178
  25.9 0.0 collective-permute-done.2.refs_2_
  25.9 2.7 %shard_map.48.refs_3_ = f32[12,136,256]{2,1,0:T(8,128)S(1)} custom-call(s32[32]{0:T(128)S(1)} %copy-done.1, bf16[384,1024]{1,0:T(8,128)(2,1)S(1)} %copy-done, bf16[2,384,256]{2,1,0:T(8,128)(2,1)S(1)} %collective-permute-done.2.refs_2_, f32[12,136,256]{2,1,0:T(8,128)S(1)} %shard_map.47.refs_3_), custom_call_target="tpu_custom_call", output_to_operand_aliasing={{}: (3, {})} | custom-call | flops 603979776 | bytes 1048576 | tf_op jit(solution)/shard_map/pallas_call | solution.py:178
  28.6 5.0 %collective-permute-done.3.refs_2_ = bf16[2,384,256]{2,1,0:T(8,128)(2,1)S(1)} collective-permute-done((bf16[2,384,256]{2,1,0:T(8,128)(2,1)S(1)}, bf16[2,384,256]{2,1,0:T(8,128)(2,1)S(1)}, u32[]{:S(2)}, u32[]{:S(2)}) %collective-permute-start.3) | collective-permute-done | bytes 393248 | tf_op jit(solution)/shard_map/ppermute | solution.py:199
  33.6 2.9 %collective-permute-start.4 = (bf16[2,384,256]{2,1,0:T(8,128)(2,1)S(1)}, bf16[2,384,256]{2,1,0:T(8,128)(2,1)S(1)}, u32[]{:S(2)}, u32[]{:S(2)}) collective-permute-start(bf16[2,384,256]{2,1,0:T(8,128)(2,1)S(1)} %collective-permute-done.3.refs_2_), channel_id=1, source_target_pairs={{0,4},{4,0},{8,12},{12,8},{16,20},{20,16},{24,28},{28,24},{32,36},... | collective-permute-start | bytes 1179656 | tf_op jit(solution)/shard_map/ppermute | solution.py:199
  36.5 0.7 %collective-permute-start.5 = (bf16[2,384,256]{2,1,0:T(8,128)(2,1)S(1)}, bf16[2,384,256]{2,1,0:T(8,128)(2,1)S(1)}, u32[]{:S(2)}, u32[]{:S(2)}) collective-permute-start(bf16[2,384,256]{2,1,0:T(8,128)(2,1)S(1)} %collective-permute-done.refs_2_), channel_id=1, source_target_pairs={{48,32},{56,40},{0,48},{8,56},{16,64},{24,72},{32,80},{40,88},{112... | collective-permute-start | bytes 1179656 | tf_op jit(solution)/shard_map/ppermute | solution.py:199
  37.2 1.9 %collective-permute-start.6 = (bf16[2,384,256]{2,1,0:T(8,128)(2,1)S(1)}, bf16[2,384,256]{2,1,0:T(8,128)(2,1)S(1)}, u32[]{:S(2)}, u32[]{:S(2)}) collective-permute-start(bf16[2,384,256]{2,1,0:T(8,128)(2,1)S(1)} %collective-permute-done.3.refs_2_), channel_id=1, source_target_pairs={{0,8},{4,12},{8,16},{12,20},{16,24},{20,28},{24,32},{28,36},{32,40... | collective-permute-start | bytes 1179656 | tf_op jit(solution)/shard_map/ppermute | solution.py:199
  39.1 2.7 %shard_map.49.refs_4_ = f32[12,136,256]{2,1,0:T(8,128)S(1)} custom-call(s32[32]{0:T(128)S(1)} %copy-done.1, bf16[384,1024]{1,0:T(8,128)(2,1)S(1)} %copy-done, bf16[2,384,256]{2,1,0:T(8,128)(2,1)S(1)} %collective-permute-done.3.refs_2_, f32[12,136,256]{2,1,0:T(8,128)S(1)} %shard_map.48.refs_3_), custom_call_target="tpu_custom_call", output_to_operand_aliasing={{}: (3, {})} | custom-call | flops 603979776 | bytes 1048576 | tf_op jit(solution)/shard_map/pallas_call | solution.py:178
  41.8 0.0 collective-permute-done.4.refs_2_
  41.8 0.0 collective-permute-done.5.refs_3_
  41.8 2.9 %shard_map.50.refs_3_ = f32[12,136,256]{2,1,0:T(8,128)S(1)} custom-call(s32[32]{0:T(128)S(1)} %copy-done.1, bf16[384,1024]{1,0:T(8,128)(2,1)S(1)} %copy-done, bf16[2,384,256]{2,1,0:T(8,128)(2,1)S(1)} %collective-permute-done.4.refs_2_, bf16[2,384,256]{2,1,0:T(8,128)(2,1)S(1)} %collective-permute-done.5.refs_3_, ...), custom_call_target="tpu_custom_call", output_to_operand_aliasing={{}: (4, {})} | custom-call | flops 1207959552 | bytes 1048576 | tf_op jit(solution)/shard_map/pallas_call | solution.py:178
  44.8 9.6 %collective-permute-done.6.refs_2_ = bf16[2,384,256]{2,1,0:T(8,128)(2,1)S(1)} collective-permute-done((bf16[2,384,256]{2,1,0:T(8,128)(2,1)S(1)}, bf16[2,384,256]{2,1,0:T(8,128)(2,1)S(1)}, u32[]{:S(2)}, u32[]{:S(2)}) %collective-permute-start.6) | collective-permute-done | bytes 393248 | tf_op jit(solution)/shard_map/ppermute | solution.py:199
  54.4 4.3 %collective-permute-start.7 = (bf16[2,384,256]{2,1,0:T(8,128)(2,1)S(1)}, bf16[2,384,256]{2,1,0:T(8,128)(2,1)S(1)}, u32[]{:S(2)}, u32[]{:S(2)}) collective-permute-start(bf16[2,384,256]{2,1,0:T(8,128)(2,1)S(1)} %collective-permute-done.6.refs_2_), channel_id=1, source_target_pairs={{0,4},{4,0},{8,12},{12,8},{16,20},{20,16},{24,28},{28,24},{32,36},... | collective-permute-start | bytes 1179656 | tf_op jit(solution)/shard_map/ppermute | solution.py:199
  58.7 2.7 %shard_map.51.refs_3_ = f32[12,136,256]{2,1,0:T(8,128)S(1)} custom-call(s32[32]{0:T(128)S(1)} %copy-done.1, bf16[384,1024]{1,0:T(8,128)(2,1)S(1)} %copy-done, bf16[2,384,256]{2,1,0:T(8,128)(2,1)S(1)} %collective-permute-done.6.refs_2_, f32[12,136,256]{2,1,0:T(8,128)S(1)} %shard_map.50.refs_3_), custom_call_target="tpu_custom_call", output_to_operand_aliasing={{}: (3, {})} | custom-call | flops 603979776 | bytes 1048576 | tf_op jit(solution)/shard_map/pallas_call | solution.py:178
  61.4 0.0 collective-permute-done.7.refs_2_
  61.4 3.9 %shard_map.52 = bf16[384,1024]{1,0:T(8,128)(2,1)} custom-call(s32[32]{0:T(128)S(1)} %copy-done.1, bf16[384,1024]{1,0:T(8,128)(2,1)S(1)} %copy-done, bf16[2,384,256]{2,1,0:T(8,128)(2,1)S(1)} %collective-permute-done.7.refs_2_, f32[12,136,256]{2,1,0:T(8,128)S(1)} %shard_map.51.refs_3_), custom_call_target="tpu_custom_call" | custom-call | flops 603979776 | bytes 1048576 | tf_op jit(solution)/shard_map/pallas_call | solution.py:178
Async XLA Ops:
  1.1 15.7 %collective-permute-start.1 = (bf16[2,384,256]{2,1,0:T(8,128)(2,1)S(1)}, bf16[2,384,256]{2,1,0:T(8,128)(2,1)S(1)}, u32[]{:S(2)}, u32[]{:S(2)}) collective-permute-start(bf16[2,384,256]{2,1,0:T(8,128)(2,1)S(1)} %pad_maximum_fusion.refs_2_), channel_id=1, source_target_pairs={{0,12},{4,8},{8,20},{12,16},{16,28},{20,24},{24,36},{28,32},{32,44... | collective-permute-start | bytes 1179656 | tf_op jit(solution)/shard_map/ppermute | solution.py:199
  4.8 16.1 %collective-permute-start = (bf16[2,384,256]{2,1,0:T(8,128)(2,1)S(1)}, bf16[2,384,256]{2,1,0:T(8,128)(2,1)S(1)}, u32[]{:S(2)}, u32[]{:S(2)}) collective-permute-start(bf16[2,384,256]{2,1,0:T(8,128)(2,1)S(1)} %pad_maximum_fusion.refs_2_), channel_id=1, source_target_pairs={{4,48},{12,56},{20,0},{28,8},{36,16},{44,24},{52,32},{60,40},{68,1... | collective-permute-start | bytes 1179656 | tf_op jit(solution)/shard_map/ppermute | solution.py:199
  9.5 1.1 %copy-start = (bf16[384,1024]{1,0:T(8,128)(2,1)S(1)}, bf16[384,1024]{1,0:T(8,128)(2,1)}, u32[]{:S(2)}) copy-start(bf16[384,1024]{1,0:T(8,128)(2,1)} %refs_1_.13) | copy-start | bytes 2359300
  10.7 0.7 %copy-start.1 = (s32[32]{0:T(128)S(1)}, s32[32]{0:T(128)}, u32[]{:S(2)}) copy-start(s32[32]{0:T(128)} %refs_0_.13) | copy-start | bytes 388
  16.7 9.1 %collective-permute-start.2 = (bf16[2,384,256]{2,1,0:T(8,128)(2,1)S(1)}, bf16[2,384,256]{2,1,0:T(8,128)(2,1)S(1)}, u32[]{:S(2)}, u32[]{:S(2)}) collective-permute-start(bf16[2,384,256]{2,1,0:T(8,128)(2,1)S(1)} %collective-permute-done.1.refs_3_), channel_id=1, source_target_pairs={{0,4},{4,0},{8,12},{12,8},{16,20},{20,16},{24,28},{28,24},{32,36},... | collective-permute-start | bytes 1179656 | tf_op jit(solution)/shard_map/ppermute | solution.py:199
  19.0 14.6 %collective-permute-start.3 = (bf16[2,384,256]{2,1,0:T(8,128)(2,1)S(1)}, bf16[2,384,256]{2,1,0:T(8,128)(2,1)S(1)}, u32[]{:S(2)}, u32[]{:S(2)}) collective-permute-start(bf16[2,384,256]{2,1,0:T(8,128)(2,1)S(1)} %collective-permute-done.1.refs_3_), channel_id=1, source_target_pairs={{0,8},{4,12},{8,16},{12,20},{16,24},{20,28},{24,32},{28,36},{32,40... | collective-permute-start | bytes 1179656 | tf_op jit(solution)/shard_map/ppermute | solution.py:199
  33.6 8.2 %collective-permute-start.4 = (bf16[2,384,256]{2,1,0:T(8,128)(2,1)S(1)}, bf16[2,384,256]{2,1,0:T(8,128)(2,1)S(1)}, u32[]{:S(2)}, u32[]{:S(2)}) collective-permute-start(bf16[2,384,256]{2,1,0:T(8,128)(2,1)S(1)} %collective-permute-done.3.refs_2_), channel_id=1, source_target_pairs={{0,4},{4,0},{8,12},{12,8},{16,20},{20,16},{24,28},{28,24},{32,36},... | collective-permute-start | bytes 1179656 | tf_op jit(solution)/shard_map/ppermute | solution.py:199
  36.5 5.3 %collective-permute-start.5 = (bf16[2,384,256]{2,1,0:T(8,128)(2,1)S(1)}, bf16[2,384,256]{2,1,0:T(8,128)(2,1)S(1)}, u32[]{:S(2)}, u32[]{:S(2)}) collective-permute-start(bf16[2,384,256]{2,1,0:T(8,128)(2,1)S(1)} %collective-permute-done.refs_2_), channel_id=1, source_target_pairs={{48,32},{56,40},{0,48},{8,56},{16,64},{24,72},{32,80},{40,88},{112... | collective-permute-start | bytes 1179656 | tf_op jit(solution)/shard_map/ppermute | solution.py:199
  37.2 17.2 %collective-permute-start.6 = (bf16[2,384,256]{2,1,0:T(8,128)(2,1)S(1)}, bf16[2,384,256]{2,1,0:T(8,128)(2,1)S(1)}, u32[]{:S(2)}, u32[]{:S(2)}) collective-permute-start(bf16[2,384,256]{2,1,0:T(8,128)(2,1)S(1)} %collective-permute-done.3.refs_2_), channel_id=1, source_target_pairs={{0,8},{4,12},{8,16},{12,20},{16,24},{20,28},{24,32},{28,36},{32,40... | collective-permute-start | bytes 1179656 | tf_op jit(solution)/shard_map/ppermute | solution.py:199
  54.4 7.0 %collective-permute-start.7 = (bf16[2,384,256]{2,1,0:T(8,128)(2,1)S(1)}, bf16[2,384,256]{2,1,0:T(8,128)(2,1)S(1)}, u32[]{:S(2)}, u32[]{:S(2)}) collective-permute-start(bf16[2,384,256]{2,1,0:T(8,128)(2,1)S(1)} %collective-permute-done.6.refs_2_), channel_id=1, source_target_pairs={{0,4},{4,0},{8,12},{12,8},{16,20},{20,16},{24,28},{28,24},{32,36},... | collective-permute-start | bytes 1179656 | tf_op jit(solution)/shard_map/ppermute | solution.py:199

commit v6 on v5

--- a/solution.py
+++ b/solution.py
@@ -25,7 +25,6 @@
     back = lambda n: n - n % RING + (n % RING - RING // 4) % RING
     inside = [n for n in range(chips) if n + 4 < chips]
     return {
-        "cross": [(dev(n, c), dev(n + 1, 1 - c)) for n in range(chips - 1) for c in (0, 1)],
         "ahead": [(dev(n, c), dev(n + 1, c)) for n in range(chips - 1) for c in (0, 1)],
         "swap": [(dev(n, c), dev(n, 1 - c)) for n in range(chips) for c in (0, 1)],
         "back1": [(dev(n, 1), dev(back(n), 0)) for n in inside] + [(dev(n, 0), dev(n, 1)) for n in range(chips)],
@@ -201,28 +200,28 @@
     after = lax.optimization_barrier
     own = jnp.stack([keys, values])
     step = functools.partial(attend, lengths, queries)
-    got1 = move(own, "cross")
+    got1 = move(own, "ahead")
     mix1 = move(own, "back1")
     state = step([own], [(0, 0)], None, False)
     state, got1 = after((state, got1))
     got2 = move(got1, "ahead")
     mate1 = move(got1, "swap")
     far2 = move(mix1, "back2")
-    state = step([mix1, got1], [(NONE, 1), (1, 3)], state, False)
+    state = step([mix1, got1], [(NONE, 1), (2, 2)], state, False)
     state, mate1 = after((state, mate1))
-    state = step([mate1], [(2, 2)], state, False)
+    state = step([mate1], [(1, 3)], state, False)
     state, got2 = after((state, got2))
     got3 = move(got2, "ahead")
     mate2 = move(got2, "swap")
-    state = step([got2], [(3, 5)], state, False)
+    state = step([got2], [(4, 4)], state, False)
     state, mate2 = after((state, mate2))
     state, far2 = after((state, far2))
-    state = step([mate2, far2], [(4, 4), (7, NONE)], state, False)
+    state = step([mate2, far2], [(3, 5), (7, NONE)], state, False)
     state, got3 = after((state, got3))
     mate3 = move(got3, "swap")
-    state = step([got3], [(5, 7)], state, False)
+    state = step([got3], [(6, 6)], state, False)
     state, mate3 = after((state, mate3))
-    return step([mate3], [(6, 6)], state, True)
+    return step([mate3], [(5, 7)], state, True)
 
 
 def solution(mesh):

time: 65.6 us -> 65.1 us (level)
  the two profiles are of different devices: /device:TPU:451 before, /device:TPU:453 now
where the time goes in v6:
time: 65.1 us; the launch traced here: 64.7 us
  starting transfers between devices  24.1 us (37%)
  Pallas kernels  22.2 us (34%)
  waiting for transfers between devices  15.4 us (24%)
  local copies, waits for them, and re-layouts  1.78 us (3%)
  other arithmetic  1.06 us (2%)
    ppermute x8, starting transfers between devices, move(): return lax.ppermute(x, 'cp', ways[way])  24.1 us
    pallas_call x7, Pallas kernels, attend(): pl.pallas_call(functools.partial(attend_kernel, blocks, first, final, tok...  22.2 us
    ppermute x8, waiting for transfers between devices, move(): return lax.ppermute(x, 'cp', ways[way])  15.4 us
    unnamed x4, local copies, waits for them, and re-layouts  1.78 us
  transfers between devices with their start and end apart: 8, of which 3 were waited for; matrix products, arithmetic and copies ran while one was open for 0% of the time, Pallas kernels for 28%

profile of v6, /device:TPU:453, one launch (start us, length us, event | category | flops | bytes accessed | tf_op | source)
XLA Modules:
  0.0 64.7 jit_solution(16541441161187836516)
XLA Ops:
  0.0 1.1 %pad_maximum_fusion.refs_2_ = bf16[2,384,256]{2,1,0:T(8,128)(2,1)S(1)} fusion(bf16[1,384,256]{2,1,0:T(8,128)(2,1)} %bitcast.2, bf16[1,384,256]{2,1,0:T(8,128)(2,1)} %bitcast.3), kind=kLoop, calls=%fused_computation | loop fusion | flops 196608 | bytes 786432 | tf_op jit(solution)/shard_map/stack | solution.py:201
  1.1 3.2 %collective-permute-start.1 = (bf16[2,384,256]{2,1,0:T(8,128)(2,1)S(1)}, bf16[2,384,256]{2,1,0:T(8,128)(2,1)S(1)}, u32[]{:S(2)}, u32[]{:S(2)}) collective-permute-start(bf16[2,384,256]{2,1,0:T(8,128)(2,1)S(1)} %pad_maximum_fusion.refs_2_), channel_id=1, source_target_pairs={{0,8},{4,12},{8,16},{12,20},{16,24},{20,28},{24,32},{28,36},{32,40... | collective-permute-start | bytes 1179656 | tf_op jit(solution)/shard_map/ppermute | solution.py:198
  4.3 5.8 %collective-permute-start = (bf16[2,384,256]{2,1,0:T(8,128)(2,1)S(1)}, bf16[2,384,256]{2,1,0:T(8,128)(2,1)S(1)}, u32[]{:S(2)}, u32[]{:S(2)}) collective-permute-start(bf16[2,384,256]{2,1,0:T(8,128)(2,1)S(1)} %pad_maximum_fusion.refs_2_), channel_id=1, source_target_pairs={{4,48},{12,56},{20,0},{28,8},{36,16},{44,24},{52,32},{60,40},{68,1... | collective-permute-start | bytes 1179656 | tf_op jit(solution)/shard_map/ppermute | solution.py:198
  10.1 0.0 copy-start
  10.1 1.1 %copy-done = bf16[384,1024]{1,0:T(8,128)(2,1)S(1)} copy-done((bf16[384,1024]{1,0:T(8,128)(2,1)S(1)}, bf16[384,1024]{1,0:T(8,128)(2,1)}, u32[]{:S(2)}) %copy-start) | copy-done | bytes 786456
  11.2 0.0 copy-start.1
  11.2 0.7 %copy-done.1 = s32[32]{0:T(128)S(1)} copy-done((s32[32]{0:T(128)S(1)}, s32[32]{0:T(128)}, u32[]{:S(2)}) %copy-start.1) | copy-done | bytes 152
  11.9 2.5 %shard_map.46.refs_4_ = f32[12,136,256]{2,1,0:T(8,128)S(1)} custom-call(s32[32]{0:T(128)S(1)} %copy-done.1, bf16[384,1024]{1,0:T(8,128)(2,1)S(1)} %copy-done, bf16[2,384,256]{2,1,0:T(8,128)(2,1)S(1)} %pad_maximum_fusion.refs_2_), custom_call_target="tpu_custom_call" | custom-call | flops 603979776 | bytes 1048576 | tf_op jit(solution)/shard_map/pallas_call | solution.py:177
  14.4 0.7 %collective-permute-done.1.refs_3_ = bf16[2,384,256]{2,1,0:T(8,128)(2,1)S(1)} collective-permute-done((bf16[2,384,256]{2,1,0:T(8,128)(2,1)S(1)}, bf16[2,384,256]{2,1,0:T(8,128)(2,1)S(1)}, u32[]{:S(2)}, u32[]{:S(2)}) %collective-permute-start.1) | collective-permute-done | bytes 393248 | tf_op jit(solution)/shard_map/ppermute | solution.py:198
  15.1 3.4 %collective-permute-start.2 = (bf16[2,384,256]{2,1,0:T(8,128)(2,1)S(1)}, bf16[2,384,256]{2,1,0:T(8,128)(2,1)S(1)}, u32[]{:S(2)}, u32[]{:S(2)}) collective-permute-start(bf16[2,384,256]{2,1,0:T(8,128)(2,1)S(1)} %collective-permute-done.1.refs_3_), channel_id=1, source_target_pairs={{0,4},{4,0},{8,12},{12,8},{16,20},{20,16},{24,28},{28,24},{32,36},... | collective-permute-start | bytes 1179656 | tf_op jit(solution)/shard_map/ppermute | solution.py:198
  18.5 1.9 %collective-permute-start.3 = (bf16[2,384,256]{2,1,0:T(8,128)(2,1)S(1)}, bf16[2,384,256]{2,1,0:T(8,128)(2,1)S(1)}, u32[]{:S(2)}, u32[]{:S(2)}) collective-permute-start(bf16[2,384,256]{2,1,0:T(8,128)(2,1)S(1)} %collective-permute-done.1.refs_3_), channel_id=1, source_target_pairs={{0,8},{4,12},{8,16},{12,20},{16,24},{20,28},{24,32},{28,36},{32,40... | collective-permute-start | bytes 1179656 | tf_op jit(solution)/shard_map/ppermute | solution.py:198
  20.4 0.0 collective-permute-done.refs_2_
  20.4 4.9 %shard_map.47.refs_3_ = f32[12,136,256]{2,1,0:T(8,128)S(1)} custom-call(s32[32]{0:T(128)S(1)} %copy-done.1, bf16[384,1024]{1,0:T(8,128)(2,1)S(1)} %copy-done, bf16[2,384,256]{2,1,0:T(8,128)(2,1)S(1)} %collective-permute-done.refs_2_, bf16[2,384,256]{2,1,0:T(8,128)(2,1)S(1)} %collective-permute-done.1.refs_3_, ...), custom_call_target="tpu_custom_call", output_to_operand_aliasing={{}: (4, {})} | custom-call | flops 1207959552 | bytes 1048576 | tf_op jit(solution)/shard_map/pallas_call | solution.py:177
  25.3 0.0 collective-permute-done.2.refs_2_
  25.4 2.7 %shard_map.48.refs_3_ = f32[12,136,256]{2,1,0:T(8,128)S(1)} custom-call(s32[32]{0:T(128)S(1)} %copy-done.1, bf16[384,1024]{1,0:T(8,128)(2,1)S(1)} %copy-done, bf16[2,384,256]{2,1,0:T(8,128)(2,1)S(1)} %collective-permute-done.2.refs_2_, f32[12,136,256]{2,1,0:T(8,128)S(1)} %shard_map.47.refs_3_), custom_call_target="tpu_custom_call", output_to_operand_aliasing={{}: (3, {})} | custom-call | flops 603979776 | bytes 1048576 | tf_op jit(solution)/shard_map/pallas_call | solution.py:177
  28.0 5.1 %collective-permute-done.3.refs_2_ = bf16[2,384,256]{2,1,0:T(8,128)(2,1)S(1)} collective-permute-done((bf16[2,384,256]{2,1,0:T(8,128)(2,1)S(1)}, bf16[2,384,256]{2,1,0:T(8,128)(2,1)S(1)}, u32[]{:S(2)}, u32[]{:S(2)}) %collective-permute-start.3) | collective-permute-done | bytes 393248 | tf_op jit(solution)/shard_map/ppermute | solution.py:198
  33.2 2.8 %collective-permute-start.4 = (bf16[2,384,256]{2,1,0:T(8,128)(2,1)S(1)}, bf16[2,384,256]{2,1,0:T(8,128)(2,1)S(1)}, u32[]{:S(2)}, u32[]{:S(2)}) collective-permute-start(bf16[2,384,256]{2,1,0:T(8,128)(2,1)S(1)} %collective-permute-done.3.refs_2_), channel_id=1, source_target_pairs={{0,4},{4,0},{8,12},{12,8},{16,20},{20,16},{24,28},{28,24},{32,36},... | collective-permute-start | bytes 1179656 | tf_op jit(solution)/shard_map/ppermute | solution.py:198
  35.9 0.7 %collective-permute-start.5 = (bf16[2,384,256]{2,1,0:T(8,128)(2,1)S(1)}, bf16[2,384,256]{2,1,0:T(8,128)(2,1)S(1)}, u32[]{:S(2)}, u32[]{:S(2)}) collective-permute-start(bf16[2,384,256]{2,1,0:T(8,128)(2,1)S(1)} %collective-permute-done.refs_2_), channel_id=1, source_target_pairs={{48,32},{56,40},{0,48},{8,56},{16,64},{24,72},{32,80},{40,88},{112... | collective-permute-start | bytes 1179656 | tf_op jit(solution)/shard_map/ppermute | solution.py:198
  36.6 1.9 %collective-permute-start.6 = (bf16[2,384,256]{2,1,0:T(8,128)(2,1)S(1)}, bf16[2,384,256]{2,1,0:T(8,128)(2,1)S(1)}, u32[]{:S(2)}, u32[]{:S(2)}) collective-permute-start(bf16[2,384,256]{2,1,0:T(8,128)(2,1)S(1)} %collective-permute-done.3.refs_2_), channel_id=1, source_target_pairs={{0,8},{4,12},{8,16},{12,20},{16,24},{20,28},{24,32},{28,36},{32,40... | collective-permute-start | bytes 1179656 | tf_op jit(solution)/shard_map/ppermute | solution.py:198
  38.6 2.7 %shard_map.49.refs_4_ = f32[12,136,256]{2,1,0:T(8,128)S(1)} custom-call(s32[32]{0:T(128)S(1)} %copy-done.1, bf16[384,1024]{1,0:T(8,128)(2,1)S(1)} %copy-done, bf16[2,384,256]{2,1,0:T(8,128)(2,1)S(1)} %collective-permute-done.3.refs_2_, f32[12,136,256]{2,1,0:T(8,128)S(1)} %shard_map.48.refs_3_), custom_call_target="tpu_custom_call", output_to_operand_aliasing={{}: (3, {})} | custom-call | flops 603979776 | bytes 1048576 | tf_op jit(solution)/shard_map/pallas_call | solution.py:177
  41.2 0.0 collective-permute-done.4.refs_2_
  41.2 0.0 collective-permute-done.5.refs_3_
  41.3 2.9 %shard_map.50.refs_3_ = f32[12,136,256]{2,1,0:T(8,128)S(1)} custom-call(s32[32]{0:T(128)S(1)} %copy-done.1, bf16[384,1024]{1,0:T(8,128)(2,1)S(1)} %copy-done, bf16[2,384,256]{2,1,0:T(8,128)(2,1)S(1)} %collective-permute-done.4.refs_2_, bf16[2,384,256]{2,1,0:T(8,128)(2,1)S(1)} %collective-permute-done.5.refs_3_, ...), custom_call_target="tpu_custom_call", output_to_operand_aliasing={{}: (4, {})} | custom-call | flops 1207959552 | bytes 1048576 | tf_op jit(solution)/shard_map/pallas_call | solution.py:177
  44.2 9.6 %collective-permute-done.6.refs_2_ = bf16[2,384,256]{2,1,0:T(8,128)(2,1)S(1)} collective-permute-done((bf16[2,384,256]{2,1,0:T(8,128)(2,1)S(1)}, bf16[2,384,256]{2,1,0:T(8,128)(2,1)S(1)}, u32[]{:S(2)}, u32[]{:S(2)}) %collective-permute-start.6) | collective-permute-done | bytes 393248 | tf_op jit(solution)/shard_map/ppermute | solution.py:198
  53.8 4.3 %collective-permute-start.7 = (bf16[2,384,256]{2,1,0:T(8,128)(2,1)S(1)}, bf16[2,384,256]{2,1,0:T(8,128)(2,1)S(1)}, u32[]{:S(2)}, u32[]{:S(2)}) collective-permute-start(bf16[2,384,256]{2,1,0:T(8,128)(2,1)S(1)} %collective-permute-done.6.refs_2_), channel_id=1, source_target_pairs={{0,4},{4,0},{8,12},{12,8},{16,20},{20,16},{24,28},{28,24},{32,36},... | collective-permute-start | bytes 1179656 | tf_op jit(solution)/shard_map/ppermute | solution.py:198
  58.2 2.7 %shard_map.51.refs_3_ = f32[12,136,256]{2,1,0:T(8,128)S(1)} custom-call(s32[32]{0:T(128)S(1)} %copy-done.1, bf16[384,1024]{1,0:T(8,128)(2,1)S(1)} %copy-done, bf16[2,384,256]{2,1,0:T(8,128)(2,1)S(1)} %collective-permute-done.6.refs_2_, f32[12,136,256]{2,1,0:T(8,128)S(1)} %shard_map.50.refs_3_), custom_call_target="tpu_custom_call", output_to_operand_aliasing={{}: (3, {})} | custom-call | flops 603979776 | bytes 1048576 | tf_op jit(solution)/shard_map/pallas_call | solution.py:177
  60.8 0.0 collective-permute-done.7.refs_2_
  60.8 3.9 %shard_map.52 = bf16[384,1024]{1,0:T(8,128)(2,1)} custom-call(s32[32]{0:T(128)S(1)} %copy-done.1, bf16[384,1024]{1,0:T(8,128)(2,1)S(1)} %copy-done, bf16[2,384,256]{2,1,0:T(8,128)(2,1)S(1)} %collective-permute-done.7.refs_2_, f32[12,136,256]{2,1,0:T(8,128)S(1)} %shard_map.51.refs_3_), custom_call_target="tpu_custom_call" | custom-call | flops 603979776 | bytes 1048576 | tf_op jit(solution)/shard_map/pallas_call | solution.py:177
Async XLA Ops:
  1.1 14.0 %collective-permute-start.1 = (bf16[2,384,256]{2,1,0:T(8,128)(2,1)S(1)}, bf16[2,384,256]{2,1,0:T(8,128)(2,1)S(1)}, u32[]{:S(2)}, u32[]{:S(2)}) collective-permute-start(bf16[2,384,256]{2,1,0:T(8,128)(2,1)S(1)} %pad_maximum_fusion.refs_2_), channel_id=1, source_target_pairs={{0,8},{4,12},{8,16},{12,20},{16,24},{20,28},{24,32},{28,36},{32,40... | collective-permute-start | bytes 1179656 | tf_op jit(solution)/shard_map/ppermute | solution.py:198
  4.3 16.2 %collective-permute-start = (bf16[2,384,256]{2,1,0:T(8,128)(2,1)S(1)}, bf16[2,384,256]{2,1,0:T(8,128)(2,1)S(1)}, u32[]{:S(2)}, u32[]{:S(2)}) collective-permute-start(bf16[2,384,256]{2,1,0:T(8,128)(2,1)S(1)} %pad_maximum_fusion.refs_2_), channel_id=1, source_target_pairs={{4,48},{12,56},{20,0},{28,8},{36,16},{44,24},{52,32},{60,40},{68,1... | collective-permute-start | bytes 1179656 | tf_op jit(solution)/shard_map/ppermute | solution.py:198
  10.1 1.1 %copy-start = (bf16[384,1024]{1,0:T(8,128)(2,1)S(1)}, bf16[384,1024]{1,0:T(8,128)(2,1)}, u32[]{:S(2)}) copy-start(bf16[384,1024]{1,0:T(8,128)(2,1)} %refs_1_.13) | copy-start | bytes 2359300
  11.2 0.7 %copy-start.1 = (s32[32]{0:T(128)S(1)}, s32[32]{0:T(128)}, u32[]{:S(2)}) copy-start(s32[32]{0:T(128)} %refs_0_.13) | copy-start | bytes 388
  15.1 10.3 %collective-permute-start.2 = (bf16[2,384,256]{2,1,0:T(8,128)(2,1)S(1)}, bf16[2,384,256]{2,1,0:T(8,128)(2,1)S(1)}, u32[]{:S(2)}, u32[]{:S(2)}) collective-permute-start(bf16[2,384,256]{2,1,0:T(8,128)(2,1)S(1)} %collective-permute-done.1.refs_3_), channel_id=1, source_target_pairs={{0,4},{4,0},{8,12},{12,8},{16,20},{20,16},{24,28},{28,24},{32,36},... | collective-permute-start | bytes 1179656 | tf_op jit(solution)/shard_map/ppermute | solution.py:198
  18.5 14.7 %collective-permute-start.3 = (bf16[2,384,256]{2,1,0:T(8,128)(2,1)S(1)}, bf16[2,384,256]{2,1,0:T(8,128)(2,1)S(1)}, u32[]{:S(2)}, u32[]{:S(2)}) collective-permute-start(bf16[2,384,256]{2,1,0:T(8,128)(2,1)S(1)} %collective-permute-done.1.refs_3_), channel_id=1, source_target_pairs={{0,8},{4,12},{8,16},{12,20},{16,24},{20,28},{24,32},{28,36},{32,40... | collective-permute-start | bytes 1179656 | tf_op jit(solution)/shard_map/ppermute | solution.py:198
  33.2 8.1 %collective-permute-start.4 = (bf16[2,384,256]{2,1,0:T(8,128)(2,1)S(1)}, bf16[2,384,256]{2,1,0:T(8,128)(2,1)S(1)}, u32[]{:S(2)}, u32[]{:S(2)}) collective-permute-start(bf16[2,384,256]{2,1,0:T(8,128)(2,1)S(1)} %collective-permute-done.3.refs_2_), channel_id=1, source_target_pairs={{0,4},{4,0},{8,12},{12,8},{16,20},{20,16},{24,28},{28,24},{32,36},... | collective-permute-start | bytes 1179656 | tf_op jit(solution)/shard_map/ppermute | solution.py:198
  35.9 5.3 %collective-permute-start.5 = (bf16[2,384,256]{2,1,0:T(8,128)(2,1)S(1)}, bf16[2,384,256]{2,1,0:T(8,128)(2,1)S(1)}, u32[]{:S(2)}, u32[]{:S(2)}) collective-permute-start(bf16[2,384,256]{2,1,0:T(8,128)(2,1)S(1)} %collective-permute-done.refs_2_), channel_id=1, source_target_pairs={{48,32},{56,40},{0,48},{8,56},{16,64},{24,72},{32,80},{40,88},{112... | collective-permute-start | bytes 1179656 | tf_op jit(solution)/shard_map/ppermute | solution.py:198
  36.6 17.2 %collective-permute-start.6 = (bf16[2,384,256]{2,1,0:T(8,128)(2,1)S(1)}, bf16[2,384,256]{2,1,0:T(8,128)(2,1)S(1)}, u32[]{:S(2)}, u32[]{:S(2)}) collective-permute-start(bf16[2,384,256]{2,1,0:T(8,128)(2,1)S(1)} %collective-permute-done.3.refs_2_), channel_id=1, source_target_pairs={{0,8},{4,12},{8,16},{12,20},{16,24},{20,28},{24,32},{28,36},{32,40... | collective-permute-start | bytes 1179656 | tf_op jit(solution)/shard_map/ppermute | solution.py:198
  53.8 7.0 %collective-permute-start.7 = (bf16[2,384,256]{2,1,0:T(8,128)(2,1)S(1)}, bf16[2,384,256]{2,1,0:T(8,128)(2,1)S(1)}, u32[]{:S(2)}, u32[]{:S(2)}) collective-permute-start(bf16[2,384,256]{2,1,0:T(8,128)(2,1)S(1)} %collective-permute-done.6.refs_2_), channel_id=1, source_target_pairs={{0,4},{4,0},{8,12},{12,8},{16,20},{20,16},{24,28},{28,24},{32,36},... | collective-permute-start | bytes 1179656 | tf_op jit(solution)/shard_map/ppermute | solution.py:198

commit v7 on v6

--- a/solution.py
+++ b/solution.py
@@ -39,10 +39,11 @@
     while len(kv_refs) < len(blocks):
         ref = refs.pop(0)
         kv_refs += [ref] if len(ref.shape) == 3 else [ref.at[j] for j in range(ref.shape[0])]
-    state_in = None if first else refs.pop(0)
+    if not first:
+        refs.pop(0)
     out_ref = refs.pop(0)
+    state = refs.pop(0) if final else out_ref
     s_ref, p_ref, mask_ref = refs.pop(0), refs.pop(0), refs.pop(0)
-    state = refs.pop(0) if final else out_ref
     me = lax.axis_index("cp")
     anchor = me * tok
     odd = me % 2 == 1
@@ -129,8 +130,6 @@
                 if 0 <= n - 2 * BATCH < total_tiles:
                     value_stage(n - 2 * BATCH)
 
-    if not first and final:
-        state[...] = state_in[...]
     for j, (kv_ref, (even_back, odd_back)) in enumerate(zip(kv_refs, blocks)):
         if first and j == 0:
             key_row = anchor + lax.broadcasted_iota(jnp.int32, (tok, LANES), 0)
@@ -172,18 +171,18 @@
     state_shape = jax.ShapeDtypeStruct((count, HEAD_DIM + 8, TILE), jnp.float32)
     vmem = pl.BlockSpec(memory_space=pltpu.VMEM)
     args = [lengths, queries, *kvs] + ([] if first else [state])
-    aliases = {} if first or final else {len(args) - 1: 0}
+    aliases = {} if first else {len(args) - 1: int(final)}
+    attended = jax.ShapeDtypeStruct((tok, width), jnp.bfloat16)
     flops = 4 * tok * tok * width * len(blocks)
     return pl.pallas_call(
         functools.partial(attend_kernel, blocks, first, final, tok, heads, group),
-        out_shape=jax.ShapeDtypeStruct((tok, width), jnp.bfloat16) if final else state_shape,
+        out_shape=(attended, state_shape) if final else state_shape,
         in_specs=[pl.BlockSpec(memory_space=pltpu.SMEM)] + [vmem] * (len(args) - 1),
-        out_specs=vmem,
+        out_specs=(vmem, vmem) if final else vmem,
         scratch_shapes=[
             pltpu.VMEM((DEPTH, tok, TILE), jnp.float32),
             pltpu.VMEM((DEPTH, tok, TILE), jnp.bfloat16),
             pltpu.VMEM((tok, tok), jnp.float32),
-            *([pltpu.VMEM(state_shape.shape, jnp.float32)] if final else []),
         ],
         input_output_aliases=aliases,
         compiler_params=pltpu.CompilerParams(vmem_limit_bytes=16 << 20),
@@ -221,7 +220,7 @@
     mate3 = move(got3, "swap")
     state = step([got3], [(6, 6)], state, False)
     state, mate3 = after((state, mate3))
-    return step([mate3], [(5, 7)], state, True)
+    return step([mate3], [(5, 7)], state, True)[0]
 
 
 def solution(mesh):

time: 65.1 us -> 65 us (level)
  no operation moved by 1% of the time
where the time goes in v7:
time: 65 us; the launch traced here: 64.7 us
  starting transfers between devices  24.1 us (37%)
  Pallas kernels  22.2 us (34%)
  waiting for transfers between devices  15.4 us (24%)
  local copies, waits for them, and re-layouts  1.78 us (3%)
  other arithmetic  1.06 us (2%)
    ppermute x8, starting transfers between devices, move(): return lax.ppermute(x, 'cp', ways[way])  24.1 us
    pallas_call x7, Pallas kernels, attend(): pl.pallas_call(functools.partial(attend_kernel, blocks, first, final, tok...  22.2 us
    ppermute x8, waiting for transfers between devices, move(): return lax.ppermute(x, 'cp', ways[way])  15.4 us
    unnamed x4, local copies, waits for them, and re-layouts  1.78 us
  transfers between devices with their start and end apart: 8, of which 3 were waited for; matrix products, arithmetic and copies ran while one was open for 0% of the time, Pallas kernels for 28%

profile of v7, /device:TPU:453, one launch (start us, length us, event | category | flops | bytes accessed | tf_op | source)
XLA Modules:
  0.0 64.7 jit_solution(11451232173772778587)
XLA Ops:
  0.0 1.1 %pad_maximum_fusion.refs_2_ = bf16[2,384,256]{2,1,0:T(8,128)(2,1)S(1)} fusion(bf16[1,384,256]{2,1,0:T(8,128)(2,1)} %bitcast.2, bf16[1,384,256]{2,1,0:T(8,128)(2,1)} %bitcast.3), kind=kLoop, calls=%fused_computation | loop fusion | flops 196608 | bytes 786432 | tf_op jit(solution)/shard_map/stack | solution.py:200
  1.1 3.2 %collective-permute-start.1 = (bf16[2,384,256]{2,1,0:T(8,128)(2,1)S(1)}, bf16[2,384,256]{2,1,0:T(8,128)(2,1)S(1)}, u32[]{:S(2)}, u32[]{:S(2)}) collective-permute-start(bf16[2,384,256]{2,1,0:T(8,128)(2,1)S(1)} %pad_maximum_fusion.refs_2_), channel_id=1, source_target_pairs={{0,8},{4,12},{8,16},{12,20},{16,24},{20,28},{24,32},{28,36},{32,40... | collective-permute-start | bytes 1179656 | tf_op jit(solution)/shard_map/ppermute | solution.py:197
  4.3 5.8 %collective-permute-start = (bf16[2,384,256]{2,1,0:T(8,128)(2,1)S(1)}, bf16[2,384,256]{2,1,0:T(8,128)(2,1)S(1)}, u32[]{:S(2)}, u32[]{:S(2)}) collective-permute-start(bf16[2,384,256]{2,1,0:T(8,128)(2,1)S(1)} %pad_maximum_fusion.refs_2_), channel_id=1, source_target_pairs={{4,48},{12,56},{20,0},{28,8},{36,16},{44,24},{52,32},{60,40},{68,1... | collective-permute-start | bytes 1179656 | tf_op jit(solution)/shard_map/ppermute | solution.py:197
  10.1 0.0 copy-start
  10.1 1.1 %copy-done = bf16[384,1024]{1,0:T(8,128)(2,1)S(1)} copy-done((bf16[384,1024]{1,0:T(8,128)(2,1)S(1)}, bf16[384,1024]{1,0:T(8,128)(2,1)}, u32[]{:S(2)}) %copy-start) | copy-done | bytes 786456
  11.2 0.0 copy-start.1
  11.2 0.7 %copy-done.1 = s32[32]{0:T(128)S(1)} copy-done((s32[32]{0:T(128)S(1)}, s32[32]{0:T(128)}, u32[]{:S(2)}) %copy-start.1) | copy-done | bytes 152
  11.9 2.5 %shard_map.46.refs_4_ = f32[12,136,256]{2,1,0:T(8,128)S(1)} custom-call(s32[32]{0:T(128)S(1)} %copy-done.1, bf16[384,1024]{1,0:T(8,128)(2,1)S(1)} %copy-done, bf16[2,384,256]{2,1,0:T(8,128)(2,1)S(1)} %pad_maximum_fusion.refs_2_), custom_call_target="tpu_custom_call" | custom-call | flops 603979776 | bytes 1048576 | tf_op jit(solution)/shard_map/pallas_call | solution.py:177
  14.4 0.7 %collective-permute-done.1.refs_3_ = bf16[2,384,256]{2,1,0:T(8,128)(2,1)S(1)} collective-permute-done((bf16[2,384,256]{2,1,0:T(8,128)(2,1)S(1)}, bf16[2,384,256]{2,1,0:T(8,128)(2,1)S(1)}, u32[]{:S(2)}, u32[]{:S(2)}) %collective-permute-start.1) | collective-permute-done | bytes 393248 | tf_op jit(solution)/shard_map/ppermute | solution.py:197
  15.1 3.4 %collective-permute-start.2 = (bf16[2,384,256]{2,1,0:T(8,128)(2,1)S(1)}, bf16[2,384,256]{2,1,0:T(8,128)(2,1)S(1)}, u32[]{:S(2)}, u32[]{:S(2)}) collective-permute-start(bf16[2,384,256]{2,1,0:T(8,128)(2,1)S(1)} %collective-permute-done.1.refs_3_), channel_id=1, source_target_pairs={{0,4},{4,0},{8,12},{12,8},{16,20},{20,16},{24,28},{28,24},{32,36},... | collective-permute-start | bytes 1179656 | tf_op jit(solution)/shard_map/ppermute | solution.py:197
  18.5 1.9 %collective-permute-start.3 = (bf16[2,384,256]{2,1,0:T(8,128)(2,1)S(1)}, bf16[2,384,256]{2,1,0:T(8,128)(2,1)S(1)}, u32[]{:S(2)}, u32[]{:S(2)}) collective-permute-start(bf16[2,384,256]{2,1,0:T(8,128)(2,1)S(1)} %collective-permute-done.1.refs_3_), channel_id=1, source_target_pairs={{0,8},{4,12},{8,16},{12,20},{16,24},{20,28},{24,32},{28,36},{32,40... | collective-permute-start | bytes 1179656 | tf_op jit(solution)/shard_map/ppermute | solution.py:197
  20.4 0.0 collective-permute-done.refs_2_
  20.4 4.9 %shard_map.47.refs_3_ = f32[12,136,256]{2,1,0:T(8,128)S(1)} custom-call(s32[32]{0:T(128)S(1)} %copy-done.1, bf16[384,1024]{1,0:T(8,128)(2,1)S(1)} %copy-done, bf16[2,384,256]{2,1,0:T(8,128)(2,1)S(1)} %collective-permute-done.refs_2_, bf16[2,384,256]{2,1,0:T(8,128)(2,1)S(1)} %collective-permute-done.1.refs_3_, ...), custom_call_target="tpu_custom_call", output_to_operand_aliasing={{}: (4, {})} | custom-call | flops 1207959552 | bytes 1048576 | tf_op jit(solution)/shard_map/pallas_call | solution.py:177
  25.3 0.0 collective-permute-done.2.refs_2_
  25.4 2.7 %shard_map.48.refs_3_ = f32[12,136,256]{2,1,0:T(8,128)S(1)} custom-call(s32[32]{0:T(128)S(1)} %copy-done.1, bf16[384,1024]{1,0:T(8,128)(2,1)S(1)} %copy-done, bf16[2,384,256]{2,1,0:T(8,128)(2,1)S(1)} %collective-permute-done.2.refs_2_, f32[12,136,256]{2,1,0:T(8,128)S(1)} %shard_map.47.refs_3_), custom_call_target="tpu_custom_call", output_to_operand_aliasing={{}: (3, {})} | custom-call | flops 603979776 | bytes 1048576 | tf_op jit(solution)/shard_map/pallas_call | solution.py:177
  28.0 5.1 %collective-permute-done.3.refs_2_ = bf16[2,384,256]{2,1,0:T(8,128)(2,1)S(1)} collective-permute-done((bf16[2,384,256]{2,1,0:T(8,128)(2,1)S(1)}, bf16[2,384,256]{2,1,0:T(8,128)(2,1)S(1)}, u32[]{:S(2)}, u32[]{:S(2)}) %collective-permute-start.3) | collective-permute-done | bytes 393248 | tf_op jit(solution)/shard_map/ppermute | solution.py:197
  33.2 2.8 %collective-permute-start.4 = (bf16[2,384,256]{2,1,0:T(8,128)(2,1)S(1)}, bf16[2,384,256]{2,1,0:T(8,128)(2,1)S(1)}, u32[]{:S(2)}, u32[]{:S(2)}) collective-permute-start(bf16[2,384,256]{2,1,0:T(8,128)(2,1)S(1)} %collective-permute-done.3.refs_2_), channel_id=1, source_target_pairs={{0,4},{4,0},{8,12},{12,8},{16,20},{20,16},{24,28},{28,24},{32,36},... | collective-permute-start | bytes 1179656 | tf_op jit(solution)/shard_map/ppermute | solution.py:197
  35.9 0.7 %collective-permute-start.5 = (bf16[2,384,256]{2,1,0:T(8,128)(2,1)S(1)}, bf16[2,384,256]{2,1,0:T(8,128)(2,1)S(1)}, u32[]{:S(2)}, u32[]{:S(2)}) collective-permute-start(bf16[2,384,256]{2,1,0:T(8,128)(2,1)S(1)} %collective-permute-done.refs_2_), channel_id=1, source_target_pairs={{48,32},{56,40},{0,48},{8,56},{16,64},{24,72},{32,80},{40,88},{112... | collective-permute-start | bytes 1179656 | tf_op jit(solution)/shard_map/ppermute | solution.py:197
  36.6 1.9 %collective-permute-start.6 = (bf16[2,384,256]{2,1,0:T(8,128)(2,1)S(1)}, bf16[2,384,256]{2,1,0:T(8,128)(2,1)S(1)}, u32[]{:S(2)}, u32[]{:S(2)}) collective-permute-start(bf16[2,384,256]{2,1,0:T(8,128)(2,1)S(1)} %collective-permute-done.3.refs_2_), channel_id=1, source_target_pairs={{0,8},{4,12},{8,16},{12,20},{16,24},{20,28},{24,32},{28,36},{32,40... | collective-permute-start | bytes 1179656 | tf_op jit(solution)/shard_map/ppermute | solution.py:197
  38.6 2.7 %shard_map.49.refs_4_ = f32[12,136,256]{2,1,0:T(8,128)S(1)} custom-call(s32[32]{0:T(128)S(1)} %copy-done.1, bf16[384,1024]{1,0:T(8,128)(2,1)S(1)} %copy-done, bf16[2,384,256]{2,1,0:T(8,128)(2,1)S(1)} %collective-permute-done.3.refs_2_, f32[12,136,256]{2,1,0:T(8,128)S(1)} %shard_map.48.refs_3_), custom_call_target="tpu_custom_call", output_to_operand_aliasing={{}: (3, {})} | custom-call | flops 603979776 | bytes 1048576 | tf_op jit(solution)/shard_map/pallas_call | solution.py:177
  41.2 0.0 collective-permute-done.4.refs_2_
  41.2 0.0 collective-permute-done.5.refs_3_
  41.3 2.9 %shard_map.50.refs_3_ = f32[12,136,256]{2,1,0:T(8,128)S(1)} custom-call(s32[32]{0:T(128)S(1)} %copy-done.1, bf16[384,1024]{1,0:T(8,128)(2,1)S(1)} %copy-done, bf16[2,384,256]{2,1,0:T(8,128)(2,1)S(1)} %collective-permute-done.4.refs_2_, bf16[2,384,256]{2,1,0:T(8,128)(2,1)S(1)} %collective-permute-done.5.refs_3_, ...), custom_call_target="tpu_custom_call", output_to_operand_aliasing={{}: (4, {})} | custom-call | flops 1207959552 | bytes 1048576 | tf_op jit(solution)/shard_map/pallas_call | solution.py:177
  44.2 9.6 %collective-permute-done.6.refs_2_ = bf16[2,384,256]{2,1,0:T(8,128)(2,1)S(1)} collective-permute-done((bf16[2,384,256]{2,1,0:T(8,128)(2,1)S(1)}, bf16[2,384,256]{2,1,0:T(8,128)(2,1)S(1)}, u32[]{:S(2)}, u32[]{:S(2)}) %collective-permute-start.6) | collective-permute-done | bytes 393248 | tf_op jit(solution)/shard_map/ppermute | solution.py:197
  53.8 4.3 %collective-permute-start.7 = (bf16[2,384,256]{2,1,0:T(8,128)(2,1)S(1)}, bf16[2,384,256]{2,1,0:T(8,128)(2,1)S(1)}, u32[]{:S(2)}, u32[]{:S(2)}) collective-permute-start(bf16[2,384,256]{2,1,0:T(8,128)(2,1)S(1)} %collective-permute-done.6.refs_2_), channel_id=1, source_target_pairs={{0,4},{4,0},{8,12},{12,8},{16,20},{20,16},{24,28},{28,24},{32,36},... | collective-permute-start | bytes 1179656 | tf_op jit(solution)/shard_map/ppermute | solution.py:197
  58.2 2.7 %shard_map.51.refs_3_ = f32[12,136,256]{2,1,0:T(8,128)S(1)} custom-call(s32[32]{0:T(128)S(1)} %copy-done.1, bf16[384,1024]{1,0:T(8,128)(2,1)S(1)} %copy-done, bf16[2,384,256]{2,1,0:T(8,128)(2,1)S(1)} %collective-permute-done.6.refs_2_, f32[12,136,256]{2,1,0:T(8,128)S(1)} %shard_map.50.refs_3_), custom_call_target="tpu_custom_call", output_to_operand_aliasing={{}: (3, {})} | custom-call | flops 603979776 | bytes 1048576 | tf_op jit(solution)/shard_map/pallas_call | solution.py:177
  60.8 0.0 collective-permute-done.7.refs_2_
  60.8 3.8 %shard_map.52 = (bf16[384,1024]{1,0:T(8,128)(2,1)}, f32[12,136,256]{2,1,0:T(8,128)S(1)}) custom-call(s32[32]{0:T(128)S(1)} %copy-done.1, bf16[384,1024]{1,0:T(8,128)(2,1)S(1)} %copy-done, bf16[2,384,256]{2,1,0:T(8,128)(2,1)S(1)} %collective-permute-done.7.refs_2_, f32[12,136,256]{2,1,0:T(8,128)S(1)} %shard_map.51.refs_3_), custom_call_target="tpu_custom_call", output_to_operand_aliasing={{1}: (3, {})} | custom-call | flops 603979776 | bytes 1048576 | tf_op jit(solution)/shard_map/pallas_call | solution.py:177
Async XLA Ops:
  1.1 14.0 %collective-permute-start.1 = (bf16[2,384,256]{2,1,0:T(8,128)(2,1)S(1)}, bf16[2,384,256]{2,1,0:T(8,128)(2,1)S(1)}, u32[]{:S(2)}, u32[]{:S(2)}) collective-permute-start(bf16[2,384,256]{2,1,0:T(8,128)(2,1)S(1)} %pad_maximum_fusion.refs_2_), channel_id=1, source_target_pairs={{0,8},{4,12},{8,16},{12,20},{16,24},{20,28},{24,32},{28,36},{32,40... | collective-permute-start | bytes 1179656 | tf_op jit(solution)/shard_map/ppermute | solution.py:197
  4.3 16.2 %collective-permute-start = (bf16[2,384,256]{2,1,0:T(8,128)(2,1)S(1)}, bf16[2,384,256]{2,1,0:T(8,128)(2,1)S(1)}, u32[]{:S(2)}, u32[]{:S(2)}) collective-permute-start(bf16[2,384,256]{2,1,0:T(8,128)(2,1)S(1)} %pad_maximum_fusion.refs_2_), channel_id=1, source_target_pairs={{4,48},{12,56},{20,0},{28,8},{36,16},{44,24},{52,32},{60,40},{68,1... | collective-permute-start | bytes 1179656 | tf_op jit(solution)/shard_map/ppermute | solution.py:197
  10.1 1.1 %copy-start = (bf16[384,1024]{1,0:T(8,128)(2,1)S(1)}, bf16[384,1024]{1,0:T(8,128)(2,1)}, u32[]{:S(2)}) copy-start(bf16[384,1024]{1,0:T(8,128)(2,1)} %refs_1_.13) | copy-start | bytes 2359300
  11.2 0.7 %copy-start.1 = (s32[32]{0:T(128)S(1)}, s32[32]{0:T(128)}, u32[]{:S(2)}) copy-start(s32[32]{0:T(128)} %refs_0_.13) | copy-start | bytes 388
  15.1 10.3 %collective-permute-start.2 = (bf16[2,384,256]{2,1,0:T(8,128)(2,1)S(1)}, bf16[2,384,256]{2,1,0:T(8,128)(2,1)S(1)}, u32[]{:S(2)}, u32[]{:S(2)}) collective-permute-start(bf16[2,384,256]{2,1,0:T(8,128)(2,1)S(1)} %collective-permute-done.1.refs_3_), channel_id=1, source_target_pairs={{0,4},{4,0},{8,12},{12,8},{16,20},{20,16},{24,28},{28,24},{32,36},... | collective-permute-start | bytes 1179656 | tf_op jit(solution)/shard_map/ppermute | solution.py:197
  18.5 14.7 %collective-permute-start.3 = (bf16[2,384,256]{2,1,0:T(8,128)(2,1)S(1)}, bf16[2,384,256]{2,1,0:T(8,128)(2,1)S(1)}, u32[]{:S(2)}, u32[]{:S(2)}) collective-permute-start(bf16[2,384,256]{2,1,0:T(8,128)(2,1)S(1)} %collective-permute-done.1.refs_3_), channel_id=1, source_target_pairs={{0,8},{4,12},{8,16},{12,20},{16,24},{20,28},{24,32},{28,36},{32,40... | collective-permute-start | bytes 1179656 | tf_op jit(solution)/shard_map/ppermute | solution.py:197
  33.2 8.1 %collective-permute-start.4 = (bf16[2,384,256]{2,1,0:T(8,128)(2,1)S(1)}, bf16[2,384,256]{2,1,0:T(8,128)(2,1)S(1)}, u32[]{:S(2)}, u32[]{:S(2)}) collective-permute-start(bf16[2,384,256]{2,1,0:T(8,128)(2,1)S(1)} %collective-permute-done.3.refs_2_), channel_id=1, source_target_pairs={{0,4},{4,0},{8,12},{12,8},{16,20},{20,16},{24,28},{28,24},{32,36},... | collective-permute-start | bytes 1179656 | tf_op jit(solution)/shard_map/ppermute | solution.py:197
  35.9 5.3 %collective-permute-start.5 = (bf16[2,384,256]{2,1,0:T(8,128)(2,1)S(1)}, bf16[2,384,256]{2,1,0:T(8,128)(2,1)S(1)}, u32[]{:S(2)}, u32[]{:S(2)}) collective-permute-start(bf16[2,384,256]{2,1,0:T(8,128)(2,1)S(1)} %collective-permute-done.refs_2_), channel_id=1, source_target_pairs={{48,32},{56,40},{0,48},{8,56},{16,64},{24,72},{32,80},{40,88},{112... | collective-permute-start | bytes 1179656 | tf_op jit(solution)/shard_map/ppermute | solution.py:197
  36.6 17.2 %collective-permute-start.6 = (bf16[2,384,256]{2,1,0:T(8,128)(2,1)S(1)}, bf16[2,384,256]{2,1,0:T(8,128)(2,1)S(1)}, u32[]{:S(2)}, u32[]{:S(2)}) collective-permute-start(bf16[2,384,256]{2,1,0:T(8,128)(2,1)S(1)} %collective-permute-done.3.refs_2_), channel_id=1, source_target_pairs={{0,8},{4,12},{8,16},{12,20},{16,24},{20,28},{24,32},{28,36},{32,40... | collective-permute-start | bytes 1179656 | tf_op jit(solution)/shard_map/ppermute | solution.py:197
  53.8 7.0 %collective-permute-start.7 = (bf16[2,384,256]{2,1,0:T(8,128)(2,1)S(1)}, bf16[2,384,256]{2,1,0:T(8,128)(2,1)S(1)}, u32[]{:S(2)}, u32[]{:S(2)}) collective-permute-start(bf16[2,384,256]{2,1,0:T(8,128)(2,1)S(1)} %collective-permute-done.6.refs_2_), channel_id=1, source_target_pairs={{0,4},{4,0},{8,12},{12,8},{16,20},{20,16},{24,28},{28,24},{32,36},... | collective-permute-start | bytes 1179656 | tf_op jit(solution)/shard_map/ppermute | solution.py:197
